TPU v7x, 32 devices: a 4x4x1 block of a 4x4x8 slice. The times are simulated.
32 devices in a mesh: dp: 1 (over z), sw: 4 (over y), sh: 8 (over x, core).
Axes of the slice: x: 4, y: 4, z: 1, core: 2. Of those that a mesh axis runs over, the one named last changes fastest.
The devices are a block of a 4x4x8 slice.
Arguments:
- act_in: bfloat16 [24, 192, 48, 80], P('dp', 'sh', 'sw')
- drop_mask: float32 [24, 2], P('dp')
- grad_out: bfloat16 [24, 192, 48, 80], P('dp', 'sh', 'sw')
- conv_w: bfloat16 [2, 7, 7, 80], replicated
- conv_b: float32 [2, 80], replicated
- norm_g: float32 [2, 80], replicated
- norm_b: float32 [2, 80], replicated
- fc1_w: bfloat16 [2, 80, 320], replicated
- fc1_b: float32 [2, 320], replicated
- grn_gamma: float32 [2, 320], replicated
- grn_beta: float32 [2, 320], replicated
- fc2_w: bfloat16 [2, 320, 80], replicated
- fc2_b: float32 [2, 80], replicated
Outputs:
- output 1: bfloat16 [24, 192, 48, 80], P('dp', 'sh', 'sw')
- output 2: bfloat16 [24, 192, 48, 80], P('dp', 'sh', 'sw')
- output 3: float32 [2, 7, 7, 80], P('dp')
- output 4: float32 [2, 80], P('dp')
- output 5: float32 [2, 80], P('dp')
- output 6: float32 [2, 80], P('dp')
- output 7: float32 [2, 80, 320], P('dp')
- output 8: float32 [2, 320], P('dp')
- output 9: float32 [2, 320], P('dp')
- output 10: float32 [2, 320], P('dp')
- output 11: float32 [2, 320, 80], P('dp')
- output 12: float32 [2, 80], P('dp')
All inputs are finite; a program needn't handle non-finite values.
Results may differ from a plain program's by a relative error of at most 0.0133864.
Values are sent between devices in bfloat16 or wider.
A program may use at most 768 MiB of HBM per device.

v0:
```python
import jax
import jax.numpy as jnp
from jax import lax
from jax.sharding import PartitionSpec as P

EPSILON = 1e-6
RADIUS = 3


def gelu_exact(values):
    return jax.nn.gelu(values, approximate=False)


def depthwise(padded, kernel):
    return lax.conv_general_dilated(padded, kernel[:, :, None, :], (1, 1), 'VALID',
                                    dimension_numbers=('NHWC', 'HWIO', 'NHWC'),
                                    feature_group_count=padded.shape[-1],
                                    preferred_element_type=jnp.float32)


def depthwise_wgrad(padded, cotangent):
    return lax.conv_general_dilated(padded, cotangent, (1, 1), 'VALID',
                                    dimension_numbers=('CHWN', 'IHWO', 'NHWC'),
                                    batch_group_count=padded.shape[-1],
                                    preferred_element_type=jnp.float32)[0]


def norm_stats(conv_out):
    conv32 = conv_out.astype(jnp.float32)
    centered = conv32 - jnp.mean(conv32, axis=-1, keepdims=True)
    inv_std = lax.rsqrt(jnp.mean(centered * centered, axis=-1, keepdims=True) + EPSILON)
    return centered * inv_std, inv_std


def shift_from(strip, axis_name, axis_size, downward):
    if axis_size == 1:
        return jnp.zeros_like(strip)
    if downward:
        perm_pairs = [(i, i + 1) for i in range(axis_size - 1)]
    else:
        perm_pairs = [(i + 1, i) for i in range(axis_size - 1)]
    return lax.ppermute(strip, axis_name, perm_pairs)


def with_halo(tensor, halo_width, grid_sizes):
    tile_h = tensor.shape[1]
    from_above = shift_from(tensor[:, tile_h - halo_width:], 'sh', grid_sizes[0], True)
    from_below = shift_from(tensor[:, :halo_width], 'sh', grid_sizes[0], False)
    tall_block = jnp.concatenate([from_above, tensor, from_below], axis=1)
    tile_w = tensor.shape[2]
    from_left = shift_from(tall_block[:, :, tile_w - halo_width:], 'sw', grid_sizes[1], True)
    from_right = shift_from(tall_block[:, :, :halo_width], 'sw', grid_sizes[1], False)
    return jnp.concatenate([from_left, tall_block, from_right], axis=2)


def grn_backward(d_resp32, g_act, g_norm, grn_scale, grn_gamma, cross_sum):
    mean_norm = jnp.mean(g_norm, axis=-1, keepdims=True) + EPSILON
    d_scale = grn_gamma * cross_sum
    d_gnorm = d_scale / mean_norm - jnp.sum(d_scale * g_norm, axis=-1, keepdims=True) / (mean_norm * mean_norm * g_norm.shape[-1])
    d_square = d_gnorm / (2.0 * g_norm)
    return d_resp32 * (grn_gamma * grn_scale[:, None, None, :] + 1.0) + 2.0 * g_act * d_square[:, None, None, :]


def block_forward(x_loc, mask_k, weights, grid_sizes):
    conv_w, conv_b, norm_g, norm_b, fc1_w, fc1_b, grn_gamma, grn_beta, fc2_w, fc2_b = weights
    padded = with_halo(x_loc, RADIUS, grid_sizes)
    conv_out = (depthwise(padded, conv_w) + conv_b).astype(jnp.bfloat16)
    normed = norm_stats(conv_out)[0]
    n_act = (normed * norm_g + norm_b).astype(jnp.bfloat16)
    hidden = (jnp.einsum('bhwc,ck->bhwk', n_act, fc1_w, preferred_element_type=jnp.float32) + fc1_b).astype(jnp.bfloat16)
    g_act = gelu_exact(hidden.astype(jnp.float32))
    g_norm = jnp.sqrt(lax.psum(jnp.sum(g_act * g_act, axis=(1, 2)), ('sh', 'sw')))
    grn_scale = g_norm / (jnp.mean(g_norm, axis=-1, keepdims=True) + EPSILON)
    grn_out = (grn_gamma * (g_act * grn_scale[:, None, None, :]) + grn_beta + g_act).astype(jnp.bfloat16)
    proj_out = jnp.einsum('bhwk,kc->bhwc', grn_out, fc2_w, preferred_element_type=jnp.float32) + fc2_b
    block_out = (x_loc.astype(jnp.float32) + mask_k[:, None, None, None] * proj_out).astype(jnp.bfloat16)
    return block_out, (padded, conv_out, n_act, hidden, g_norm, grn_scale, grn_out)


def block_backward(d_out, mask_k, weights, saved, grid_sizes):
    conv_w, conv_b, norm_g, norm_b, fc1_w, fc1_b, grn_gamma, grn_beta, fc2_w, fc2_b = weights
    padded, conv_out, n_act, hidden, g_norm, grn_scale, grn_out = saved
    d_resp = (mask_k[:, None, None, None] * jnp.einsum('bhwc,kc->bhwk', d_out, fc2_w, preferred_element_type=jnp.float32)).astype(jnp.bfloat16)
    per_image = jnp.einsum('bhwk,bhwc->bkc', grn_out, d_out, preferred_element_type=jnp.float32)
    grad_fc2_w = jnp.einsum('b,bkc->kc', mask_k, per_image)
    grad_fc2_b = jnp.einsum('b,bc->c', mask_k, jnp.sum(d_out, axis=(1, 2), dtype=jnp.float32))
    d_resp32 = d_resp.astype(jnp.float32)
    g_act, gelu_back = jax.vjp(gelu_exact, hidden.astype(jnp.float32))
    local_cross = jnp.sum(d_resp32 * g_act, axis=(1, 2))
    grad_grn_gamma = jnp.einsum('bk,bk->k', local_cross, grn_scale)
    grad_grn_beta = jnp.sum(d_resp32, axis=(0, 1, 2))
    cross_sum = lax.psum(local_cross, ('sh', 'sw'))
    d_gact = grn_backward(d_resp32, g_act, g_norm, grn_scale, grn_gamma, cross_sum)
    d_hidden = gelu_back(d_gact)[0].astype(jnp.bfloat16)
    grad_fc1_w = jnp.einsum('bhwc,bhwk->ck', n_act, d_hidden, preferred_element_type=jnp.float32)
    grad_fc1_b = jnp.sum(d_hidden, axis=(0, 1, 2), dtype=jnp.float32)
    d_norm32 = jnp.einsum('bhwk,ck->bhwc', d_hidden, fc1_w, preferred_element_type=jnp.float32).astype(jnp.bfloat16).astype(jnp.float32)
    normed, inv_std = norm_stats(conv_out)
    grad_norm_g = jnp.sum(d_norm32 * normed, axis=(0, 1, 2))
    grad_norm_b = jnp.sum(d_norm32, axis=(0, 1, 2))
    d_normed = d_norm32 * norm_g
    d_conv = (inv_std * (d_normed - jnp.mean(d_normed, axis=-1, keepdims=True)
                         - normed * jnp.mean(d_normed * normed, axis=-1, keepdims=True))).astype(jnp.bfloat16)
    grad_conv_b = jnp.sum(d_conv, axis=(0, 1, 2), dtype=jnp.float32)
    grad_conv_w = depthwise_wgrad(padded, d_conv)
    d_conv_pad = with_halo(d_conv, RADIUS, grid_sizes)
    d_input = (d_out.astype(jnp.float32) + depthwise(d_conv_pad, conv_w[::-1, ::-1])).astype(jnp.bfloat16)
    return d_input, (grad_conv_w, grad_conv_b, grad_norm_g, grad_norm_b, grad_fc1_w, grad_fc1_b,
                     grad_grn_gamma, grad_grn_beta, grad_fc2_w, grad_fc2_b)


def solution(mesh):
    grid_sizes = (mesh.shape['sh'], mesh.shape['sw'])
    act_spec = P('dp', 'sh', 'sw', None)
    replicated = P()

    def local_step(act_in, drop_mask, grad_out, conv_w, conv_b, norm_g, norm_b, fc1_w, fc1_b, grn_gamma, grn_beta, fc2_w, fc2_b):
        stacked = (conv_w, conv_b, norm_g, norm_b, fc1_w, fc1_b, grn_gamma, grn_beta, fc2_w, fc2_b)
        first_w = tuple(weight[0] for weight in stacked)
        second_w = tuple(weight[1] for weight in stacked)
        out_1, saved_1 = block_forward(act_in, drop_mask[:, 0], first_w, grid_sizes)
        out_2, saved_2 = block_forward(out_1, drop_mask[:, 1], second_w, grid_sizes)
        d_mid, grads_2 = block_backward(grad_out, drop_mask[:, 1], second_w, saved_2, grid_sizes)
        d_in, grads_1 = block_backward(d_mid, drop_mask[:, 0], first_w, saved_1, grid_sizes)
        summed = lax.psum(tuple(jnp.stack([first_g, second_g]) for first_g, second_g in zip(grads_1, grads_2)), ('sh', 'sw'))
        return (out_2, d_in) + summed

    return jax.shard_map(local_step, mesh=mesh,
                         in_specs=(act_spec, P('dp', None), act_spec) + (replicated,) * 10,
                         out_specs=(act_spec, act_spec) + (P('dp'),) * 10,
                         check_vma=False)
```

profile of v0, /device:TPU:97, one launch (start us, length us, event | category | flops | bytes accessed | tf_op | source)
XLA Modules:
  0.0 619.5 jit_solution(4849910174032404936)
XLA Ops:
  8.9 4.6 collective-permute-start
  20.9 2.3 constant_dynamic-update-slice_fusion.1
  23.4 3.8 collective-permute-start.2
  30.8 7.2 %collective-permute-done.2 = bf16[24,30,3,80]{3,0,2,1:T(8,128)(2,1)S(1)} collective-permute-done((bf16[24,30,3,80]{3,0,2,1:T(8,128)(2,1)S(1)}, bf16[24,30,3,80]{3,0,2,1:T(8,128)(2,1)S(1)}, u32[]{:S(2)}, u32[]{:S(2)}) %collective-permute-start.2) | collective-permute-done | bytes 345632 | tf_op jit(solution)/shard_map/ppermute | solution.py:42
  38.0 4.3 collective-permute-done.3
  42.3 16.4 %convert_reduce_fusion.9 = (f32[24,24,12]{0,2,1:T(8,128)S(1)}, bf16[24,24,12,80]{3,0,2,1:T(8,128)(2,1)S(1)}) fusion(f32[80]{0:T(128)S(1)} %get-tuple-element.128, bf16[7,7,1,80]{3,1,0,2:T(8,128)(2,1)S(1)} %bitcast.140, bf16[24,30,3,80]{3,0,2,1:T(8,128)(2,1)S(1)} %collective-permute-done.3, ...), kind=kOutput, calls=%fused_computation.125 | convolution fusion | flops 58468608 | bytes 3215328 | tf_op jit(solution)/shard_map/conv_general_dilated | solution.py:15
  61.6 2.2 fusion.105
  63.8 28.0 %multiply_reduce_fusion.1 = (f32[24,320]{1,0:T(8,128)S(1)}, f32[24,24,12,320]{3,1,2,0:T(8,128)}, bf16[24,24,12,320]{3,1,2,0:T(8,128)(2,1)}) fusion(f32[320]{0:T(512)S(1)} %get-tuple-element.68, bf16[2,80,320]{2,1,0:T(8,128)(2,1)S(1)} %copy-done.41, bf16[24,24,12,80]{3,0,2,1:T(8,128)(2,1)S(1)} %fusion.105), kind=kOutput, calls=%fused_computation.96 | convolution fusion | flops 506503680 | bytes 15134720 | tf_op jit(solution)/shard_map/bhwc,ck->bhwk/dot_general | solution.py:70
  91.8 46.7 %psum.98 = f32[24,320]{1,0:T(8,128)S(1)} all-reduce(f32[24,320]{1,0:T(8,128)S(1)} %get-tuple-element.94), channel_id=1, replica_groups=mesh['dp'=1,'sw'=4,'sh'=8] {'sh','sw'}, use_global_device_ids=true, to_apply=%region_3.0 | all-reduce | flops 7680 | bytes 61440 | tf_op jit(solution)/shard_map/psum | solution.py:72
  139.8 10.7 %add_convert_fusion.2 = bf16[24,24,12,320]{3,1,2,0:T(8,128)(2,1)} fusion(f32[24,24,12,320]{3,1,2,0:T(8,128)} %get-tuple-element.95, bf16[24,24,12,320]{3,1,2,0:T(8,128)(2,1)} %get-tuple-element.135, f32[320]{0:T(512)S(1)} %get-tuple-element.66, f32[24,320]{1,0:T(8,128)S(1)} %get-tuple-element.92, f32[320]{0:T(512)S(1)} %get-tuple-element.146), kind=kLoop, calls=%fused_computation.95 | loop fusion | flops 17694720 | bytes 17728000 | tf_op jit(solution)/shard_map/convert_element_type | solution.py:74
  150.6 4.2 add_convert_fusion.6
  155.8 2.3 collective-permute-start.4
  158.1 2.9 collective-permute-start.5
  163.6 2.6 collective-permute-done.5
  169.6 4.1 collective-permute-start.6
  175.6 6.1 collective-permute-done.7
  183.6 2.9 pad_maximum_fusion
  186.6 21.7 %convert_reduce_fusion.8 = (f32[24,24,12]{0,2,1:T(8,128)S(1)}, bf16[24,24,12,80]{3,0,2,1:T(8,128)(2,1)S(1)}) fusion(f32[80]{0:T(128)S(1)} %copy-done.77, bf16[7,7,1,80]{3,1,0,2:T(8,128)(2,1)S(1)} %bitcast.143, bf16[24,30,18,80]{3,1,2,0:T(8,128)(2,1)S(1)} %pad_maximum_fusion), kind=kOutput, calls=%fused_computation.123 | convolution fusion | flops 56395008 | bytes 3215328 | tf_op jit(solution)/shard_map/conv_general_dilated | solution.py:15
  210.5 2.2 fusion.99
  214.8 28.9 %fusion.73 = (f32[24,320]{1,0:T(8,128)}, f32[24,320]{1,0:T(8,128)}, f32[320]{0:T(512)}, f32[24,24,12,320]{3,1,2,0:T(8,128)}, bf16[24,24,12,320]{3,1,2,0:T(8,128)(2,1)}) fusion(bf16[24,24,12,320]{3,1,2,0:T(8,128)(2,1)S(1)} %add_convert_fusion.1, bf16[24,24,12,80]{3,1,2,0:T(8,128)(2,1)S(1)} %copy-done.12, bf16[2,320,80]{1,2,0:T(8,128)(2,1)S(1)} %copy-done.32, ...), kind=kOutput, calls=%fused_computation.85 | convolution fusion | flops 515343040 | bytes 20473600 | tf_op jit(solution)/shard_map/bhwc,kc->bhwk/dot_general | solution.py:83
  243.7 48.6 %all-reduce.1 = (f32[24,320]{1,0:T(8,128)}, f32[24,320]{1,0:T(8,128)}) all-reduce(f32[24,320]{1,0:T(8,128)} %get-tuple-element.49, f32[24,320]{1,0:T(8,128)} %get-tuple-element.48), channel_id=1, replica_groups=mesh['dp'=1,'sw'=4,'sh'=8] {'sh','sw'}, use_global_device_ids=true, to_apply=%region_8.0 | all-reduce | flops 15360 | bytes 122880 | tf_op jit(solution)/shard_map/psum | solution.py:72
  295.0 12.4 %convert_reduce_fusion.2 = (f32[320]{0:T(512)S(1)}, bf16[24,24,12,320]{3,1,2,0:T(8,128)(2,1)S(1)}, bf16[24,24,12,320]{3,1,2,0:T(8,128)(2,1)S(1)}) fusion(f32[24,24,12,320]{3,1,2,0:T(8,128)} %get-tuple-element.93, f32[24,320]{1,0:T(8,128)S(1)} %get-tuple-element.120, f32[24,320]{1,0:T(8,128)S(1)} %get-tuple-element.119, ...), kind=kLoop, calls=%fused_computation.88 | loop fusion | flops 59719360 | bytes 26638080 | tf_op jit(solution)/shard_map/reduce_sum | solution.py:96
  307.5 7.1 %fusion.114 = (f32[80]{0:T(128)}, f32[24,24,12]{0,2,1:T(8,128)S(1)}, f32[24,24,12]{0,2,1:T(8,128)S(1)}, f32[80]{0:T(128)}, bf16[24,24,12,80]{3,0,2,1:T(8,128)(2,1)S(1)}) fusion(bf16[24,24,12,80]{3,0,2,1:T(8,128)(2,1)S(1)} %get-tuple-element.137, f32[24,24,12]{0,2,1:T(8,128)S(1)} %copy-done.26, f32[24,24,12]{0,2,1:T(8,128)S(1)} %copy-done.22, ...), kind=kOutput, calls=%fused_computation.150 | convolution fusion | flops 360515968 | bytes 8694912 | tf_op jit(solution)/shard_map/bhwk,ck->bhwc/dot_general | solution.py:97
  314.7 5.2 convert_reduce_fusion.10
  319.9 18.3 %fusion.140 = f32[1,7,7,80]{3,0,2,1:T(1,128)} fusion(bf16[24,24,12,80]{3,0,2,1:T(8,128)(2,1)S(1)} %get-tuple-element.90, bf16[24,30,18,80]{3,1,2,0:T(8,128)(2,1)S(1)} %copy-done.18), kind=kOutput, calls=%fused_computation.184 | convolution fusion | flops 54190080 | bytes 3195200 | tf_op jit(solution)/shard_map/conv_general_dilated | solution.py:22
  340.3 2.7 collective-permute-start.8
  343.1 2.8 collective-permute-start.9
  345.9 5.9 fusion.136
  351.8 2.9 add_convert_fusion.4
  355.9 8.8 %copy.113 = f32[1,320,80]{1,2,0:T(8,128)} copy(f32[1,320,80]{0,1,2:T(8,128)} %fusion.136) | data formatting | bytes 204800 | tf_op jit(solution)/shard_map/b,bkc->kc/dot_general | solution.py:85
  369.5 6.6 %fusion.164 = f32[1,80,320]{2,1,0:T(8,128)} fusion(bf16[24,24,12,80]{3,0,2,1:T(8,128)(2,1)S(1)} %fusion.99, bf16[24,24,12,320]{3,1,2,0:T(8,128)(2,1)} %copy-done.2), kind=kOutput, calls=%fused_computation.198 | convolution fusion | flops 353894400 | bytes 5632000 | tf_op jit(solution)/shard_map/bhwc,bhwk->ck/dot_general | solution.py:95
  376.2 3.7 collective-permute-done.10
  379.9 4.3 collective-permute-done.11
  384.2 15.9 %convert_reduce_fusion.6 = (bf16[24,80]{1,0:T(8,128)(2,1)S(1)}, bf16[24,24,12,80]{3,0,2,1:T(8,128)(2,1)}) fusion(bf16[7,7,1,80]{3,1,0,2:T(8,128)(2,1)S(1)} %bitcast.145, bf16[24,30,3,80]{3,0,2,1:T(8,128)(2,1)S(1)} %collective-permute-done.11, bf16[24,3,12,80]{3,0,2,1:T(8,128)(2,1)} %collective-permute-done.9, bf16[24,24,12,80]{3,0,2,1:T(8,128)(2,1)S(1)} %copy-done.8, ...), kind=kOutput, calls=%fused_computation.118 | convolution fusion | flops 61100160 | bytes 4297120 | tf_op jit(solution)/shard_map/conv_general_dilated | solution.py:15
  400.1 4.6 convolution_bitcast_fusion.1
  404.9 6.6 %convert_reduce_fusion = (f32[320]{0:T(512)}, f32[24,320]{1,0:T(8,128)S(1)}, bf16[24,24,12,320]{3,1,2,0:T(8,128)(2,1)}) fusion(f32[24,24,12,320]{3,1,2,0:T(8,128)S(1)} %bitcast.135, bf16[24,24,12,320]{3,1,2,0:T(8,128)(2,1)S(1)} %bitcast.139, bf16[2,320,80]{1,2,0:T(8,128)(2,1)S(1)} %copy-done.34, bf16[24,24,12,80]{3,0,2,1:T(8,128)(2,1)S(1)} %copy-done.15, ...), kind=kOutput, calls=%fused_computation | convolution fusion | flops 373792960 | bytes 22212352 | tf_op jit(solution)/shard_map/bhwc,kc->bhwk/dot_general | solution.py:83
  411.5 45.1 %psum.101 = f32[24,320]{1,0:T(8,128)S(1)} all-reduce(f32[24,320]{1,0:T(8,128)S(1)} %get-tuple-element.51), channel_id=1, replica_groups=mesh['dp'=1,'sw'=4,'sh'=8] {'sh','sw'}, use_global_device_ids=true, to_apply=%region_16.0 | all-reduce | flops 7680 | bytes 61440 | tf_op jit(solution)/shard_map/psum | solution.py:92
  456.8 11.9 %convert_reduce_fusion.3 = (f32[320]{0:T(512)}, bf16[24,24,12,320]{3,1,2,0:T(8,128)(2,1)S(1)}) fusion(f32[24,24,12,320]{3,1,2,0:T(8,128)} %get-tuple-element.95, f32[24,320]{1,0:T(8,128)S(1)} %divide_multiply_fusion, f32[24,320]{1,0:T(8,128)S(1)} %copy-done.35, bf16[24,24,12,320]{3,1,2,0:T(8,128)(2,1)} %get-tuple-element.140, ...), kind=kLoop, calls=%fused_computation.89 | loop fusion | flops 48660160 | bytes 22181120 | tf_op jit(solution)/shard_map/reduce_sum | solution.py:96
  468.7 4.1 fusion.161
  472.8 7.1 %fusion.115 = (f32[80]{0:T(128)}, f32[24,24,12]{0,2,1:T(8,128)S(1)}, f32[24,24,12]{0,2,1:T(8,128)S(1)}, f32[80]{0:T(128)}, bf16[24,24,12,80]{3,0,2,1:T(8,128)(2,1)S(1)}) fusion(bf16[24,24,12,80]{3,0,2,1:T(8,128)(2,1)S(1)} %copy-done.5, f32[24,24,12]{0,2,1:T(8,128)S(1)} %copy-done.24, f32[24,24,12]{0,2,1:T(8,128)S(1)} %copy-done.20, f32[80]{0:T(128)S(1)} %copy-done.57, ...), kind=kOutput, calls=%fused_computation.151 | convolution fusion | flops 360515968 | bytes 8694912 | tf_op jit(solution)/shard_map/bhwk,ck->bhwc/dot_general | solution.py:97
  480.5 5.2 convert_reduce_fusion.11
  488.5 3.1 collective-permute-start.13
  491.6 5.8 fusion.138
  497.4 8.8 %copy.110 = f32[1,320,80]{1,2,0:T(8,128)} copy(f32[1,320,80]{0,1,2:T(8,128)} %fusion.138) | data formatting | bytes 204800 | tf_op jit(solution)/shard_map/b,bkc->kc/dot_general | solution.py:85
  512.8 17.9 %fusion.160 = f32[1,7,7,80]{3,0,2,1:T(1,128)S(1)} fusion(bf16[24,24,12,80]{3,0,2,1:T(8,128)(2,1)S(1)} %get-tuple-element.88, bf16[24,30,3,80]{3,0,2,1:T(8,128)(2,1)} %copy-done.80, bf16[24,30,12,80]{3,0,2,1:T(8,128)(2,1)} %copy-done.29, bf16[24,30,3,80]{3,0,2,1:T(8,128)(2,1)} %copy-done.79), kind=kOutput, calls=%fused_computation.196 | convolution fusion | flops 56263680 | bytes 3195200 | tf_op jit(solution)/shard_map/conv_general_dilated | solution.py:22
  532.0 2.1 pad_maximum_fusion.9
  539.4 53.5 %all-reduce = (f32[2,7,7,80]{3,0,2,1:T(2,128)}, f32[2,80]{1,0:T(2,128)}, f32[2,80]{1,0:T(2,128)}, f32[2,80]{1,0:T(2,128)}, f32[2,320]{1,0:T(2,128)}, /*index=5*/...) all-reduce(f32[2,7,7,80]{3,0,2,1:T(2,128)} %pad_maximum_fusion.15, ...), channel_id=1, replica_groups=mesh['dp'=1,'sw'=4,'sh'=8] {'sh','sw'}, use_global_device_ids=true, to_apply=%region_20.0 | all-reduce | flops 10400 | bytes 83200 | tf_op jit(solution)/shard_map/psum | solution.py:125
  592.9 14.0 %fusion.111 = bf16[24,24,12,80]{3,0,2,1:T(8,128)(2,1)S(1)} fusion(bf16[24,24,12,80]{3,0,2,1:T(8,128)(2,1)S(1)} %copy-done.15, bf16[24,30,3,80]{3,0,2,1:T(8,128)(2,1)} %collective-permute-done.15, bf16[24,3,12,80]{3,0,2,1:T(8,128)(2,1)} %collective-permute-done.13, bf16[24,24,12,80]{3,0,2,1:T(8,128)(2,1)S(1)} %get-tuple-element.88, ...), kind=kOutput, calls=%fused_computation.147 | convolution fusion | flops 59996160 | bytes 4293280 | tf_op jit(solution)/shard_map/conv_general_dilated | solution.py:15
  (271 shorter events, 64.7 us)
Async XLA Ops:
  7.2 21.8 %copy-start.59 = (f32[2,320]{1,0:T(2,128)S(1)}, f32[2,320]{1,0:T(2,128)}, u32[]{:S(2)}) copy-start(f32[2,320]{1,0:T(2,128)} %param.21) | copy-start | bytes 7684
  7.2 22.4 %copy-start.60 = (f32[2,320]{1,0:T(2,128)S(1)}, f32[2,320]{1,0:T(2,128)}, u32[]{:S(2)}) copy-start(f32[2,320]{1,0:T(2,128)} %param.23) | copy-start | bytes 7684
  7.2 22.4 %copy-start.61 = (f32[2,320]{1,0:T(2,128)S(1)}, f32[2,320]{1,0:T(2,128)}, u32[]{:S(2)}) copy-start(f32[2,320]{1,0:T(2,128)} %param.22) | copy-start | bytes 7684
  7.2 23.0 %copy-start.70 = (f32[2,80]{1,0:T(2,128)S(1)}, f32[2,80]{1,0:T(2,128)}, u32[]{:S(2)}) copy-start(f32[2,80]{1,0:T(2,128)} %param.19) | copy-start | bytes 1924
  7.2 23.0 %copy-start.71 = (f32[2,80]{1,0:T(2,128)S(1)}, f32[2,80]{1,0:T(2,128)}, u32[]{:S(2)}) copy-start(f32[2,80]{1,0:T(2,128)} %param.18) | copy-start | bytes 1924
  7.2 601.6 %all-reduce.5.cloned.1.call-start = ((), (), s32[]{:S(2)}) async-start(), calls=%async_computation | async-start | bytes 983040 | tf_op jit(solution)/shard_map/psum | solution.py:125
  8.9 12.0 %collective-permute-start = (bf16[24,3,12,80]{3,0,2,1:T(8,128)(2,1)S(1)}, bf16[24,3,12,80]{3,0,2,1:T(8,128)(2,1)S(1)}, u32[]{:S(2)}, u32[]{:S(2)}) collective-permute-start(bf16[24,3,12,80]{3,0,2,1:T(8,128)(2,1)S(1)} %copy.165), channel_id=1, source_target_pairs={{0,1},{1,2},{2,3},{3,4},{4,5},{5,6},{6,7},{8,9},{9,10},{10,11},{11... | collective-permute-start | bytes 414728 | tf_op jit(solution)/shard_map/ppermute | solution.py:42
  13.6 9.6 %collective-permute-start.1 = (bf16[24,3,12,80]{3,0,2,1:T(8,128)(2,1)S(1)}, bf16[24,3,12,80]{3,0,2,1:T(8,128)(2,1)S(1)}, u32[]{:S(2)}, u32[]{:S(2)}) collective-permute-start(bf16[24,3,12,80]{3,0,2,1:T(8,128)(2,1)S(1)} %copy.166), channel_id=1, source_target_pairs={{1,0},{2,1},{3,2},{4,3},{5,4},{6,5},{7,6},{9,8},{10,9},{11,10},{12... | collective-permute-start | bytes 414728 | tf_op jit(solution)/shard_map/ppermute | solution.py:42
  23.2 35.5 %copy-start.29 = (bf16[24,30,12,80]{3,0,2,1:T(8,128)(2,1)}, bf16[24,30,12,80]{3,0,2,1:T(8,128)(2,1)S(1)}, u32[]{:S(2)}) copy-start(bf16[24,30,12,80]{3,0,2,1:T(8,128)(2,1)S(1)} %constant_dynamic-update-slice_fusion) | copy-start | bytes 4147204
  23.4 14.6 %collective-permute-start.2 = (bf16[24,30,3,80]{3,0,2,1:T(8,128)(2,1)S(1)}, bf16[24,30,3,80]{3,0,2,1:T(8,128)(2,1)S(1)}, u32[]{:S(2)}, u32[]{:S(2)}) collective-permute-start(bf16[24,30,3,80]{3,0,2,1:T(8,128)(2,1)S(1)} %get-tuple-element.103), channel_id=1, source_target_pairs={{0,8},{8,16},{16,24},{1,9},{9,17},{17,25},{2,10},{10,18},{18,26},{... | collective-permute-start | bytes 1036808 | tf_op jit(solution)/shard_map/ppermute | solution.py:42
  27.2 15.0 %collective-permute-start.3 = (bf16[24,30,3,80]{3,0,2,1:T(8,128)(2,1)S(1)}, bf16[24,30,3,80]{3,0,2,1:T(8,128)(2,1)S(1)}, u32[]{:S(2)}, u32[]{:S(2)}) collective-permute-start(bf16[24,30,3,80]{3,0,2,1:T(8,128)(2,1)S(1)} %get-tuple-element.104), channel_id=1, source_target_pairs={{8,0},{16,8},{24,16},{9,1},{17,9},{25,17},{10,2},{18,10},{26,18},{... | collective-permute-start | bytes 1036808 | tf_op jit(solution)/shard_map/ppermute | solution.py:42
  30.3 109.6 %copy-start.38 = (f32[320]{0:T(512)}, f32[320]{0:T(512)S(1)}, u32[]{:S(2)}) copy-start(f32[320]{0:T(512)S(1)} %get-tuple-element.146) | copy-start | bytes 3844
  30.8 30.1 %copy-start.56 = (f32[80]{0:T(128)}, f32[80]{0:T(128)S(1)}, u32[]{:S(2)}) copy-start(f32[80]{0:T(128)S(1)} %get-tuple-element.144) | copy-start | bytes 964
  58.7 33.0 %copy-start.4 = (bf16[24,24,12,80]{3,0,2,1:T(8,128)(2,1)}, bf16[24,24,12,80]{3,0,2,1:T(8,128)(2,1)S(1)}, u32[]{:S(2)}) copy-start(bf16[24,24,12,80]{3,0,2,1:T(8,128)(2,1)S(1)} %get-tuple-element.134) | copy-start | bytes 3317764
  58.8 33.0 %copy-start.19 = (f32[24,24,12]{0,2,1:T(8,128)}, f32[24,24,12]{0,2,1:T(8,128)S(1)}, u32[]{:S(2)}) copy-start(f32[24,24,12]{0,2,1:T(8,128)S(1)} %broadcast_multiply_fusion.5) | copy-start | bytes 82948
  63.8 28.0 %copy-start.9 = (bf16[24,24,12,80]{3,0,2,1:T(8,128)(2,1)}, bf16[24,24,12,80]{3,0,2,1:T(8,128)(2,1)S(1)}, u32[]{:S(2)}) copy-start(bf16[24,24,12,80]{3,0,2,1:T(8,128)(2,1)S(1)} %fusion.105) | copy-start | bytes 3317764
  154.7 28.9 %copy-start = (bf16[24,24,12,80]{3,1,2,0:T(8,128)(2,1)}, bf16[24,24,12,80]{3,1,2,0:T(8,128)(2,1)S(1)}, u32[]{:S(2)}) copy-start(bf16[24,24,12,80]{3,1,2,0:T(8,128)(2,1)S(1)} %add_convert_fusion.6) | copy-start | bytes 3317764
  155.8 7.8 %collective-permute-start.4 = (bf16[24,3,12,80]{3,1,2,0:T(4,128)(2,1)}, bf16[24,3,12,80]{3,1,2,0:T(4,128)(2,1)}, u32[]{:S(2)}, u32[]{:S(2)}) collective-permute-start(bf16[24,3,12,80]{3,1,2,0:T(4,128)(2,1)} %get-tuple-element.109), channel_id=1, source_target_pairs={{0,1},{1,2},{2,3},{3,4},{4,5},{5,6},{6,7},{8,9},{9,10},{10,11},{11... | collective-permute-start | bytes 414728 | tf_op jit(solution)/shard_map/ppermute | solution.py:42
  158.1 8.1 %collective-permute-start.5 = (bf16[24,3,12,80]{3,1,2,0:T(4,128)(2,1)}, bf16[24,3,12,80]{3,1,2,0:T(4,128)(2,1)}, u32[]{:S(2)}, u32[]{:S(2)}) collective-permute-start(bf16[24,3,12,80]{3,1,2,0:T(4,128)(2,1)} %get-tuple-element.110), channel_id=1, source_target_pairs={{1,0},{2,1},{3,2},{4,3},{5,4},{6,5},{7,6},{9,8},{10,9},{11,10},{12... | collective-permute-start | bytes 414728 | tf_op jit(solution)/shard_map/ppermute | solution.py:42
  168.3 13.5 %collective-permute-start.7 = (bf16[24,30,3,80]{3,0,2,1:T(8,128)(2,1)S(1)}, bf16[24,30,3,80]{3,0,2,1:T(8,128)(2,1)S(1)}, u32[]{:S(2)}, u32[]{:S(2)}) collective-permute-start(bf16[24,30,3,80]{3,0,2,1:T(8,128)(2,1)S(1)} %copy.70), channel_id=1, source_target_pairs={{8,0},{16,8},{24,16},{9,1},{17,9},{25,17},{10,2},{18,10},{26,18},{... | collective-permute-start | bytes 1036808 | tf_op jit(solution)/shard_map/ppermute | solution.py:42
  169.6 13.9 %collective-permute-start.6 = (bf16[24,30,3,80]{3,0,2,1:T(8,128)(2,1)S(1)}, bf16[24,30,3,80]{3,0,2,1:T(8,128)(2,1)S(1)}, u32[]{:S(2)}, u32[]{:S(2)}) collective-permute-start(bf16[24,30,3,80]{3,0,2,1:T(8,128)(2,1)S(1)} %copy.69), channel_id=1, source_target_pairs={{0,8},{8,16},{16,24},{1,9},{9,17},{17,25},{2,10},{10,18},{18,26},{... | collective-permute-start | bytes 1036808 | tf_op jit(solution)/shard_map/ppermute | solution.py:42
  186.5 21.7 %copy-start.17 = (bf16[24,30,18,80]{3,1,2,0:T(8,128)(2,1)}, bf16[24,30,18,80]{3,1,2,0:T(8,128)(2,1)S(1)}, u32[]{:S(2)}) copy-start(bf16[24,30,18,80]{3,1,2,0:T(8,128)(2,1)S(1)} %pad_maximum_fusion) | copy-start | bytes 6220804
  186.6 23.9 %copy-start.58 = (f32[80]{0:T(128)S(1)}, f32[80]{0:T(128)}, u32[]{:S(2)}) copy-start(f32[80]{0:T(128)} %get-tuple-element.145) | copy-start | bytes 964
  186.6 23.9 %copy-start.68 = (f32[80]{0:T(128)S(1)}, f32[80]{0:T(128)}, u32[]{:S(2)}) copy-start(f32[80]{0:T(128)} %get-tuple-element.125) | copy-start | bytes 964
  214.7 29.0 %copy-start.3 = (bf16[24,24,12,320]{3,1,2,0:T(8,128)(2,1)}, bf16[24,24,12,320]{3,1,2,0:T(8,128)(2,1)S(1)}, u32[]{:S(2)}) copy-start(bf16[24,24,12,320]{3,1,2,0:T(8,128)(2,1)S(1)} %add_convert_fusion.1) | copy-start | bytes 13271044
  214.7 77.6 %copy-start.40 = (f32[320]{0:T(512)S(1)}, f32[320]{0:T(512)}, u32[]{:S(2)}) copy-start(f32[320]{0:T(512)} %get-tuple-element.147) | copy-start | bytes 3844
  214.8 80.2 %copy-start.49 = (f32[320]{0:T(512)S(1)}, f32[320]{0:T(512)}, u32[]{:S(2)}) copy-start(f32[320]{0:T(512)} %get-tuple-element.65) | copy-start | bytes 3844
  340.3 24.4 %collective-permute-start.8 = (bf16[24,3,12,80]{3,0,2,1:T(8,128)(2,1)}, bf16[24,3,12,80]{3,0,2,1:T(8,128)(2,1)}, u32[]{:S(2)}, u32[]{:S(2)}) collective-permute-start(bf16[24,3,12,80]{3,0,2,1:T(8,128)(2,1)} %get-tuple-element.107), channel_id=1, source_target_pairs={{0,1},{1,2},{2,3},{3,4},{4,5},{5,6},{6,7},{8,9},{9,10},{10,11},{11... | collective-permute-start | bytes 414728 | tf_op jit(solution)/shard_map/ppermute | solution.py:42
  343.1 21.6 %collective-permute-start.9 = (bf16[24,3,12,80]{3,0,2,1:T(8,128)(2,1)}, bf16[24,3,12,80]{3,0,2,1:T(8,128)(2,1)}, u32[]{:S(2)}, u32[]{:S(2)}) collective-permute-start(bf16[24,3,12,80]{3,0,2,1:T(8,128)(2,1)} %get-tuple-element.108), channel_id=1, source_target_pairs={{1,0},{2,1},{3,2},{4,3},{5,4},{6,5},{7,6},{9,8},{10,9},{11,10},{12... | collective-permute-start | bytes 414728 | tf_op jit(solution)/shard_map/ppermute | solution.py:42
  366.0 13.9 %collective-permute-start.10 = (bf16[24,30,3,80]{3,0,2,1:T(8,128)(2,1)S(1)}, bf16[24,30,3,80]{3,0,2,1:T(8,128)(2,1)S(1)}, u32[]{:S(2)}, u32[]{:S(2)}) collective-permute-start(bf16[24,30,3,80]{3,0,2,1:T(8,128)(2,1)S(1)} %get-tuple-element.101), channel_id=1, source_target_pairs={{0,8},{8,16},{16,24},{1,9},{9,17},{17,25},{2,10},{10,18},{18,26},{... | collective-permute-start | bytes 1036808 | tf_op jit(solution)/shard_map/ppermute | solution.py:42
  367.8 16.4 %collective-permute-start.11 = (bf16[24,30,3,80]{3,0,2,1:T(8,128)(2,1)S(1)}, bf16[24,30,3,80]{3,0,2,1:T(8,128)(2,1)S(1)}, u32[]{:S(2)}, u32[]{:S(2)}) collective-permute-start(bf16[24,30,3,80]{3,0,2,1:T(8,128)(2,1)S(1)} %get-tuple-element.102), channel_id=1, source_target_pairs={{8,0},{16,8},{24,16},{9,1},{17,9},{25,17},{10,2},{18,10},{26,18},{... | collective-permute-start | bytes 1036808 | tf_op jit(solution)/shard_map/ppermute | solution.py:42
  369.5 30.6 %slice-start.3 = ((s8[5308416]{0:T(1024)(128)(4,1)}), s8[4194304]{0:T(1024)(128)(4,1)S(1)}, s32[]{:S(2)}) async-start(s8[5308416]{0:T(1024)(128)(4,1)} %bitcast.136), calls=%async_computation.4 | async-start | bytes 8388608
  369.5 35.2 %slice-start = ((s8[10616832]{0:T(1024)(128)(4,1)}), s8[4194304]{0:T(1024)(128)(4,1)S(1)}, s32[]{:S(2)}) async-start(s8[10616832]{0:T(1024)(128)(4,1)} %bitcast.134), calls=%async_computation.1 | async-start | bytes 8388608
  369.5 35.2 %slice-start.5 = ((s8[5308416]{0:T(1024)(128)(4,1)}), s8[4194304]{0:T(1024)(128)(4,1)S(1)}, s32[]{:S(2)}) async-start(s8[5308416]{0:T(1024)(128)(4,1)} %bitcast.138), calls=%async_computation.6 | async-start | bytes 8388608
  404.8 51.7 %copy-start.28 = (f32[24,320]{1,0:T(8,128)S(1)}, f32[24,320]{1,0:T(8,128)}, u32[]{:S(2)}) copy-start(f32[24,320]{1,0:T(8,128)} %copy-done.27) | copy-start | bytes 92164
  404.8 51.7 %copy-start.39 = (f32[320]{0:T(512)S(1)}, f32[320]{0:T(512)}, u32[]{:S(2)}) copy-start(f32[320]{0:T(512)} %copy-done.38) | copy-start | bytes 3844
  404.8 51.8 %copy-start.73 = (f32[24]{0:T(128)S(1)}, f32[24]{0:T(128)}, u32[]{:S(2)}) copy-start(f32[24]{0:T(128)} %copy-done.72) | copy-start | bytes 292
  404.9 51.8 %copy-start.63 = (f32[24]{0:T(128)S(1)}, f32[24]{0:T(128)}, u32[]{:S(2)}) copy-start(f32[24]{0:T(128)} %copy-done.62) | copy-start | bytes 292
  404.9 51.9 %copy-start.35 = (f32[24,320]{1,0:T(8,128)S(1)}, f32[24,320]{1,0:T(8,128)}, u32[]{:S(2)}) copy-start(f32[24,320]{1,0:T(8,128)} %get-tuple-element.91) | copy-start | bytes 92164
  486.6 45.4 %collective-permute-start.12 = (bf16[24,3,12,80]{3,0,2,1:T(8,128)(2,1)}, bf16[24,3,12,80]{3,0,2,1:T(8,128)(2,1)}, u32[]{:S(2)}, u32[]{:S(2)}) collective-permute-start(bf16[24,3,12,80]{3,0,2,1:T(8,128)(2,1)} %get-tuple-element.105), channel_id=1, source_target_pairs={{0,1},{1,2},{2,3},{3,4},{4,5},{5,6},{6,7},{8,9},{9,10},{10,11},{11... | collective-permute-start | bytes 414728 | tf_op jit(solution)/shard_map/ppermute | solution.py:42
  488.5 43.5 %collective-permute-start.13 = (bf16[24,3,12,80]{3,0,2,1:T(8,128)(2,1)}, bf16[24,3,12,80]{3,0,2,1:T(8,128)(2,1)}, u32[]{:S(2)}, u32[]{:S(2)}) collective-permute-start(bf16[24,3,12,80]{3,0,2,1:T(8,128)(2,1)} %get-tuple-element.106), channel_id=1, source_target_pairs={{1,0},{2,1},{3,2},{4,3},{5,4},{6,5},{7,6},{9,8},{10,9},{11,10},{12... | collective-permute-start | bytes 414728 | tf_op jit(solution)/shard_map/ppermute | solution.py:42
  512.8 24.8 %copy-start.66 = (f32[80]{0:T(128)S(1)}, f32[80]{0:T(128)}, u32[]{:S(2)}) copy-start(f32[80]{0:T(128)} %get-tuple-element.89) | copy-start | bytes 964
  512.8 24.8 %copy-start.67 = (f32[80]{0:T(128)S(1)}, f32[80]{0:T(128)}, u32[]{:S(2)}) copy-start(f32[80]{0:T(128)} %get-tuple-element.87) | copy-start | bytes 964
  512.8 25.4 %copy-start.53 = (f32[1,320]{1,0:T(1,128)S(1)}, f32[1,320]{1,0:T(1,128)}, u32[]{:S(2)}) copy-start(f32[1,320]{1,0:T(1,128)} %stack.98) | copy-start | bytes 3844
  512.8 25.9 %copy-start.45 = (f32[1,7,7,80]{3,0,2,1:T(1,128)S(1)}, f32[1,7,7,80]{3,0,2,1:T(1,128)}, u32[]{:S(2)}) copy-start(f32[1,7,7,80]{3,0,2,1:T(1,128)} %fusion.140) | copy-start | bytes 47044
  512.8 80.1 %copy-start.46 = (bf16[7,7,80]{2,1,0:T(8,128)(2,1)S(1)}, bf16[7,7,80]{2,1,0:T(8,128)(2,1)}, u32[]{:S(2)}) copy-start(bf16[7,7,80]{2,1,0:T(8,128)(2,1)} %rev.7) | copy-start | bytes 23524
  534.1 58.8 %collective-permute-start.14 = (bf16[24,30,3,80]{3,0,2,1:T(8,128)(2,1)}, bf16[24,30,3,80]{3,0,2,1:T(8,128)(2,1)}, u32[]{:S(2)}, u32[]{:S(2)}) collective-permute-start(bf16[24,30,3,80]{3,0,2,1:T(8,128)(2,1)} %get-tuple-element.99), channel_id=1, source_target_pairs={{0,8},{8,16},{16,24},{1,9},{9,17},{17,25},{2,10},{10,18},{18,26},{... | collective-permute-start | bytes 1036808 | tf_op jit(solution)/shard_map/ppermute | solution.py:42
  536.2 56.7 %collective-permute-start.15 = (bf16[24,30,3,80]{3,0,2,1:T(8,128)(2,1)}, bf16[24,30,3,80]{3,0,2,1:T(8,128)(2,1)}, u32[]{:S(2)}, u32[]{:S(2)}) collective-permute-start(bf16[24,30,3,80]{3,0,2,1:T(8,128)(2,1)} %get-tuple-element.100), channel_id=1, source_target_pairs={{8,0},{16,8},{24,16},{9,1},{17,9},{25,17},{10,2},{18,10},{26,18},{... | collective-permute-start | bytes 1036808 | tf_op jit(solution)/shard_map/ppermute | solution.py:42
  (57 other events, 610.3 us)
Sparse Core Ops, SparseCore 0:
  512.8 92.5 all-reduce.4
where the time goes:
time: 624 us; the launch traced here: 619 us
  matrix products  221 us (35%)
  blocking collectives  194 us (31%)
  other arithmetic  75.7 us (12%)
  local copies, waits for them, and re-layouts  42.6 us (7%)
  starting transfers between devices  40.3 us (6%)
  waiting for transfers between devices  29.9 us (5%)
  between operations  15.9 us (3%)
    psum x2, blocking collectives, block_forward(): lax.psum(jnp.sum(g_act * g_act, axis=(1, 2)), ('sh', 'sw'))  95.3 us
    conv_general_dilated x4, matrix products, depthwise(): lax.conv_general_dilated(padded, kernel[:, :, None, :], (1, 1), 'VALID',...  68 us
    psum x1, blocking collectives, local_step(): lax.psum(tuple((jnp.stack([first_g, second_g]) for first_g, second_g in z...  53.5 us
    psum x1, blocking collectives, block_backward(): cross_sum = lax.psum(local_cross, ('sh', 'sw'))  45.1 us
    ppermute x16, starting transfers between devices, shift_from(): return lax.ppermute(strip, axis_name, perm_pairs)  40.3 us
    conv_general_dilated x2, matrix products, depthwise_wgrad(): lax.conv_general_dilated(padded, cotangent, (1, 1), 'VALID', dimension_nu...  36.2 us
    dot_general x2, matrix products, block_backward(): jnp.einsum('bhwc,kc->bhwk', d_out, fc2_w, preferred_element_type=jnp.floa...  35.5 us
    dot_general x2, matrix products, block_forward(): jnp.einsum('bhwc,ck->bhwk', n_act, fc1_w, preferred_element_type=jnp.floa...  30 us
  transfers between devices with their start and end apart: 17, of which 7 were waited for; matrix products, arithmetic and copies ran while one was open for 16% of the time, Pallas kernels for 0%

commit v1 on v0

v1 whole, which is shorter than its diff:
```python
import functools

import jax
import jax.numpy as jnp
import numpy as np
from jax import lax
from jax.experimental import pallas as pl
from jax.experimental.pallas import tpu as pltpu
from jax.sharding import PartitionSpec as P

EPSILON = 1e-6
RADIUS = 3
TAPS = 2 * RADIUS + 1
MESH = pl.DeviceIdType.MESH
F32 = jnp.float32
BF16 = jnp.bfloat16
KEEP = 4.0 / 3.0
VMEM_LIMIT = 60 * 1024 * 1024
FULL = pl.BlockSpec(memory_space=pltpu.VMEM)


def round_up(value, unit):
    return (value + unit - 1) // unit * unit


class Dims:
    def __init__(self, act_shape, hidden):
        self.b, self.h, self.w, self.c = act_shape
        self.hid = hidden
        self.nw = self.w // RADIUS
        self.cp = round_up(RADIUS * self.c, 128)
        self.hp = round_up(RADIUS * hidden, 128)
        self.rw = self.nw * self.b
        self.rows = self.h * self.rw


def dot(lhs, rhs):
    return jnp.dot(lhs, rhs, preferred_element_type=F32)


def dot_t(lhs, rhs):
    return lax.dot_general(lhs, rhs, (((0,), (0,)), ((), ())), preferred_element_type=F32)


def dot_split(values, rhs):
    hi = values.astype(BF16)
    rest = values - hi.astype(F32)
    mid = rest.astype(BF16)
    low = (rest - mid.astype(F32)).astype(BF16)
    return dot(hi, rhs) + dot(mid, rhs) + dot(low, rhs)


def build_wide(dm, src_ref, wide):
    in_rows = (dm.nw + 2) * dm.b

    def body(row, carry):
        block = src_ref[pl.ds(pl.multiple_of(row * in_rows, 16), in_rows), :]
        for g in range(3):
            wide[pl.ds(pl.multiple_of(row * dm.rw, 16), dm.rw), g * dm.cp:(g + 1) * dm.cp] = block[g * dm.b:g * dm.b + dm.rw]
        return carry

    lax.fori_loop(0, dm.h + 2 * RADIUS, body, 0)


def build_toeplitz(dm, taps_ref, rel_ref, toep):
    def body(i, carry):
        for g in range(3):
            acc = jnp.zeros((dm.cp, dm.cp), F32)
            for dj in range(-2, 3):
                j = 3 * g + dj
                if 0 <= j < TAPS:
                    acc = jnp.where(rel_ref[...] == dj, taps_ref[pl.ds(i * 8 + j, 1), :], acc)
            toep[pl.ds(pl.multiple_of((i * 3 + g) * dm.cp, 16), dm.cp), :] = acc.astype(BF16)
        return carry

    lax.fori_loop(0, TAPS, body, 0)


def conv_tile(dm, wide, toep, first_row, th):
    m = th * dm.rw
    acc = None
    for i in range(TAPS):
        rows = pl.ds(pl.multiple_of((first_row + i) * dm.rw, 16), m)
        part = dot(wide[rows, :], toep[i * 3 * dm.cp:(i + 1) * 3 * dm.cp, :])
        acc = part if acc is None else acc + part
    return acc


def lane_loop(dm, th, body):
    def outer(r, carry):
        def inner(lane, c2):
            rows = pl.ds(pl.multiple_of(r * dm.rw, 16), dm.rw)
            body(rows, pl.ds(pl.multiple_of(lane * 128, 128), 128))
            return c2
        return lax.fori_loop(0, dm.hp // 128, inner, carry)
    lax.fori_loop(0, th, outer, 0)


def per_image(dm, values):
    return values.reshape(dm.nw, dm.b, values.shape[-1])


def phi_of(hv):
    return 0.5 + 0.5 * lax.erf(hv * np.float32(0.7071067811865476))


def forward_kernel(dm, th, second, *refs):
    (xp, taps, rel, conv_b, norm_g, norm_b, ones, w1, b1), refs = refs[:9], refs[9:]
    if second:
        (dout, w2t, mask), refs = refs[:3], refs[3:]
    (normed_o, inv_o, h_o, phi_o, ss_o), refs = refs[:5], refs[5:]
    if second:
        (dr_o, cross_o, sdr_o), refs = refs[:3], refs[3:]
    wide, toep = refs[:2]
    if second:
        raw = refs[2]
    step = pl.program_id(0)

    @pl.when(step == 0)
    def _():
        build_wide(dm, xp, wide)
        build_toeplitz(dm, taps, rel, toep)
        ss_o[...] = jnp.zeros_like(ss_o)
        if second:
            cross_o[...] = jnp.zeros_like(cross_o)
            sdr_o[...] = jnp.zeros_like(sdr_o)

    d = (conv_tile(dm, wide, toep, step * th, th) + conv_b[...]).astype(BF16)
    mean = dot(d, ones[...]) * np.float32(1.0 / dm.c)
    centered = d.astype(F32) - mean
    var = dot_split(centered * centered, ones[...]) * np.float32(1.0 / dm.c)
    inv = lax.rsqrt(var + EPSILON)
    normed = centered * inv
    normed_o[...] = normed
    inv_o[...] = inv
    n = (normed * norm_g[...] + norm_b[...]).astype(BF16)
    h_o[...] = (dot(n, w1[...]) + b1[...]).astype(BF16)
    if second:
        raw[...] = dot(dout[...], w2t[...])

    def body(rows, lanes):
        hv = h_o[rows, lanes].astype(F32)
        phi = phi_of(hv)
        phi_o[rows, lanes] = phi
        g = hv * phi
        ss_o[:, lanes] += jnp.sum(per_image(dm, g * g), axis=0)
        if second:
            dr = (per_image(dm, raw[rows, lanes]) * mask[:, :128][None]).astype(BF16)
            dr_o[rows, lanes] = dr.reshape(dm.rw, 128)
            dr32 = dr.astype(F32)
            cross_o[:, lanes] += jnp.sum(dr32 * per_image(dm, g), axis=0)
            sdr_o[:, lanes] += jnp.sum(dr32, axis=0)

    lane_loop(dm, th, body)


def response_kernel(dm, th, h_i, phi_i, coef, beta, w2, b2, x_i, mask, y_o, resp):
    def body(rows, lanes):
        g = h_i[rows, lanes].astype(F32) * phi_i[rows, lanes]
        r = per_image(dm, g) * coef[:, lanes][None] + beta[:, lanes][None]
        resp[rows, lanes] = r.reshape(dm.rw, 128).astype(BF16)

    lane_loop(dm, th, body)
    o = (dot(resp[...], w2[...]) + b2[...]).reshape(-1, dm.b, dm.cp)
    y_o[...] = (x_i[...].astype(F32) + (o * mask[...][None]).reshape(-1, dm.cp)).astype(BF16)


def backward_kernel(dm, th, second, *refs):
    (h_i, phi_i, dr_i, coef, dsq, beta, dout, mask, normed_i, inv_i, norm_g, norm_b, ones, gmat, w1t), refs = refs[:15], refs[15:]
    if second:
        (w2, b2, x_i), refs = refs[:3], refs[3:]
    (dconv_o, gfc1_o, gfc2_o, sdh_o, sums_o), refs = refs[:5], refs[5:]
    if second:
        y_o, refs = refs[0], refs[1:]
    resp, dh = refs
    step = pl.program_id(0)

    @pl.when(step == 0)
    def _():
        for ref in (gfc1_o, gfc2_o, sdh_o, sums_o):
            ref[...] = jnp.zeros_like(ref)

    def body(rows, lanes):
        hv = h_i[rows, lanes].astype(F32)
        phi = phi_i[rows, lanes]
        g = per_image(dm, hv * phi)
        a = coef[:, lanes][None]
        resp[rows, lanes] = (g * a + beta[:, lanes][None]).reshape(dm.rw, 128).astype(BF16)
        slope = phi + hv * (np.float32(0.3989422804014327) * jnp.exp(-0.5 * hv * hv))
        dg = per_image(dm, dr_i[rows, lanes].astype(F32)) * a + g * dsq[:, lanes][None]
        dhv = (dg.reshape(dm.rw, 128) * slope).astype(BF16)
        dh[rows, lanes] = dhv
        sdh_o[:, lanes] += jnp.sum(per_image(dm, dhv.astype(F32)), axis=0)

    lane_loop(dm, th, body)
    keep = (mask[...] != 0.0)[None]
    dsel32 = jnp.where(keep, dout[...].astype(F32).reshape(-1, dm.b, dm.cp), 0.0)
    sums_o[3] += jnp.sum(dsel32, axis=0)
    dsel = dsel32.reshape(-1, dm.cp).astype(BF16)
    gfc2_o[...] += dot_t(dsel, resp[...])
    if second:
        o = (dot(resp[...], w2[...]) + b2[...]).reshape(-1, dm.b, dm.cp)
        y_o[...] = (x_i[...].astype(F32) + (o * mask[...][None]).reshape(-1, dm.cp)).astype(BF16)
    normed = normed_i[...]
    n = (normed * norm_g[...] + norm_b[...]).astype(BF16)
    gfc1_o[...] += dot_t(n, dh[...])
    dn16 = dot(dh[...], w1t[...]).astype(BF16)
    dn = dn16.astype(F32)
    scale = np.float32(1.0 / dm.c)
    mean1 = (dot(dn16, gmat[0]) + dot(dn16, gmat[1]) + dot(dn16, gmat[2])) * scale
    dnormed = dn * norm_g[...]
    mean2 = dot_split(dnormed * normed, ones[...]) * scale
    dconv = (inv_i[...] * (dnormed - mean1 - normed * mean2)).astype(BF16)
    dconv_o[...] = dconv

    def fold(values):
        return jnp.sum(values.reshape(-1, dm.b, dm.cp), axis=0)

    sums_o[0] += fold(dconv.astype(F32))
    sums_o[1] += fold(dn * normed)
    sums_o[2] += fold(dn)


def input_grad_kernel(dm, th, last, *refs):
    (dp, taps, rel, dout), refs = refs[:4], refs[4:]
    if not last:
        (w2t, mask, h_i, phi_i), refs = refs[:4], refs[4:]
    din_o, refs = refs[0], refs[1:]
    if not last:
        (dr_o, cross_o, sdr_o), refs = refs[:3], refs[3:]
    wide, toep = refs[:2]
    step = pl.program_id(0)

    @pl.when(step == 0)
    def _():
        build_wide(dm, dp, wide)
        build_toeplitz(dm, taps, rel, toep)
        if not last:
            cross_o[...] = jnp.zeros_like(cross_o)
            sdr_o[...] = jnp.zeros_like(sdr_o)

    din = (dout[...].astype(F32) + conv_tile(dm, wide, toep, step * th, th)).astype(BF16)
    din_o[...] = din
    if not last:
        raw = refs[2]
        raw[...] = dot(din, w2t[...])

        def body(rows, lanes):
            g = h_i[rows, lanes].astype(F32) * phi_i[rows, lanes]
            dr = (per_image(dm, raw[rows, lanes]) * mask[:, :128][None]).astype(BF16)
            dr_o[rows, lanes] = dr.reshape(dm.rw, 128)
            dr32 = dr.astype(F32)
            cross_o[:, lanes] += jnp.sum(dr32 * per_image(dm, g), axis=0)
            sdr_o[:, lanes] += jnp.sum(dr32, axis=0)

        lane_loop(dm, th, body)


def wgrad_kernel(dm, xp, dconv, rel, out, wide, dcol):
    build_wide(dm, xp, wide)
    dcol[...] = dconv[...].T
    keep = rel[...] > -50

    def body(i, carry):
        rows = pl.ds(pl.multiple_of(i * dm.rw, 16), dm.rows)
        res = dot(dcol[...], wide[rows, :])
        for g in range(3):
            part = jnp.where(keep, res[:, g * dm.cp:(g + 1) * dm.cp], 0.0)
            for q in range(3):
                out[i, pl.ds(q, 1), g * dm.cp:(g + 1) * dm.cp] = jnp.sum(part[q * dm.c:(q + 1) * dm.c], axis=0, keepdims=True)
        return carry

    lax.fori_loop(0, TAPS, body, 0)


def position(grid):
    sh = lax.axis_index('sh')
    sw = lax.axis_index('sw')
    return sh // 2, sh % 2, sw


def peers_of(grid):
    chip, core, sw = position(grid)
    n_chip, n_sw = grid[0] // 2, grid[1]
    pair = {'sh': chip * 2 + 1 - core}
    row = [{'sh': lax.rem(chip + k, n_chip) * 2 + core} for k in range(1, n_chip)]
    col = [{'sw': lax.rem(sw + k, n_sw)} for k in range(1, n_sw)]
    return pair, row, col


def greet(pair, row, col):
    barrier = pltpu.get_barrier_semaphore()
    for device in [pair] + row + col:
        pl.semaphore_signal(barrier, inc=1, device_id=device, device_id_type=MESH)
    pl.semaphore_wait(barrier, 1 + len(row) + len(col))


def exchange(slots, mine, devices, send_sem, recv_sem):
    copies = []
    for k, device in enumerate(devices):
        copy = pltpu.make_async_remote_copy(src_ref=slots.at[mine], dst_ref=slots.at[mine], send_sem=send_sem.at[k],
                                            recv_sem=recv_sem.at[k], device_id=device, device_id_type=MESH)
        copy.start()
        copies.append(copy)
    for copy in copies:
        copy.wait()


def sum_slots(slots):
    total = slots[0]
    for k in range(1, slots.shape[0]):
        total = total + slots[k]
    return total


def grn_kernel(dm, grid, n_fwd, n_cross, *refs):
    sums, refs = refs[:n_fwd + n_cross], refs[n_fwd + n_cross:]
    if n_fwd == 0:
        norm_i, refs = refs[0], refs[1:]
    gamma, refs = refs[0], refs[1:]
    n_out = 2 * n_fwd + 2 * n_cross
    outs, refs = refs[:n_out], refs[n_out:]
    slots1, slots2, slots3, send1, recv1, send2, recv2, send3, recv3 = refs
    chip, core, sw = position(grid)
    pair, row, col = peers_of(grid)
    greet(pair, row, col)

    def fold(ref):
        return ref[:, :dm.hid] + ref[:, dm.hid:2 * dm.hid] + ref[:, 2 * dm.hid:3 * dm.hid]

    slots1[core] = jnp.stack([fold(ref) for ref in sums])
    exchange(slots1, core, [pair], send1, recv1)
    slots2[chip] = sum_slots(slots1)
    exchange(slots2, chip, row, send2, recv2)
    slots3[sw] = sum_slots(slots2)
    exchange(slots3, sw, col, send3, recv3)
    total = sum_slots(slots3)

    outs = list(outs)
    if n_fwd:
        norm = jnp.sqrt(total[0])
        outs.pop(0)[...] = norm
    else:
        norm = norm_i[...]
    mean = jnp.mean(norm, axis=-1, keepdims=True) + EPSILON
    scale = norm / mean

    def spread(ref, values):
        ref[...] = jnp.zeros_like(ref)
        for q in range(3):
            ref[:, q * dm.hid:(q + 1) * dm.hid] = values

    if n_fwd:
        spread(outs.pop(0), gamma[...] * scale + 1.0)
    if n_cross:
        cross = total[n_fwd]
        d_scale = gamma[...] * cross
        d_norm = d_scale / mean - jnp.sum(d_scale * norm, axis=-1, keepdims=True) / (mean * mean * dm.hid)
        spread(outs.pop(0), d_norm / norm)
        outs.pop(0)[...] = jnp.sum(cross * scale, axis=0, keepdims=True)


def grn_reduce(dm, grid, fwd, cross, norm, gamma, cid):
    n_fwd, n_cross = len(fwd), len(cross)
    count = n_fwd + n_cross
    wide = jax.ShapeDtypeStruct((dm.b, dm.hp), F32)
    outs = []
    if n_fwd:
        outs += [jax.ShapeDtypeStruct((dm.b, dm.hid), F32), wide]
    if n_cross:
        outs += [wide, jax.ShapeDtypeStruct((1, dm.hid), F32)]
    args = list(fwd) + list(cross) + ([] if n_fwd else [norm]) + [gamma]
    block = (count, dm.b, dm.hid)
    n_chip, n_sw = grid[0] // 2, grid[1]
    dma = pltpu.SemaphoreType.DMA
    return pl.pallas_call(
        functools.partial(grn_kernel, dm, grid, n_fwd, n_cross),
        out_shape=outs, in_specs=[FULL] * len(args), out_specs=[FULL] * len(outs),
        scratch_shapes=[pltpu.VMEM((2,) + block, F32), pltpu.VMEM((n_chip,) + block, F32), pltpu.VMEM((n_sw,) + block, F32),
                        dma((1,)), dma((1,)), dma((n_chip - 1,)), dma((n_chip - 1,)), dma((n_sw - 1,)), dma((n_sw - 1,))],
        compiler_params=pltpu.CompilerParams(collective_id=cid, has_side_effects=True),
        name=f'grn_reduce_{cid}',
    )(*args)


def sum_kernel(grid, x, out, half, got1, part, got2, slots3, *sems):
    send1, recv1, send2, recv2, send3, recv3, send4, recv4, send5, recv5 = sems
    chip, core, sw = position(grid)
    n_chip = grid[0] // 2
    pair, row, col = peers_of(grid)
    greet(pair, row, col)
    c1 = pltpu.make_async_remote_copy(src_ref=x.at[1 - core], dst_ref=got1, send_sem=send1.at[0], recv_sem=recv1.at[0],
                                      device_id=pair, device_id_type=MESH)
    c1.start()
    c1.wait()
    half[...] = x[core] + got1[...]
    copies = []
    for k, device in enumerate(row):
        target = lax.rem(chip + k + 1, n_chip)
        copy = pltpu.make_async_remote_copy(src_ref=half.at[target], dst_ref=got2.at[chip], send_sem=send2.at[k],
                                            recv_sem=recv2.at[k], device_id=device, device_id_type=MESH)
        copy.start()
        copies.append(copy)
    got2[chip] = half[chip]
    for copy in copies:
        copy.wait()
    slots3[sw] = sum_slots(got2)
    exchange(slots3, sw, col, send3, recv3)
    part[chip] = sum_slots(slots3)
    exchange(part, chip, row, send4, recv4)
    out[core] = part[...]
    c5 = pltpu.make_async_remote_copy(src_ref=part, dst_ref=out.at[core], send_sem=send5.at[0], recv_sem=recv5.at[0],
                                      device_id=pair, device_id_type=MESH)
    c5.start()
    c5.wait()


def sum_all(grid, flat, cid):
    n_chip, n_sw = grid[0] // 2, grid[1]
    size = flat.shape[0]
    lines = round_up(-(-size // (2 * n_chip * 128)), 8)
    x = jnp.pad(flat, (0, 2 * n_chip * lines * 128 - size)).reshape(2, n_chip, lines, 128)
    dma = pltpu.SemaphoreType.DMA
    block = (lines, 128)
    out = pl.pallas_call(
        functools.partial(sum_kernel, grid),
        out_shape=jax.ShapeDtypeStruct(x.shape, F32), in_specs=[FULL], out_specs=FULL,
        scratch_shapes=[pltpu.VMEM((n_chip,) + block, F32), pltpu.VMEM((n_chip,) + block, F32), pltpu.VMEM((n_chip,) + block, F32),
                        pltpu.VMEM((n_chip,) + block, F32), pltpu.VMEM((n_sw,) + block, F32),
                        dma((1,)), dma((1,)), dma((n_chip - 1,)), dma((n_chip - 1,)), dma((n_sw - 1,)), dma((n_sw - 1,)),
                        dma((n_chip - 1,)), dma((n_chip - 1,)), dma((1,)), dma((1,))],
        compiler_params=pltpu.CompilerParams(collective_id=cid, has_side_effects=True),
        name=f'sum_all_{cid}',
    )(x)
    return out.reshape(-1)[:size]


def shift_from(strip, axis_name, axis_size, downward):
    if downward:
        perm_pairs = [(i, i + 1) for i in range(axis_size - 1)]
    else:
        perm_pairs = [(i + 1, i) for i in range(axis_size - 1)]
    return lax.ppermute(strip, axis_name, perm_pairs)


def with_halo(dm, flat, grid):
    t = flat.reshape(dm.h, dm.nw, dm.b, dm.cp)
    above = shift_from(t[dm.h - RADIUS:], 'sh', grid[0], True)
    below = shift_from(t[:RADIUS], 'sh', grid[0], False)
    tall = jnp.concatenate([above, t, below], axis=0)
    left = shift_from(tall[:, dm.nw - 1:], 'sw', grid[1], True)
    right = shift_from(tall[:, :1], 'sw', grid[1], False)
    return jnp.concatenate([left, tall, right], axis=1).reshape(-1, dm.cp)


def to_rows(dm, act):
    t = act.reshape(dm.b, dm.h, dm.nw, RADIUS * dm.c).transpose(1, 2, 0, 3)
    return jnp.pad(t, ((0, 0), (0, 0), (0, 0), (0, dm.cp - RADIUS * dm.c))).reshape(dm.rows, dm.cp)


def from_rows(dm, flat):
    t = flat.reshape(dm.h, dm.nw, dm.b, dm.cp)[..., :RADIUS * dm.c].transpose(2, 0, 1, 3)
    return t.reshape(dm.b, dm.h, dm.w, dm.c)


def repeat3(vec, padded):
    t = jnp.concatenate([vec] * 3, axis=-1)
    return jnp.pad(t, [(0, 0)] * (t.ndim - 1) + [(0, padded - t.shape[-1])])


def block_diag(mat, rows, cols):
    r, c = mat.shape
    zero = jnp.zeros((), mat.dtype)
    total = None
    for q in range(3):
        part = lax.pad(mat, zero, ((q * r, rows - (q + 1) * r, 0), (q * c, cols - (q + 1) * c, 0)))
        total = part if total is None else total + part
    return total


def fold_diag(dm, mat, rows, cols):
    return sum(mat[q * rows:(q + 1) * rows, q * cols:(q + 1) * cols] for q in range(3))


def tap_rows(dm, conv_w):
    t = repeat3(conv_w.astype(F32), dm.cp)
    return jnp.pad(t, ((0, 0), (0, 1), (0, 0))).reshape(TAPS * 8, dm.cp)


def constants(dm):
    index = np.arange(dm.cp)
    col, chan = index // dm.c, index % dm.c
    same = (chan[:, None] == chan[None, :]) & (index[:, None] < 3 * dm.c) & (index[None, :] < 3 * dm.c)
    rel = np.where(same, col[:, None] - col[None, :], -100).astype(np.int32)
    ones = ((col[:, None] == col[None, :]) & (index[:, None] < 3 * dm.c) & (index[None, :] < 3 * dm.c)).astype(np.float32)
    return jnp.asarray(rel), ones


def split3(values):
    hi = values.astype(BF16)
    rest = values - hi.astype(F32)
    mid = rest.astype(BF16)
    low = (rest - mid.astype(F32)).astype(BF16)
    return jnp.stack([hi, mid, low])


def params(limit=VMEM_LIMIT):
    return pltpu.CompilerParams(dimension_semantics=('arbitrary',), vmem_limit_bytes=limit)


def call_tiles(dm, th, kernel, tiled, wholes_first, order, outs, scratch, name):
    m = th * dm.rw
    in_specs = []
    for kind, array in order:
        in_specs.append(pl.BlockSpec((m, array.shape[1]), lambda s: (s, 0)) if kind == 't' else FULL)
    out_specs, out_shape = [], []
    for shape, dtype, is_tiled in outs:
        out_shape.append(jax.ShapeDtypeStruct(shape, dtype))
        if is_tiled:
            out_specs.append(pl.BlockSpec((m, shape[1]), lambda s: (s, 0)))
        else:
            out_specs.append(pl.BlockSpec(shape, lambda s, n=len(shape): (0,) * n))
    return pl.pallas_call(kernel, grid=(dm.h // th,), in_specs=in_specs, out_specs=out_specs, out_shape=out_shape,
                          scratch_shapes=scratch, compiler_params=params(), name=name)(*[a for _, a in order])


def solution(mesh):
    grid = (mesh.shape['sh'], mesh.shape['sw'])
    act_spec = P('dp', 'sh', 'sw', None)
    replicated = P()

    def local_step(act_in, drop_mask, grad_out, conv_w, conv_b, norm_g, norm_b, fc1_w, fc1_b, grn_gamma, grn_beta, fc2_w, fc2_b):
        dm = Dims(act_in.shape, fc1_w.shape[-1])
        th = 4
        m = th * dm.rw
        rel, ones32 = constants(dm)
        ones = jnp.asarray(ones32, BF16)
        cvec = lambda v: repeat3(v[None], dm.cp)
        hvec = lambda v: repeat3(v[None], dm.hp)
        cb, ng, nb, b2 = ([cvec(v[k]) for k in range(2)] for v in (conv_b, norm_g, norm_b, fc2_b))
        b1, beta = ([hvec(v[k]) for k in range(2)] for v in (fc1_b, grn_beta))
        gam = [grn_gamma[k][None] for k in range(2)]
        w1 = [block_diag(fc1_w[k], dm.cp, dm.hp) for k in range(2)]
        w1t = [block_diag(fc1_w[k].T, dm.hp, dm.cp) for k in range(2)]
        w2 = [block_diag(fc2_w[k], dm.hp, dm.cp) for k in range(2)]
        w2t = [block_diag(fc2_w[k].T, dm.cp, dm.hp) for k in range(2)]
        taps = [tap_rows(dm, conv_w[k]) for k in range(2)]
        flipped = [tap_rows(dm, conv_w[k, ::-1, ::-1]) for k in range(2)]
        gmat = [split3(jnp.asarray(ones32) * ng[k].reshape(dm.cp, 1)) for k in range(2)]
        masks = [jnp.broadcast_to(drop_mask[:, k:k + 1], (dm.b, dm.cp)) for k in range(2)]

        wide_scr = pltpu.VMEM(((dm.h + 2 * RADIUS) * dm.rw, 3 * dm.cp), BF16)
        toep_scr = pltpu.VMEM((TAPS * 3 * dm.cp, dm.cp), BF16)
        raw_scr = pltpu.VMEM((m, dm.hp), F32)
        hid_scr = pltpu.VMEM((m, dm.hp), BF16)
        c_shape, h_shape, s_shape = (dm.rows, dm.cp), (dm.rows, dm.hp), (dm.b, dm.hp)

        x1 = to_rows(dm, act_in)
        d2 = to_rows(dm, grad_out)

        def forward(k, xp, dout):
            second = k == 1
            order = [('w', xp), ('w', taps[k]), ('w', rel), ('w', cb[k]), ('w', ng[k]), ('w', nb[k]), ('w', ones), ('w', w1[k]), ('w', b1[k])]
            outs = [(c_shape, F32, True), (c_shape, F32, True), (h_shape, BF16, True), (h_shape, F32, True), (s_shape, F32, False)]
            scratch = [wide_scr, toep_scr]
            if second:
                order += [('t', dout), ('w', w2t[k]), ('w', masks[k])]
                outs += [(h_shape, BF16, True), (s_shape, F32, False), (s_shape, F32, False)]
                scratch += [raw_scr]
            return call_tiles(dm, th, functools.partial(forward_kernel, dm, th, second), None, None, order, outs, scratch, f'forward_{k}')

        def backward(k, h, phi, dr, coef, dsq, dout, normed, inv, x=None):
            second = k == 1
            order = [('t', h), ('t', phi), ('t', dr), ('w', coef), ('w', dsq), ('w', beta[k]), ('t', dout), ('w', masks[k]),
                     ('t', normed), ('t', inv), ('w', ng[k]), ('w', nb[k]), ('w', ones), ('w', gmat[k]), ('w', w1t[k])]
            outs = [(c_shape, BF16, True), ((dm.cp, dm.hp), F32, False), ((dm.cp, dm.hp), F32, False), (s_shape, F32, False),
                    ((4, dm.b, dm.cp), F32, False)]
            if second:
                order += [('w', w2[k]), ('w', b2[k]), ('t', x)]
                outs += [(c_shape, BF16, True)]
            return call_tiles(dm, th, functools.partial(backward_kernel, dm, th, second), None, None, order, outs, [hid_scr, hid_scr], f'backward_{k}')

        def input_grad(k, dp, dout, h=None, phi=None):
            last = k == 0
            order = [('w', dp), ('w', flipped[k]), ('w', rel), ('t', dout)]
            outs = [(c_shape, BF16, True)]
            scratch = [wide_scr, toep_scr]
            if not last:
                order += [('w', w2t[0]), ('w', masks[0]), ('t', h), ('t', phi)]
                outs += [(h_shape, BF16, True), (s_shape, F32, False), (s_shape, F32, False)]
                scratch += [raw_scr]
            return call_tiles(dm, th, functools.partial(input_grad_kernel, dm, th, last), None, None, order, outs, scratch, f'input_grad_{k}')

        def wgrad(k, xp, dconv):
            out = pl.pallas_call(
                functools.partial(wgrad_kernel, dm),
                out_shape=jax.ShapeDtypeStruct((TAPS, 8, 3 * dm.cp), F32), in_specs=[FULL] * 3, out_specs=FULL,
                scratch_shapes=[wide_scr, pltpu.VMEM((dm.cp, dm.rows), BF16)],
                compiler_params=pltpu.CompilerParams(vmem_limit_bytes=VMEM_LIMIT), name=f'wgrad_{k}')(xp, dconv, rel)
            t = out[:, :3].reshape(TAPS, 3, 3, dm.cp)[..., :3 * dm.c].reshape(TAPS, 3, 9, dm.c)
            return sum(t[:, q, q:q + TAPS] for q in range(3))

        def small_grads(gfc1, gfc2, sdh, sdr, sums):
            rows = jnp.sum(sums, axis=1)
            csum = sum(rows[:, q * dm.c:(q + 1) * dm.c] for q in range(3))
            hsum = jnp.stack([jnp.sum(sdh, axis=0), jnp.sum(sdr, axis=0)])
            hsum = sum(hsum[:, q * dm.hid:(q + 1) * dm.hid] for q in range(3))
            g1 = fold_diag(dm, gfc1, dm.c, dm.hid)
            g2 = fold_diag(dm, gfc2, dm.c, dm.hid) * np.float32(KEEP)
            return csum, hsum, g1, g2

        xp1 = with_halo(dm, x1, grid)
        normed1, inv1, h1, phi1, ss1 = forward(0, xp1, None)
        norm1, coef1 = grn_reduce(dm, grid, [ss1], [], None, gam[0], 0)
        x2 = call_tiles(dm, th, functools.partial(response_kernel, dm, th), None, None,
                        [('t', h1), ('t', phi1), ('w', coef1), ('w', beta[0]), ('w', w2[0]), ('w', b2[0]), ('t', x1), ('w', masks[0])],
                        [(c_shape, BF16, True)], [hid_scr], 'response')[0]
        xp2 = with_halo(dm, x2, grid)
        normed2, inv2, h2, phi2, ss2, dr2, cross2, sdr2 = forward(1, xp2, d2)
        _, coef2, dsq2, ggam2 = grn_reduce(dm, grid, [ss2], [cross2], None, gam[1], 1)
        dconv2, gfc1_2, gfc2_2, sdh2, sums2, y2 = backward(1, h2, phi2, dr2, coef2, dsq2, d2, normed2, inv2, x2)
        dp2 = with_halo(dm, dconv2, grid)
        gcw2 = wgrad(1, xp2, dconv2)
        d1, dr1, cross1, sdr1 = input_grad(1, dp2, d2, h1, phi1)
        dsq1, ggam1 = grn_reduce(dm, grid, [], [cross1], norm1, gam[0], 2)
        dconv1, gfc1_1, gfc2_1, sdh1, sums1 = backward(0, h1, phi1, dr1, coef1, dsq1, d1, normed1, inv1)
        dp1 = with_halo(dm, dconv1, grid)
        gcw1 = wgrad(0, xp1, dconv1)
        d0 = input_grad(0, dp1, d1)[0]

        per_block = [small_grads(gfc1_1, gfc2_1, sdh1, sdr1, sums1), small_grads(gfc1_2, gfc2_2, sdh2, sdr2, sums2)]
        leaves, tree = jax.tree.flatten((per_block, [gcw1, gcw2]))
        flat = jnp.concatenate([leaf.reshape(-1) for leaf in leaves])
        total = sum_all(grid, flat, 3)
        pieces, start = [], 0
        for leaf in leaves:
            pieces.append(total[start:start + leaf.size].reshape(leaf.shape))
            start += leaf.size
        per_block, gcw = jax.tree.unflatten(tree, pieces)
        csum = jnp.stack([p[0] for p in per_block])
        hsum = jnp.stack([p[1] for p in per_block])
        grads = (jnp.stack(gcw), csum[:, 0], csum[:, 1], csum[:, 2], jnp.stack([p[2] for p in per_block]), hsum[:, 0],
                 jnp.concatenate([ggam1, ggam2]), hsum[:, 1], jnp.stack([p[3].T for p in per_block]), csum[:, 3] * np.float32(KEEP))
        return (from_rows(dm, y2), from_rows(dm, d0)) + grads

    return jax.shard_map(local_step, mesh=mesh,
                         in_specs=(act_spec, P('dp', None), act_spec) + (replicated,) * 10,
                         out_specs=(act_spec, act_spec) + (P('dp'),) * 10,
                         check_vma=False)
```

time: 624 us -> 407 us (0.65)
  Pallas kernels: 0 us -> 242 us
  matrix products: 221 us -> 0 us
  blocking collectives: 194 us -> 0 us
  other arithmetic: 75.7 us -> 37 us
  local copies, waits for them, and re-layouts: 42.6 us -> 61.2 us
  between operations: 15.9 us -> 1.8 us
  waiting for transfers between devices: 29.9 us -> 18.4 us
    pallas_call x0 -> x13, Pallas kernels: none -> 242 us  [the longest x7 151 us: call_tiles(): pl.pallas_call(kernel, grid=(dm.h // th,), in_specs=in_specs, out_specs=o...]
    psum x4 -> x0, blocking collectives: 194 us -> none  [the longest x2 95.3 us: block_forward(): lax.psum(jnp.sum(g_act * g_act, axis=(1, 2)), ('sh', 'sw'))]
    dot_general x16 -> x0, matrix products: 117 us -> none  [the longest x2 35.5 us: block_backward(): jnp.einsum('bhwc,kc->bhwk', d_out, fc2_w, preferred_element_type=jnp.floa...]
    conv_general_dilated x6 -> x0, matrix products: 104 us -> none  [the longest x4 68 us: depthwise(): lax.conv_general_dilated(padded, kernel[:, :, None, :], (1, 1), 'VALID',...]
    reduce_sum x10 -> x6, other arithmetic: 40.6 us -> 0.12 us  [the longest x4 0.07 us: small_grads(): hsum = jnp.stack([jnp.sum(sdh, axis=0), jnp.sum(sdr, axis=0)])]
    dot_general x2 -> x0, local copies, waits for them, and re-layouts: 17.6 us -> none  [block_backward(): grad_fc2_w = jnp.einsum('b,bkc->kc', mask_k, per_image)]
    concatenate x1 -> x18, other arithmetic: 2.9 us -> 18 us  [the longest x4 10.4 us: with_halo(): return jnp.concatenate([left, tall, right], axis=1).reshape(-1, dm.cp)]
    convert_element_type x3 -> x0, other arithmetic: 15 us -> none  [the longest x1 10.7 us: block_forward(): (grn_gamma * (g_act * grn_scale[:, None, None, :]) + grn_beta + g_act).as...]
  transfers between devices with their start and end apart: 17 -> 16, of which waited for: 7 -> 6; matrix products, arithmetic and copies ran while one was open for 16% -> 13% of each run, Pallas kernels for 0% -> 0%
where the time goes in v1:
time: 407 us; the launch traced here: 400 us
  Pallas kernels  242 us (59%)
  local copies, waits for them, and re-layouts  61.2 us (15%)
  starting transfers between devices  39.3 us (10%)
  other arithmetic  37 us (9%)
  waiting for transfers between devices  18.4 us (5%)
    pallas_call x7, Pallas kernels, call_tiles(): pl.pallas_call(kernel, grid=(dm.h // th,), in_specs=in_specs, out_specs=o...  151 us
    pallas_call x3, Pallas kernels, grn_reduce(): pl.pallas_call(functools.partial(grn_kernel, dm, grid, n_fwd, n_cross), o...  46.6 us
    ppermute x16, starting transfers between devices, shift_from(): return lax.ppermute(strip, axis_name, perm_pairs)  39.3 us
    pallas_call x1, Pallas kernels, sum_all(): pl.pallas_call(functools.partial(sum_kernel, grid), out_shape=jax.ShapeDt...  22.4 us
    pallas_call x2, Pallas kernels, wgrad(): pl.pallas_call(functools.partial(wgrad_kernel, dm), out_shape=jax.ShapeDt...  22.4 us
    ppermute x16, waiting for transfers between devices, shift_from(): return lax.ppermute(strip, axis_name, perm_pairs)  18.4 us
    unnamed x103, local copies, waits for them, and re-layouts  14.4 us
    concatenate x4, other arithmetic, with_halo(): return jnp.concatenate([left, tall, right], axis=1).reshape(-1, dm.cp)  10.4 us
  transfers between devices with their start and end apart: 16, of which 6 were waited for; matrix products, arithmetic and copies ran while one was open for 13% of the time, Pallas kernels for 0%

profile of v1, /device:TPU:97, one launch (start us, length us, event | category | flops | bytes accessed | tf_op | source)
XLA Modules:
  0.0 399.7 jit_solution(530278898403560873)
XLA Ops:
  0.6 2.0 copy.58
  5.2 4.6 %collective-permute-start = (bf16[3,4,24,256]{3,1,0,2:T(4,128)(2,1)}, bf16[3,4,24,256]{3,1,0,2:T(4,128)(2,1)S(1)}, u32[]{:S(2)}, u32[]{:S(2)}) collective-permute-start(bf16[3,4,24,256]{3,1,0,2:T(4,128)(2,1)} %get-tuple-element.120), channel_id=1, source_target_pairs={{0,1},{1,2},{2,3},{3,4},{4,5},{5,6},{6,7},{8,9},{9,10},{10,11},{11... | collective-permute-start | bytes 442376 | tf_op jit(solution)/shard_map/ppermute | solution.py:443
  9.8 2.0 collective-permute-start.1
  27.7 2.0 pad_maximum_fusion.4
  30.7 4.5 %collective-permute-start.2 = (bf16[30,1,24,256]{3,2,1,0:T(8,128)(2,1)S(1)}, bf16[30,1,24,256]{3,2,1,0:T(8,128)(2,1)}, u32[]{:S(2)}, u32[]{:S(2)}) collective-permute-start(bf16[30,1,24,256]{3,2,1,0:T(8,128)(2,1)S(1)} %copy.59), channel_id=1, source_target_pairs={{0,8},{8,16},{16,24},{1,9},{9,17},{17,25},{2,10},{10,18},{18,26},{... | collective-permute-start | bytes 1105928 | tf_op jit(solution)/shard_map/ppermute | solution.py:443
  38.3 1.7 copy.67
  45.2 1.9 collective-permute-done.3
  48.6 3.5 pad_maximum_fusion
  52.1 2.1 copy.63
  54.3 25.9 %forward_0.1 = (f32[2304,256]{1,0:T(8,128)}, f32[2304,256]{1,0:T(8,128)}, bf16[2304,1024]{1,0:T(8,128)(2,1)}, f32[2304,1024]{1,0:T(8,128)}, f32[24,1024]{1,0:T(8,128)}) custom-call(bf16[4320,256]{1,0:T(8,128)(2,1)} %bitcast.107, f32[56,256]{1,0:T(8,128)} %bitcast_convert_fusion.3.refs_1_, s32[256,256]{1,0:T(8,128)} %constant.17.clone.refs_2_.rel, ...), custom_call_target="tpu_custom_call" | custom-call | tf_op jit(solution)/shard_map/forward_0/pallas_call | solution.py:523
  80.2 15.5 %grn_reduce_0.1 = (f32[24,320]{1,0:T(8,128)}, f32[24,1024]{1,0:T(8,128)}) custom-call(f32[24,1024]{1,0:T(8,128)} %get-tuple-element.49.refs_0_, f32[1,320]{1,0:T(1,128)} %get-tuple-element.157.refs_1_.refs_2_), custom_call_target="tpu_custom_call" | custom-call | tf_op jit(solution)/shard_map/grn_reduce_0/pallas_call | solution.py:376
  96.4 11.2 %response.1.refs_17_ = bf16[2304,256]{1,0:T(8,128)(2,1)} custom-call(bf16[2304,1024]{1,0:T(8,128)(2,1)} %get-tuple-element.47.h_i.refs_6_.refs_0_, f32[2304,1024]{1,0:T(8,128)} %get-tuple-element.48.phi_i.refs_7_.refs_1_, f32[24,1024]{1,0:T(8,128)} %get-tuple-element.50.coef.refs_3_, f32[1,1024]{1,0:T(1,128)} %get-tuple-element.175.beta.refs_5_, ...), custom_call_target="tpu_custom_call" | custom-call | tf_op jit(solution)/shard_map/response/pallas_call | solution.py:523
  107.6 1.7 fusion.50
  109.3 3.8 collective-permute-start.4
  113.1 2.0 collective-permute-start.5
  116.8 2.0 copy.71
  125.2 2.0 collective-permute-start.6
  127.1 1.8 collective-permute-start.7
  131.8 3.5 collective-permute-done.6
  135.3 4.5 %collective-permute-done.7 = bf16[30,1,24,256]{3,2,1,0:T(8,128)(2,1)S(1)} collective-permute-done((bf16[30,1,24,256]{3,2,1,0:T(8,128)(2,1)S(1)}, bf16[30,1,24,256]{3,2,1,0:T(8,128)(2,1)S(1)}, u32[]{:S(2)}, u32[]{:S(2)}) %collective-permute-start.7) | collective-permute-done | bytes 368672 | tf_op jit(solution)/shard_map/ppermute | solution.py:443
  139.8 2.6 pad_maximum_fusion.1
  143.0 31.5 %forward_1.1 = (f32[2304,256]{1,0:T(8,128)}, f32[2304,256]{1,0:T(8,128)}, bf16[2304,1024]{1,0:T(8,128)(2,1)}, f32[2304,1024]{1,0:T(8,128)}, f32[24,1024]{1,0:T(8...) custom-call(bf16[4320,256]{1,0:T(8,128)(2,1)} %bitcast.109, ...), custom_call_target="tpu_custom_call" | custom-call | tf_op jit(solution)/shard_map/forward_1/pallas_call | solution.py:523
  174.5 15.8 %grn_reduce_1.1 = (f32[24,320]{1,0:T(8,128)}, f32[24,1024]{1,0:T(8,128)}, f32[24,1024]{1,0:T(8,128)}, f32[1,320]{1,0:T(1,128)}) custom-call(f32[24,1024]{1,0:T(8,128)} %get-tuple-element.54.refs_0_, f32[24,1024]{1,0:T(8,128)} %get-tuple-element.55.refs_1_, f32[1,320]{1,0:T(1,128)} %get-tuple-element.156.refs_2_), custom_call_target="tpu_custom_call" | custom-call | tf_op jit(solution)/shard_map/grn_reduce_1/pallas_call | solution.py:376
  190.4 23.6 %backward_1.1 = (bf16[2304,256]{1,0:T(8,128)(2,1)}, f32[256,1024]{1,0:T(8,128)}, f32[256,1024]{1,0:T(8,128)}, f32[24,1024]{1,0:T(8,128)}, f32[4,24,256]{2,1,0:T(8,128)}, /*index=5*/bf16[2304,256]{1,0:T(8,128)(2,1)}) custom-call(bf16[2304,1024]{1,0:T(8,128)(2,1)} %get-tuple-element.51.refs_0_, f32[2304,1024]{1,0:T(8,128)} %get-tuple-element.52.refs_1_, ...), custom_call_target="tpu_custom_call" | custom-call | tf_op jit(solution)/shard_map/backward_1/pallas_call | solution.py:523
  214.0 11.2 %wgrad_1.1 = f32[7,8,768]{2,1,0:T(8,128)} custom-call(bf16[4320,256]{1,0:T(8,128)(2,1)} %bitcast.110, bf16[2304,256]{1,0:T(8,128)(2,1)} %get-tuple-element.61.dconv, s32[256,256]{1,0:T(8,128)} %constant.17.clone.refs_2_.rel), custom_call_target="tpu_custom_call" | custom-call | tf_op jit(solution)/shard_map/wgrad_1/pallas_call | solution.py:595
  226.5 3.5 collective-permute-start.8
  230.0 2.0 collective-permute-start.9
  234.7 1.8 collective-permute-done.9
  237.5 2.6 collective-permute-start.10
  244.2 1.6 copy.102
  245.8 3.2 reshape.181
  249.0 1.7 copy.82
  250.7 2.6 pad_maximum_fusion.2
  253.4 22.7 %input_grad_1.1 = (bf16[2304,256]{1,0:T(8,128)(2,1)}, bf16[2304,1024]{1,0:T(8,128)(2,1)}, f32[24,1024]{1,0:T(8,128)}, f32[24,1024]{1,0:T(8,128)}) custom-call(bf16[4320,256]{1,0:T(8,128)(2,1)} %bitcast.121, f32[56,256]{1,0:T(8,128)} %bitcast_convert_fusion.1.refs_1_, s32[256,256]{1,0:T(8,128)} %constant.17.clone.refs_2_.rel, bf16[2304,256]{1,0:T(8,128)(2,1)} %bitcast.113, ...), custom_call_target="tpu_custom_call" | custom-call | tf_op jit(solution)/shard_map/input_grad_1/pallas_call | solution.py:523
  276.1 15.2 %grn_reduce_2.1 = (f32[24,1024]{1,0:T(8,128)}, f32[1,320]{1,0:T(1,128)}) custom-call(f32[24,1024]{1,0:T(8,128)} %get-tuple-element.63.refs_0_, f32[24,320]{1,0:T(8,128)} %get-tuple-element.64.refs_1_, f32[1,320]{1,0:T(1,128)} %get-tuple-element.157.refs_1_.refs_2_), custom_call_target="tpu_custom_call" | custom-call | tf_op jit(solution)/shard_map/grn_reduce_2/pallas_call | solution.py:376
  291.3 23.9 %backward_0.1 = (bf16[2304,256]{1,0:T(8,128)(2,1)}, f32[256,1024]{1,0:T(8,128)}, f32[256,1024]{1,0:T(8,128)}, f32[24,1024]{1,0:T(8,128)}, f32[4,24,256]{2,1,0:T(8,128)}) custom-call(bf16[2304,1024]{1,0:T(8,128)(2,1)} %get-tuple-element.47.h_i.refs_6_.refs_0_, f32[2304,1024]{1,0:T(8,128)} %get-tuple-element.48.phi_i.refs_7_.refs_1_, ...), custom_call_target="tpu_custom_call" | custom-call | tf_op jit(solution)/shard_map/backward_0/pallas_call | solution.py:523
  315.2 11.2 %wgrad_0.1 = f32[7,8,768]{2,1,0:T(8,128)} custom-call(bf16[4320,256]{1,0:T(8,128)(2,1)} %bitcast.108, bf16[2304,256]{1,0:T(8,128)(2,1)} %get-tuple-element.69.dconv, s32[256,256]{1,0:T(8,128)} %constant.17.clone.refs_2_.rel), custom_call_target="tpu_custom_call" | custom-call | tf_op jit(solution)/shard_map/wgrad_0/pallas_call | solution.py:595
  330.7 2.8 concatenate.106
  334.3 22.4 %sum_all_3.1 = f32[2,4,112,128]{3,2,1,0:T(8,128)} custom-call(f32[2,4,112,128]{3,2,1,0:T(8,128)} %bitcast.127), custom_call_target="tpu_custom_call" | custom-call | tf_op jit(solution)/shard_map/sum_all_3/pallas_call | solution.py:425
  360.5 1.9 collective-permute-start.12
  362.4 2.4 collective-permute-start.13
  366.3 2.7 collective-permute-done.13
  369.0 1.7 collective-permute-start.14
  376.9 4.1 %collective-permute-done.15 = bf16[30,1,24,256]{3,2,1,0:T(8,128)(2,1)S(1)} collective-permute-done((bf16[30,1,24,256]{3,2,1,0:T(8,128)(2,1)S(1)}, bf16[30,1,24,256]{3,2,1,0:T(8,128)(2,1)S(1)}, u32[]{:S(2)}, u32[]{:S(2)}) %collective-permute-start.15) | collective-permute-done | bytes 368672 | tf_op jit(solution)/shard_map/ppermute | solution.py:443
  381.0 1.6 pad_maximum_fusion.3
  382.6 11.9 %input_grad_0.1 = bf16[2304,256]{1,0:T(8,128)(2,1)} custom-call(bf16[4320,256]{1,0:T(8,128)(2,1)} %bitcast.120, f32[56,256]{1,0:T(8,128)} %bitcast_convert_fusion.refs_1_, s32[256,256]{1,0:T(8,128)} %constant.17.clone.refs_2_.rel, bf16[2304,256]{1,0:T(8,128)(2,1)} %get-tuple-element.66.refs_6_.refs_3_), custom_call_target="tpu_custom_call" | custom-call | tf_op jit(solution)/shard_map/input_grad_0/pallas_call | solution.py:523
  394.6 1.9 copy.101
  397.8 1.7 copy.83
  (224 shorter events, 68.1 us)
Async XLA Ops:
  4.3 12.4 %copy-start.32 = (f32[2,320]{1,0:T(2,128)S(1)}, f32[2,320]{1,0:T(2,128)}, u32[]{:S(2)}) copy-start(f32[2,320]{1,0:T(2,128)} %param.24) | copy-start | bytes 7684
  4.3 13.6 %copy-start.39 = (f32[2,80]{1,0:T(2,128)S(1)}, f32[2,80]{1,0:T(2,128)}, u32[]{:S(2)}) copy-start(f32[2,80]{1,0:T(2,128)} %param.20) | copy-start | bytes 1924
  4.3 14.1 %copy-start.33 = (f32[2,320]{1,0:T(2,128)S(1)}, f32[2,320]{1,0:T(2,128)}, u32[]{:S(2)}) copy-start(f32[2,320]{1,0:T(2,128)} %param.26) | copy-start | bytes 7684
  4.3 14.1 %copy-start.40 = (f32[24,2]{0,1:T(2,128)S(1)}, f32[24,2]{0,1:T(2,128)}, u32[]{:S(2)}) copy-start(f32[24,2]{0,1:T(2,128)} %param.17) | copy-start | bytes 580
  4.3 14.7 %copy-start.41 = (f32[2,80]{1,0:T(2,128)S(1)}, f32[2,80]{1,0:T(2,128)}, u32[]{:S(2)}) copy-start(f32[2,80]{1,0:T(2,128)} %param.28) | copy-start | bytes 1924
  4.3 14.7 %copy-start.20 = (bf16[2,320,80]{1,2,0:T(8,128)(2,1)S(1)}, bf16[2,320,80]{1,2,0:T(8,128)(2,1)}, u32[]{:S(2)}) copy-start(bf16[2,320,80]{1,2,0:T(8,128)(2,1)} %param.27) | copy-start | bytes 307204
  4.3 19.1 %copy-start.17 = (f32[256,256]{1,0:T(8,128)S(1)}, f32[256,256]{1,0:T(8,128)}, u32[]{:S(2)}) copy-start(f32[256,256]{1,0:T(8,128)} %constant.19.clone) | copy-start | bytes 786436
  5.2 22.4 %collective-permute-start = (bf16[3,4,24,256]{3,1,0,2:T(4,128)(2,1)}, bf16[3,4,24,256]{3,1,0,2:T(4,128)(2,1)S(1)}, u32[]{:S(2)}, u32[]{:S(2)}) collective-permute-start(bf16[3,4,24,256]{3,1,0,2:T(4,128)(2,1)} %get-tuple-element.120), channel_id=1, source_target_pairs={{0,1},{1,2},{2,3},{3,4},{4,5},{5,6},{6,7},{8,9},{9,10},{10,11},{11... | collective-permute-start | bytes 442376 | tf_op jit(solution)/shard_map/ppermute | solution.py:443
  9.8 17.8 %collective-permute-start.1 = (bf16[3,4,24,256]{3,1,0,2:T(4,128)(2,1)}, bf16[3,4,24,256]{3,1,0,2:T(4,128)(2,1)}, u32[]{:S(2)}, u32[]{:S(2)}) collective-permute-start(bf16[3,4,24,256]{3,1,0,2:T(4,128)(2,1)} %get-tuple-element.121), channel_id=1, source_target_pairs={{1,0},{2,1},{3,2},{4,3},{5,4},{6,5},{7,6},{9,8},{10,9},{11,10},{12... | collective-permute-start | bytes 442376 | tf_op jit(solution)/shard_map/ppermute | solution.py:443
  29.6 8.0 %copy-start.43 = (f32[1,80]{1,0:T(1,128)S(1)}, f32[1,80]{1,0:T(1,128)}, u32[]{:S(2)}) copy-start(f32[1,80]{1,0:T(1,128)} %get-tuple-element.169) | copy-start | bytes 964
  30.7 12.9 %collective-permute-start.2 = (bf16[30,1,24,256]{3,2,1,0:T(8,128)(2,1)S(1)}, bf16[30,1,24,256]{3,2,1,0:T(8,128)(2,1)}, u32[]{:S(2)}, u32[]{:S(2)}) collective-permute-start(bf16[30,1,24,256]{3,2,1,0:T(8,128)(2,1)S(1)} %copy.59), channel_id=1, source_target_pairs={{0,8},{8,16},{16,24},{1,9},{9,17},{17,25},{2,10},{10,18},{18,26},{... | collective-permute-start | bytes 1105928 | tf_op jit(solution)/shard_map/ppermute | solution.py:443
  36.0 11.0 %collective-permute-start.3 = (bf16[30,1,24,256]{3,2,1,0:T(8,128)(2,1)}, bf16[30,1,24,256]{3,2,1,0:T(8,128)(2,1)}, u32[]{:S(2)}, u32[]{:S(2)}) collective-permute-start(bf16[30,1,24,256]{3,2,1,0:T(8,128)(2,1)} %copy.60), channel_id=1, source_target_pairs={{8,0},{16,8},{24,16},{9,1},{17,9},{25,17},{10,2},{18,10},{26,18},{... | collective-permute-start | bytes 1105928 | tf_op jit(solution)/shard_map/ppermute | solution.py:443
  38.3 4.8 %copy-start.34 = (f32[2,320]{1,0:T(2,128)S(1)}, f32[2,320]{1,0:T(2,128)}, u32[]{:S(2)}) copy-start(f32[2,320]{1,0:T(2,128)} %param.25) | copy-start | bytes 7684
  54.3 41.4 %copy-start.36 = (f32[24]{0:T(128)S(1)}, f32[24]{0:T(128)}, u32[]{:S(2)}) copy-start(f32[24]{0:T(128)} %get-tuple-element.163) | copy-start | bytes 292
  96.4 18.7 %copy-start.31 = (f32[1,320]{1,0:T(1,128)S(1)}, f32[1,320]{1,0:T(1,128)}, u32[]{:S(2)}) copy-start(f32[1,320]{1,0:T(1,128)} %get-tuple-element.158) | copy-start | bytes 3844
  109.3 15.0 %collective-permute-start.4 = (bf16[3,4,24,256]{3,2,1,0:T(8,128)(2,1)}, bf16[3,4,24,256]{3,2,1,0:T(8,128)(2,1)}, u32[]{:S(2)}, u32[]{:S(2)}) collective-permute-start(bf16[3,4,24,256]{3,2,1,0:T(8,128)(2,1)} %bitcast.8), channel_id=1, source_target_pairs={{0,1},{1,2},{2,3},{3,4},{4,5},{5,6},{6,7},{8,9},{9,10},{10,11},{11... | collective-permute-start | bytes 442376 | tf_op jit(solution)/shard_map/ppermute | solution.py:443
  113.1 11.1 %collective-permute-start.5 = (bf16[3,4,24,256]{3,2,1,0:T(8,128)(2,1)}, bf16[3,4,24,256]{3,2,1,0:T(8,128)(2,1)}, u32[]{:S(2)}, u32[]{:S(2)}) collective-permute-start(bf16[3,4,24,256]{3,2,1,0:T(8,128)(2,1)} %bitcast.10), channel_id=1, source_target_pairs={{1,0},{2,1},{3,2},{4,3},{5,4},{6,5},{7,6},{9,8},{10,9},{11,10},{12... | collective-permute-start | bytes 442376 | tf_op jit(solution)/shard_map/ppermute | solution.py:443
  122.3 6.7 %copy-start.42 = (f32[1,80]{1,0:T(1,128)S(1)}, f32[1,80]{1,0:T(1,128)}, u32[]{:S(2)}) copy-start(f32[1,80]{1,0:T(1,128)} %get-tuple-element.168) | copy-start | bytes 964
  122.3 7.3 %copy-start.10 = (bf16[1,80,320]{1,2,0:T(8,128)(2,1)S(1)}, bf16[1,80,320]{1,2,0:T(8,128)(2,1)}, u32[]{:S(2)}) copy-start(bf16[1,80,320]{1,2,0:T(8,128)(2,1)} %copy-done.9) | copy-start | bytes 153604
  122.3 8.3 %copy-start.6 = (bf16[1,320,80]{2,1,0:T(8,128)(2,1)S(1)}, bf16[1,320,80]{2,1,0:T(8,128)(2,1)}, u32[]{:S(2)}) copy-start(bf16[1,320,80]{2,1,0:T(8,128)(2,1)} %copy-done.5) | copy-start | bytes 153604
  122.3 8.3 %copy-start.8 = (bf16[1,80,320]{1,2,0:T(8,128)(2,1)S(1)}, bf16[1,80,320]{1,2,0:T(8,128)(2,1)}, u32[]{:S(2)}) copy-start(bf16[1,80,320]{1,2,0:T(8,128)(2,1)} %copy-done.7) | copy-start | bytes 153604
  125.2 10.1 %collective-permute-start.6 = (bf16[30,1,24,256]{3,2,1,0:T(8,128)(2,1)S(1)}, bf16[30,1,24,256]{3,2,1,0:T(8,128)(2,1)S(1)}, u32[]{:S(2)}, u32[]{:S(2)}) collective-permute-start(bf16[30,1,24,256]{3,2,1,0:T(8,128)(2,1)S(1)} %get-tuple-element.110), channel_id=1, source_target_pairs={{0,8},{8,16},{16,24},{1,9},{9,17},{17,25},{2,10},{10,18},{18,26},{... | collective-permute-start | bytes 1105928 | tf_op jit(solution)/shard_map/ppermute | solution.py:443
  127.1 12.6 %collective-permute-start.7 = (bf16[30,1,24,256]{3,2,1,0:T(8,128)(2,1)S(1)}, bf16[30,1,24,256]{3,2,1,0:T(8,128)(2,1)S(1)}, u32[]{:S(2)}, u32[]{:S(2)}) collective-permute-start(bf16[30,1,24,256]{3,2,1,0:T(8,128)(2,1)S(1)} %get-tuple-element.111), channel_id=1, source_target_pairs={{8,0},{16,8},{24,16},{9,1},{17,9},{25,17},{10,2},{18,10},{26,18},{... | collective-permute-start | bytes 1105928 | tf_op jit(solution)/shard_map/ppermute | solution.py:443
  131.8 10.5 %copy-start.35 = (f32[24]{0:T(128)S(1)}, f32[24]{0:T(128)}, u32[]{:S(2)}) copy-start(f32[24]{0:T(128)} %get-tuple-element.162) | copy-start | bytes 292
  214.0 11.3 %copy-start.2 = (bf16[2304,256]{1,0:T(8,128)(2,1)S(1)}, bf16[2304,256]{1,0:T(8,128)(2,1)}, u32[]{:S(2)}) copy-start(bf16[2304,256]{1,0:T(8,128)(2,1)} %get-tuple-element.61.dconv) | copy-start | bytes 3538948
  214.0 18.0 %copy-start.24 = (f32[24,1024]{1,0:T(8,128)S(1)}, f32[24,1024]{1,0:T(8,128)}, u32[]{:S(2)}) copy-start(f32[24,1024]{1,0:T(8,128)} %get-tuple-element.76) | copy-start | bytes 294916
  214.0 18.0 %copy-start.22 = (f32[24,1024]{1,0:T(8,128)S(1)}, f32[24,1024]{1,0:T(8,128)}, u32[]{:S(2)}) copy-start(f32[24,1024]{1,0:T(8,128)} %get-tuple-element.77) | copy-start | bytes 294916
  226.2 17.3 %copy-start.21 = (f32[4,24,256]{2,1,0:T(8,128)S(1)}, f32[4,24,256]{2,1,0:T(8,128)}, u32[]{:S(2)}) copy-start(f32[4,24,256]{2,1,0:T(8,128)} %get-tuple-element.75) | copy-start | bytes 294916
  226.3 18.0 %copy-start.4 = (bf16[2304,256]{1,0:T(8,128)(2,1)S(1)}, bf16[2304,256]{1,0:T(8,128)(2,1)}, u32[]{:S(2)}) copy-start(bf16[2304,256]{1,0:T(8,128)(2,1)} %get-tuple-element.60) | copy-start | bytes 3538948
  226.5 8.2 %collective-permute-start.8 = (bf16[3,4,24,256]{3,2,1,0:T(8,128)(2,1)S(1)}, bf16[3,4,24,256]{3,2,1,0:T(8,128)(2,1)S(1)}, u32[]{:S(2)}, u32[]{:S(2)}) collective-permute-start(bf16[3,4,24,256]{3,2,1,0:T(8,128)(2,1)S(1)} %bitcast.144), channel_id=1, source_target_pairs={{0,1},{1,2},{2,3},{3,4},{4,5},{5,6},{6,7},{8,9},{9,10},{10,11},{11... | collective-permute-start | bytes 442376 | tf_op jit(solution)/shard_map/ppermute | solution.py:443
  230.0 6.5 %collective-permute-start.9 = (bf16[3,4,24,256]{3,2,1,0:T(8,128)(2,1)S(1)}, bf16[3,4,24,256]{3,2,1,0:T(8,128)(2,1)S(1)}, u32[]{:S(2)}, u32[]{:S(2)}) collective-permute-start(bf16[3,4,24,256]{3,2,1,0:T(8,128)(2,1)S(1)} %bitcast.143), channel_id=1, source_target_pairs={{1,0},{2,1},{3,2},{4,3},{5,4},{6,5},{7,6},{9,8},{10,9},{11,10},{12... | collective-permute-start | bytes 442376 | tf_op jit(solution)/shard_map/ppermute | solution.py:443
  234.7 11.2 %copy-start.11 = (bf16[3,4,24,256]{3,2,1,0:T(8,128)(2,1)}, bf16[3,4,24,256]{3,2,1,0:T(8,128)(2,1)S(1)}, u32[]{:S(2)}) copy-start(bf16[3,4,24,256]{3,2,1,0:T(8,128)(2,1)S(1)} %collective-permute-done.8) | copy-start | bytes 442372
  236.5 9.4 %copy-start.13 = (bf16[3,4,24,256]{3,2,1,0:T(8,128)(2,1)}, bf16[3,4,24,256]{3,2,1,0:T(8,128)(2,1)S(1)}, u32[]{:S(2)}) copy-start(bf16[3,4,24,256]{3,2,1,0:T(8,128)(2,1)S(1)} %collective-permute-done.9) | copy-start | bytes 442372
  237.5 13.2 %collective-permute-start.10 = (bf16[30,1,24,256]{3,2,1,0:T(8,128)(2,1)}, bf16[30,1,24,256]{3,2,1,0:T(8,128)(2,1)}, u32[]{:S(2)}, u32[]{:S(2)}) collective-permute-start(bf16[30,1,24,256]{3,2,1,0:T(8,128)(2,1)} %get-tuple-element.108), channel_id=1, source_target_pairs={{0,8},{8,16},{16,24},{1,9},{9,17},{17,25},{2,10},{10,18},{18,26},{... | collective-permute-start | bytes 1105928 | tf_op jit(solution)/shard_map/ppermute | solution.py:443
  240.1 10.6 %collective-permute-start.11 = (bf16[30,1,24,256]{3,2,1,0:T(8,128)(2,1)}, bf16[30,1,24,256]{3,2,1,0:T(8,128)(2,1)}, u32[]{:S(2)}, u32[]{:S(2)}) collective-permute-start(bf16[30,1,24,256]{3,2,1,0:T(8,128)(2,1)} %get-tuple-element.109), channel_id=1, source_target_pairs={{8,0},{16,8},{24,16},{9,1},{17,9},{25,17},{10,2},{18,10},{26,18},{... | collective-permute-start | bytes 1105928 | tf_op jit(solution)/shard_map/ppermute | solution.py:443
  315.1 12.5 %copy-start.26 = (f32[24,1024]{1,0:T(8,128)S(1)}, f32[24,1024]{1,0:T(8,128)}, u32[]{:S(2)}) copy-start(f32[24,1024]{1,0:T(8,128)} %get-tuple-element.71) | copy-start | bytes 294916
  315.1 12.5 %copy-start.23 = (f32[24,1024]{1,0:T(8,128)S(1)}, f32[24,1024]{1,0:T(8,128)}, u32[]{:S(2)}) copy-start(f32[24,1024]{1,0:T(8,128)} %get-tuple-element.72) | copy-start | bytes 294916
  315.1 15.3 %copy-start.25 = (f32[4,24,256]{2,1,0:T(8,128)S(1)}, f32[4,24,256]{2,1,0:T(8,128)}, u32[]{:S(2)}) copy-start(f32[4,24,256]{2,1,0:T(8,128)} %get-tuple-element.70) | copy-start | bytes 294916
  326.3 4.3 %copy-start.16 = (f32[25600]{0:T(1024)S(1)}, f32[25600]{0:T(1024)}, u32[]{:S(2)}) copy-start(f32[25600]{0:T(1024)} %reshape.199) | copy-start | bytes 307204
  326.3 4.3 %copy-start.28 = (f32[640]{0:T(1024)S(1)}, f32[640]{0:T(1024)}, u32[]{:S(2)}) copy-start(f32[640]{0:T(1024)} %reshape.197) | copy-start | bytes 7684
  326.3 4.3 %copy-start.30 = (f32[320]{0:T(512)S(1)}, f32[320]{0:T(512)}, u32[]{:S(2)}) copy-start(f32[320]{0:T(512)} %reshape.196) | copy-start | bytes 3844
  329.1 31.2 %copy-start.1 = (bf16[2304,256]{1,0:T(8,128)(2,1)S(1)}, bf16[2304,256]{1,0:T(8,128)(2,1)}, u32[]{:S(2)}) copy-start(bf16[2304,256]{1,0:T(8,128)(2,1)} %get-tuple-element.69.dconv) | copy-start | bytes 3538948
  334.3 38.0 %copy-start.37 = (f32[1,320]{1,0:T(1,128)S(1)}, f32[1,320]{1,0:T(1,128)}, u32[]{:S(2)}) copy-start(f32[1,320]{1,0:T(1,128)} %get-tuple-element.81) | copy-start | bytes 3844
  334.3 38.0 %copy-start.38 = (f32[1,320]{1,0:T(1,128)S(1)}, f32[1,320]{1,0:T(1,128)}, u32[]{:S(2)}) copy-start(f32[1,320]{1,0:T(1,128)} %get-tuple-element.80) | copy-start | bytes 3844
  360.5 5.8 %collective-permute-start.12 = (bf16[3,4,24,256]{3,2,1,0:T(8,128)(2,1)S(1)}, bf16[3,4,24,256]{3,2,1,0:T(8,128)(2,1)S(1)}, u32[]{:S(2)}, u32[]{:S(2)}) collective-permute-start(bf16[3,4,24,256]{3,2,1,0:T(8,128)(2,1)S(1)} %bitcast.146), channel_id=1, source_target_pairs={{0,1},{1,2},{2,3},{3,4},{4,5},{5,6},{6,7},{8,9},{9,10},{10,11},{11... | collective-permute-start | bytes 442376 | tf_op jit(solution)/shard_map/ppermute | solution.py:443
  362.4 6.5 %collective-permute-start.13 = (bf16[3,4,24,256]{3,2,1,0:T(8,128)(2,1)S(1)}, bf16[3,4,24,256]{3,2,1,0:T(8,128)(2,1)S(1)}, u32[]{:S(2)}, u32[]{:S(2)}) collective-permute-start(bf16[3,4,24,256]{3,2,1,0:T(8,128)(2,1)S(1)} %bitcast.145), channel_id=1, source_target_pairs={{1,0},{2,1},{3,2},{4,3},{5,4},{6,5},{7,6},{9,8},{10,9},{11,10},{12... | collective-permute-start | bytes 442376 | tf_op jit(solution)/shard_map/ppermute | solution.py:443
  369.0 7.8 %collective-permute-start.14 = (bf16[30,1,24,256]{3,2,1,0:T(8,128)(2,1)S(1)}, bf16[30,1,24,256]{3,2,1,0:T(8,128)(2,1)S(1)}, u32[]{:S(2)}, u32[]{:S(2)}) collective-permute-start(bf16[30,1,24,256]{3,2,1,0:T(8,128)(2,1)S(1)} %get-tuple-element.106), channel_id=1, source_target_pairs={{0,8},{8,16},{16,24},{1,9},{9,17},{17,25},{2,10},{10,18},{18,26},{... | collective-permute-start | bytes 1105928 | tf_op jit(solution)/shard_map/ppermute | solution.py:443
  370.7 10.3 %collective-permute-start.15 = (bf16[30,1,24,256]{3,2,1,0:T(8,128)(2,1)S(1)}, bf16[30,1,24,256]{3,2,1,0:T(8,128)(2,1)S(1)}, u32[]{:S(2)}, u32[]{:S(2)}) collective-permute-start(bf16[30,1,24,256]{3,2,1,0:T(8,128)(2,1)S(1)} %get-tuple-element.107), channel_id=1, source_target_pairs={{8,0},{16,8},{24,16},{9,1},{17,9},{25,17},{10,2},{18,10},{26,18},{... | collective-permute-start | bytes 1105928 | tf_op jit(solution)/shard_map/ppermute | solution.py:443
  (12 other events, 33.6 us)

commit v2 on v0

v2 whole, which is shorter than its diff:
```python
import functools

import jax
import jax.numpy as jnp
import numpy as np
from jax import lax
from jax.experimental import pallas as pl
from jax.experimental.pallas import tpu as pltpu
from jax.sharding import PartitionSpec as P

EPSILON = 1e-6
RADIUS = 3
TAPS = 2 * RADIUS + 1
MESH = pl.DeviceIdType.MESH
F32 = jnp.float32
BF16 = jnp.bfloat16
KEEP = 4.0 / 3.0
VMEM_LIMIT = 60 * 1024 * 1024
FULL = pl.BlockSpec(memory_space=pltpu.VMEM)
WHOLE = None
CONV_B, NORM_G, NORM_B, FC2_B = range(4)
FC1_B, BETA = range(2)
ONE, TWO = range(2)


def round_up(value, unit):
    return (value + unit - 1) // unit * unit


class Dims:
    def lanes(self, g):
        return slice(g * self.cp, (g + 1) * self.cp)

    def __init__(self, act_shape, hidden):
        self.b, self.h, self.w, self.c = act_shape
        self.hid = hidden
        self.nw = self.w // RADIUS
        self.cp = round_up(RADIUS * self.c, 128)
        self.hp = round_up(RADIUS * hidden, 128)
        self.rw = self.nw * self.b
        self.rows = self.h * self.rw
        self.inner = slice(self.b, self.b + self.rw)
        self.cs = [slice(q * self.c, (q + 1) * self.c) for q in range(RADIUS)]
        self.hs = [slice(q * hidden, (q + 1) * hidden) for q in range(RADIUS)]


def dot(lhs, rhs):
    return jnp.dot(lhs, rhs, preferred_element_type=F32)


def dot_t(lhs, rhs):
    return lax.dot_general(lhs, rhs, (((0,), (0,)), ((), ())), preferred_element_type=F32)


def dot_split(values, rhs):
    hi = values.astype(BF16)
    rest = values - hi.astype(F32)
    mid = rest.astype(BF16)
    low = (rest - mid.astype(F32)).astype(BF16)
    return dot(hi, rhs) + dot(mid, rhs) + dot(low, rhs)


def build_wide(dm, src_ref, wide):

    def body(row, carry):
        block = src_ref[row]
        for g in range(RADIUS):
            wide[pl.ds(pl.multiple_of(row * dm.rw, 16), dm.rw), dm.lanes(g)] = block[g * dm.b:g * dm.b + dm.rw]
        return carry

    lax.fori_loop(0, dm.h + 2 * RADIUS, body, 0)


def build_toeplitz(dm, taps_ref, rel_ref, toep):
    def body(i, carry):
        for g in range(RADIUS):
            acc = jnp.zeros((dm.cp, dm.cp), F32)
            for dj in range(-2, 3):
                j = 3 * g + dj
                if 0 <= j < TAPS:
                    acc = jnp.where(rel_ref[...] == dj, taps_ref[pl.ds(i * 8 + j, 1), :], acc)
            toep[pl.ds(pl.multiple_of((i * 3 + g) * dm.cp, 16), dm.cp), :] = acc.astype(BF16)
        return carry

    lax.fori_loop(0, TAPS, body, 0)


def conv_tile(dm, wide, toep, first_row, th):
    m = th * dm.rw
    acc = None
    for i in range(TAPS):
        rows = pl.ds(pl.multiple_of((first_row + i) * dm.rw, 16), m)
        part = dot(wide[rows, :], toep[i * 3 * dm.cp:(i + 1) * 3 * dm.cp, :])
        acc = part if acc is None else acc + part
    return acc


def lane_loop(dm, th, body):
    def outer(r, carry):
        def inner(lane, c2):
            rows = pl.ds(pl.multiple_of(r * dm.rw, 16), dm.rw)
            body(rows, pl.ds(pl.multiple_of(lane * 128, 128), 128))
            return c2
        return lax.fori_loop(0, dm.hp // 128, inner, carry)
    lax.fori_loop(0, th, outer, 0)


def line(ref, k, row, lanes=slice(None)):
    return ref[k, row:row + 1, lanes]


def image_lines(ref, lanes):
    return ref[:, lanes][None]


def per_image(dm, values):
    return values.reshape(dm.nw, dm.b, values.shape[-1])


def phi_of(hv):
    return 0.5 + 0.5 * lax.erf(hv * np.float32(0.7071067811865476))


def gelu_chunk(dm, h_ref, phi_ref, rows, lanes):
    hv = h_ref[rows, lanes].astype(F32)
    phi = phi_of(hv)
    phi_ref[rows, lanes] = phi
    return hv * phi


def forward_tile(dm, k, th, first, wide, toep, cvec, hvec, ones, w1, normed_o, inv_o, h_o):
    d = (conv_tile(dm, wide, toep, first, th) + line(cvec, k, CONV_B)).astype(BF16)
    mean = dot(d, ones[...]) * np.float32(1.0 / dm.c)
    centered = d.astype(F32) - mean
    var = dot_split(centered * centered, ones[...]) * np.float32(1.0 / dm.c)
    inv = lax.rsqrt(var + EPSILON)
    normed = centered * inv
    normed_o[...] = normed
    inv_o[...] = inv
    n = (normed * line(cvec, k, NORM_G) + line(cvec, k, NORM_B)).astype(BF16)
    h_o[...] = (dot(n, w1[k]) + line(hvec, k, FC1_B)).astype(BF16)


def dot_bt(lhs, rhs):
    return lax.dot_general(lhs, rhs, (((1,), (1,)), ((), ())), preferred_element_type=F32)


def cross_chunk(dm, k, raw, mask, g, dr_o, cross, sdr, rows, lanes):
    dr = (per_image(dm, raw[rows, lanes]) * mask[k, :, :128][None]).astype(BF16)
    dr_o[rows, lanes] = dr.reshape(dm.rw, 128)
    dr32 = dr.astype(F32)
    cross[:, lanes] += jnp.sum(dr32 * per_image(dm, g), axis=0)
    sdr[:, lanes] += jnp.sum(dr32, axis=0)


def position():
    sh = lax.axis_index('sh')
    return sh // 2, sh % 2, lax.axis_index('sw')


def peers_of(grid):
    chip, core, sw = position()
    n_chip, n_sw = grid[0] // 2, grid[1]
    pair = {'sh': chip * 2 + 1 - core}
    row = [{'sh': lax.rem(chip + j, n_chip) * 2 + core} for j in range(1, n_chip)]
    col = [{'sw': lax.rem(sw + j, n_sw)} for j in range(1, n_sw)]
    return pair, row, col


DIRECTIONS = [(0, 1), (0, -1), (1, 0), (-1, 0), (1, 1), (1, -1), (-1, 1), (-1, -1)]


def greet(grid, halo, reduce):
    devices = []
    if halo:
        sh, sw = lax.axis_index('sh'), lax.axis_index('sw')
        for dh, dw in DIRECTIONS:
            devices.append({'sh': lax.rem(sh + dh + grid[0], grid[0]), 'sw': lax.rem(sw + dw + grid[1], grid[1])})
    if reduce:
        pair, row, col = peers_of(grid)
        devices += [pair] + row + col
    barrier = pltpu.get_barrier_semaphore()
    for device in devices:
        pl.semaphore_signal(barrier, inc=1, device_id=device, device_id_type=MESH)
    pl.semaphore_wait(barrier, len(devices))


def clear_halo(dm, xp):
    b, r = dm.b, RADIUS
    edge = (dm.nw + 1) * b
    xp[:r] = jnp.zeros((r,) + xp.shape[1:], BF16)
    xp[dm.h + r:] = jnp.zeros((r,) + xp.shape[1:], BF16)
    xp[r:dm.h + r, :b] = jnp.zeros((dm.h, b, dm.cp), BF16)
    xp[r:dm.h + r, edge:] = jnp.zeros((dm.h, b, dm.cp), BF16)


def halo_copies(dm, grid, xp, send_sem, recv_sem):
    sh, sw = lax.axis_index('sh'), lax.axis_index('sw')
    r, b = RADIUS, dm.b
    rows = {1: (dm.h, r, 0), -1: (r, r, dm.h + r), 0: (r, dm.h, r)}
    cols = {1: (dm.nw * b, b, 0), -1: (b, b, (dm.nw + 1) * b), 0: (b, dm.nw * b, b)}

    def inside(a, c):
        return (a >= 0) & (a < grid[0]) & (c >= 0) & (c < grid[1])

    found = []
    for d, (dh, dw) in enumerate(DIRECTIONS):
        r0, rn, rt = rows[dh]
        c0, cn, ct = cols[dw]
        target = {'sh': lax.rem(sh + dh + grid[0], grid[0]), 'sw': lax.rem(sw + dw + grid[1], grid[1])}
        copy = pltpu.make_async_remote_copy(
            src_ref=xp.at[pl.ds(r0, rn), pl.ds(c0, cn)], dst_ref=xp.at[pl.ds(rt, rn), pl.ds(ct, cn)],
            send_sem=send_sem.at[d], recv_sem=recv_sem.at[d], device_id=target, device_id_type=MESH)
        found.append((copy, inside(sh + dh, sw + dw), inside(sh - dh, sw - dw)))
    return found


def halo_start(copies):
    for copy, sends, _ in copies:
        @pl.when(sends)
        def _():
            copy.start()


def halo_wait(copies):
    for copy, sends, receives in copies:
        @pl.when(sends)
        def _():
            copy.wait_send()

        @pl.when(receives)
        def _():
            copy.wait_recv()


def exchange(slots, mine, devices, send_sem, recv_sem):
    copies = []
    for j, device in enumerate(devices):
        copy = pltpu.make_async_remote_copy(src_ref=slots.at[mine], dst_ref=slots.at[mine], send_sem=send_sem.at[j],
                                            recv_sem=recv_sem.at[j], device_id=device, device_id_type=MESH)
        copies.append(copy)
    return copies


def go(copies):
    for copy in copies:
        copy.start()


def finish(copies):
    for copy in copies:
        copy.wait()


def fold(values, parts):
    return sum(values[:, part] for part in parts)


def sum_slots(slots):
    total = slots[0]
    for j in range(1, slots.shape[0]):
        total = total + slots[j]
    return total


def grn_scratch(dm, grid, count):
    n_chip, n_sw = grid[0] // 2, grid[1]
    dma = pltpu.SemaphoreType.DMA
    block = (count, dm.b, dm.hid)
    return [pltpu.VMEM((2,) + block, F32), pltpu.VMEM((n_chip,) + block, F32), pltpu.VMEM((n_sw,) + block, F32),
            dma((1,)), dma((1,)), dma((n_chip - 1,)), dma((n_chip - 1,)), dma((n_sw - 1,)), dma((n_sw - 1,))]


def grn_total(dm, grid, sums, scratch):
    slots1, slots2, slots3, send1, recv1, send2, recv2, send3, recv3 = scratch
    chip, core, sw = position()
    pair, row, col = peers_of(grid)
    for j, ref in enumerate(sums):
        slots1[core, j] = fold(ref, dm.hs)
    for slots, mine, devices, send, recv, after in ((slots1, core, [pair], send1, recv1, (slots2, chip)),
                                                   (slots2, chip, row, send2, recv2, (slots3, sw)),
                                                   (slots3, sw, col, send3, recv3, WHOLE)):
        copies = exchange(slots, mine, devices, send, recv)
        go(copies)
        finish(copies)
        total = sum_slots(slots)
        if after:
            after[0][after[1]] = total
    return total


def spread(dm, ref, values):
    ref[...] = jnp.zeros_like(ref)
    for part in dm.hs:
        ref[:, part] = values


def grn_cross(dm, norm, gamma, cross, dsq_o, ggam_o):
    mean = jnp.mean(norm, axis=-1, keepdims=True) + EPSILON
    d_scale = gamma * cross
    d_norm = d_scale / mean - jnp.sum(d_scale * norm, axis=-1, keepdims=True) / (mean * mean * dm.hid)
    spread(dm, dsq_o, d_norm / norm)
    ggam_o[...] = jnp.sum(cross * (norm / mean), axis=0, keepdims=True)


def grn_coef(dm, norm, gamma, coef_o):
    mean = jnp.mean(norm, axis=-1, keepdims=True) + EPSILON
    spread(dm, coef_o, gamma * (norm / mean) + 1.0)


def prep_kernel(dm, conv_w, conv_b, norm_g, norm_b, fc1_w, fc1_b, beta, fc2_w, fc2_b, mask_i, ones,
                taps_o, cvec_o, hvec_o, w1_o, w2_o, gmat_o, mask_o):
    for ref in (taps_o, cvec_o, hvec_o, w1_o, w2_o):
        ref[...] = jnp.zeros_like(ref)
    for k in range(2):
        for q in range(RADIUS):
            cs, hs = dm.cs[q], dm.hs[q]
            for i in range(TAPS):
                rows = conv_w[k, i].astype(F32)
                taps_o[k, i * 8:i * 8 + TAPS, cs] = rows
                for j in range(TAPS):
                    taps_o[2 + k, pl.ds((TAPS - 1 - i) * 8 + TAPS - 1 - j, 1), cs] = rows[j:j + 1]
            for j, ref in enumerate((conv_b, norm_g, norm_b, fc2_b)):
                cvec_o[k, j:j + 1, cs] = ref[k:k + 1, :]
            for j, ref in enumerate((fc1_b, beta)):
                hvec_o[k, j:j + 1, hs] = ref[k:k + 1, :]
            w1_o[k, cs, hs] = fc1_w[k]
            w2_o[k, hs, cs] = fc2_w[k]
        mask_o[k] = jnp.broadcast_to(mask_i[:, k:k + 1], (dm.b, dm.cp))
    for k in range(2):
        values = ones[...].astype(F32) * line(cvec_o, k, NORM_G)
        for j in range(RADIUS):
            part = values.astype(BF16)
            gmat_o[k, j] = part
            values = values - part.astype(F32)


def first_kernel(dm, grid, th, x, taps, rel, cvec, hvec, ones, w1, gamma,
                 normed_o, inv_o, h_o, phi_o, xp_o, norm_o, coef_o, wide, toep, ss, xp, keep_sem, send, recv, *grn):
    step = pl.program_id(0)

    @pl.when(step == 0)
    def _():
        clear_halo(dm, xp)
        for row in range(dm.h):
            xp[row + RADIUS, dm.inner] = x[row * dm.rw:(row + 1) * dm.rw]
        greet(grid, True, True)
        copies = halo_copies(dm, grid, xp, send, recv)
        halo_start(copies)
        build_toeplitz(dm, taps.at[0], rel, toep)
        ss[...] = jnp.zeros_like(ss)
        halo_wait(copies)
        pltpu.make_async_copy(xp, xp_o, keep_sem).start()
        build_wide(dm, xp, wide)

    forward_tile(dm, 0, th, step * th, wide, toep, cvec, hvec, ones, w1, normed_o, inv_o, h_o)

    def body(rows, lanes):
        g = gelu_chunk(dm, h_o, phi_o, rows, lanes)
        ss[:, lanes] += jnp.sum(per_image(dm, g * g), axis=0)

    lane_loop(dm, th, body)

    @pl.when(step == pl.num_programs(0) - 1)
    def _():
        pltpu.make_async_copy(xp, xp_o, keep_sem).wait()
        norm = jnp.sqrt(grn_total(dm, grid, [ss], grn)[0])
        norm_o[...] = norm
        grn_coef(dm, norm, gamma[pl.ds(ONE, 1), :], coef_o)


def second_kernel(dm, grid, th, h1, phi1, x1, coef1, taps, rel, cvec, hvec, ones, w1, w2, gamma, mask, dout,
                  normed_o, inv_o, h_o, phi_o, dr_o, xp_o, sdr_o, coef_o, dsq_o, ggam_o,
                  wide, toep, resp, raw, ss, cross, xp, keep_sem, send, recv, *grn):
    step = pl.program_id(0)
    tiles = dm.h // th

    @pl.when(step == 0)
    def _():
        clear_halo(dm, xp)
        greet(grid, True, True)
        for ref in (ss, cross, sdr_o):
            ref[...] = jnp.zeros_like(ref)

    @pl.when(step < tiles)
    def _():
        def body(rows, lanes):
            g = h1[rows, lanes].astype(F32) * phi1[rows, lanes]
            r = per_image(dm, g) * image_lines(coef1, lanes) + line(hvec, ONE, BETA, lanes)
            resp[rows, lanes] = r.reshape(dm.rw, 128).astype(BF16)

        lane_loop(dm, th, body)
        o = (dot(resp[...], w2[ONE]) + line(cvec, ONE, FC2_B)).reshape(-1, dm.b, dm.cp)
        y = (x1[...].astype(F32) + (o * mask[ONE][None]).reshape(-1, dm.cp)).astype(BF16)
        for r in range(th):
            xp[step * th + r + RADIUS, dm.inner] = y[r * dm.rw:(r + 1) * dm.rw]

    @pl.when(step == tiles)
    def _():
        copies = halo_copies(dm, grid, xp, send, recv)
        halo_start(copies)
        build_toeplitz(dm, taps.at[1], rel, toep)
        halo_wait(copies)
        pltpu.make_async_copy(xp, xp_o, keep_sem).start()
        build_wide(dm, xp, wide)

    @pl.when(step >= tiles)
    def _():
        forward_tile(dm, 1, th, (step - tiles) * th, wide, toep, cvec, hvec, ones, w1, normed_o, inv_o, h_o)
        raw[...] = dot_bt(dout[...], w2[TWO])

        def body(rows, lanes):
            g = gelu_chunk(dm, h_o, phi_o, rows, lanes)
            ss[:, lanes] += jnp.sum(per_image(dm, g * g), axis=0)
            cross_chunk(dm, 1, raw, mask, g, dr_o, cross, sdr_o, rows, lanes)

        lane_loop(dm, th, body)

    @pl.when(step == pl.num_programs(0) - 1)
    def _():
        pltpu.make_async_copy(xp, xp_o, keep_sem).wait()
        total = grn_total(dm, grid, [ss, cross], grn)
        norm = jnp.sqrt(total[0])
        grn_coef(dm, norm, gamma[pl.ds(TWO, 1), :], coef_o)
        grn_cross(dm, norm, gamma[pl.ds(TWO, 1), :], total[1], dsq_o, ggam_o)


def backward_tile(dm, k, h_i, phi_i, dr_i, coef, dsq, dout, normed_i, inv_i, cvec, hvec, ones, gmat, w1, w2, mask,
                  resp, dh, gfc1, gfc2, sdh, sums, th, x_rows, y_o):
    def body(rows, lanes):
        hv = h_i[rows, lanes].astype(F32)
        phi = phi_i[rows, lanes]
        g = per_image(dm, hv * phi)
        a = image_lines(coef, lanes)
        resp[rows, lanes] = (g * a + line(hvec, k, BETA, lanes)).reshape(dm.rw, 128).astype(BF16)
        slope = phi + hv * (np.float32(0.3989422804014327) * jnp.exp(-0.5 * hv * hv))
        dg = per_image(dm, dr_i[rows, lanes].astype(F32)) * a + g * image_lines(dsq, lanes)
        dhv = (dg.reshape(dm.rw, 128) * slope).astype(BF16)
        dh[rows, lanes] = dhv
        sdh[:, lanes] += jnp.sum(per_image(dm, dhv.astype(F32)), axis=0)

    lane_loop(dm, th, body)
    dsel32 = jnp.where((mask[k] != 0.0)[None], dout[...].astype(F32).reshape(-1, dm.b, dm.cp), 0.0)
    sums[FC2_B] += jnp.sum(dsel32, axis=0)
    gfc2[...] += dot_t(dsel32.reshape(-1, dm.cp).astype(BF16), resp[...])
    if y_o is not None:
        o = (dot(resp[...], w2[k]) + line(cvec, k, FC2_B)).reshape(-1, dm.b, dm.cp)
        y_o[...] = (x_rows.astype(F32) + (o * mask[k][None]).reshape(-1, dm.cp)).astype(BF16)
    normed = normed_i[...]
    norm_g = line(cvec, k, NORM_G)
    n = (normed * norm_g + line(cvec, k, NORM_B)).astype(BF16)
    gfc1[...] += dot_t(n, dh[...])
    dn16 = dot_bt(dh[...], w1[k]).astype(BF16)
    dn = dn16.astype(F32)
    scale = np.float32(1.0 / dm.c)
    mean1 = (dot_bt(dn16, gmat[k, 0]) + dot_bt(dn16, gmat[k, 1]) + dot_bt(dn16, gmat[k, 2])) * scale
    dnormed = dn * norm_g
    mean2 = dot_split(dnormed * normed, ones[...]) * scale
    dconv = (inv_i[...] * (dnormed - mean1 - normed * mean2)).astype(BF16)

    for row, values in ((CONV_B, dconv.astype(F32)), (NORM_G, dn * normed), (NORM_B, dn)):
        sums[row] += jnp.sum(values.reshape(-1, dm.b, dm.cp), axis=0)
    return dconv


def wgrad(dm, wide, dcol, rel, out):
    keep = rel[...] > -50

    def body(i, carry):
        rows = pl.ds(pl.multiple_of(i * dm.rw, 16), dm.rows)
        res = dot(dcol[...], wide[rows, :])
        for g in range(RADIUS):
            part = jnp.where(keep, res[:, dm.lanes(g)], 0.0)
            for q in range(RADIUS):
                out[q, pl.ds(i, 1), dm.lanes(g)] = jnp.sum(part[dm.cs[q]], axis=0, keepdims=True)
        return carry

    lax.fori_loop(0, TAPS, body, 0)


PACK_ROWS = 256


def pack_grads(dm, pack, gfc1, gfc2, corr, sdh, sdr, sums):
    c, hid = dm.c, dm.hid
    for base, ref in ((0, gfc1), (c, gfc2)):
        pack[base:base + c, :hid] = sum(ref[cs, hs] for cs, hs in zip(dm.cs, dm.hs))
    base = 2 * c
    for j in range(TAPS):
        total = None
        for q in range(RADIUS):
            p = q + j
            lane = (p // 3) * dm.cp + (p % 3) * c
            part = corr[q, :, lane:lane + c]
            total = part if total is None else total + part
        pack[base + 8 * j:base + 8 * j + 8, :c] = total
    base += 8 * TAPS
    for row, ref in enumerate((sdh, sdr)):
        vec = jnp.sum(ref[...], axis=0, keepdims=True)
        pack[base + row:base + row + 1, :hid] = fold(vec, dm.hs)
    for row in range(4):
        vec = jnp.sum(sums[row], axis=0, keepdims=True)
        pack[base + 2 + row:base + 3 + row, :c] = fold(vec, dm.cs)


def pack_shape(dm, grid):
    return (PACK_ROWS, round_up(dm.hid, 128))


def sum_scratch(dm, grid):
    rows, lanes = pack_shape(dm, grid)
    n_chip, n_sw = grid[0] // 2, grid[1]
    half, chunk = rows // 2, rows // (2 * n_chip)
    dma = pltpu.SemaphoreType.DMA
    return [pltpu.VMEM((half, lanes), F32), pltpu.VMEM((n_chip, chunk, lanes), F32), pltpu.VMEM((n_chip, chunk, lanes), F32),
            pltpu.VMEM((n_chip, chunk, lanes), F32), pltpu.VMEM((n_sw, chunk, lanes), F32),
            dma((1,)), dma((1,)), dma((n_chip - 1,)), dma((n_chip - 1,)), dma((n_sw - 1,)), dma((n_sw - 1,)),
            dma((n_chip - 1,)), dma((n_chip - 1,)), dma((1,)), dma((1,))]


N_SUM = 15


def sum_stages(grid, x, out, scratch):
    got1, half, got2, part, slots3, send1, recv1, send2, recv2, send3, recv3, send4, recv4, send5, recv5 = scratch
    chip, core, sw = position()
    n_chip = grid[0] // 2
    pair, row, col = peers_of(grid)
    rows = got1.shape[0]
    chunk = half.shape[1]

    def whole(ref, which):
        return ref.at[pl.ds(pl.multiple_of(which * rows, 8), rows)]

    def copies1():
        return [pltpu.make_async_remote_copy(src_ref=whole(x, 1 - core), dst_ref=got1, send_sem=send1.at[0], recv_sem=recv1.at[0],
                                             device_id=pair, device_id_type=MESH)]

    def copies2():
        made = []
        for j, device in enumerate(row):
            made.append(pltpu.make_async_remote_copy(
                src_ref=half.at[lax.rem(chip + j + 1, n_chip)], dst_ref=got2.at[chip], send_sem=send2.at[j],
                recv_sem=recv2.at[j], device_id=device, device_id_type=MESH))
        return made

    def copies5():
        return [pltpu.make_async_remote_copy(src_ref=whole(out, core), dst_ref=whole(out, core), send_sem=send5.at[0],
                                             recv_sem=recv5.at[0], device_id=pair, device_id_type=MESH)]

    def stage0():
        go(copies1())

    def stage1():
        finish(copies1())
        for j in range(n_chip):
            start = pl.multiple_of(core * rows + j * chunk, 8)
            half[j] = x[pl.ds(start, chunk)] + got1[j * chunk:(j + 1) * chunk]
        go(copies2())

    def stage2():
        got2[chip] = half[chip]
        finish(copies2())
        slots3[sw] = sum_slots(got2)
        go(exchange(slots3, sw, col, send3, recv3))

    def stage3():
        finish(exchange(slots3, sw, col, send3, recv3))
        part[chip] = sum_slots(slots3)
        go(exchange(part, chip, row, send4, recv4))

    def stage4():
        finish(exchange(part, chip, row, send4, recv4))
        for j in range(n_chip):
            out[pl.ds(pl.multiple_of(core * rows + j * chunk, 8), chunk)] = part[j]
        go(copies5())

    def stage5():
        finish(copies5())

    return [stage0, stage1, stage2, stage3, stage4, stage5]


def third_kernel(dm, grid, th, h2, phi2, dr2, coef2, dsq2, dout, normed, inv, xp2, h1, phi1, norm1, taps, rel, cvec, hvec, ones, gmat,
                 w1, w2, gamma, mask, sdr2,
                 y_o, d1_o, dr1_o, pack, sdr_o, dsq_o, ggam_o,
                 wide, toep, dp, dcol, corr, resp, dh, raw, gfc1, gfc2, sdh, sums, cross, send, recv, *grn):
    step = pl.program_id(0)
    tiles = dm.h // th

    @pl.when(step == 0)
    def _():
        clear_halo(dm, dp)
        greet(grid, True, True)
        build_wide(dm, xp2, wide)
        for ref in (cross, sdr_o, gfc1, gfc2, sdh, sums, corr, pack):
            ref[...] = jnp.zeros_like(ref)

    @pl.when(step < tiles)
    def _():
        x_rows = jnp.concatenate([xp2[step * th + r + RADIUS, dm.inner] for r in range(th)], axis=0)
        dconv = backward_tile(dm, 1, h2, phi2, dr2, coef2, dsq2, dout, normed, inv, cvec, hvec, ones, gmat, w1, w2, mask,
                              resp, dh, gfc1, gfc2, sdh, sums, th, x_rows, y_o)
        for r in range(th):
            dp[step * th + r + RADIUS, dm.inner] = dconv[r * dm.rw:(r + 1) * dm.rw]
        for j in range(tiles):
            @pl.when(step == j)
            def _():
                dcol[:, j * th * dm.rw:(j + 1) * th * dm.rw] = dconv.T

    @pl.when(step == tiles)
    def _():
        copies = halo_copies(dm, grid, dp, send, recv)
        halo_start(copies)
        build_toeplitz(dm, taps.at[3], rel, toep)
        wgrad(dm, wide, dcol, rel, corr)
        pack_grads(dm, pack, gfc1, gfc2, corr, sdh, sdr2, sums)
        halo_wait(copies)
        build_wide(dm, dp, wide)

    @pl.when(step >= tiles)
    def _():
        din = (dout[...].astype(F32) + conv_tile(dm, wide, toep, (step - tiles) * th, th)).astype(BF16)
        d1_o[...] = din
        raw[...] = dot_bt(din, w2[ONE])

        def body(rows, lanes):
            g = h1[rows, lanes].astype(F32) * phi1[rows, lanes]
            cross_chunk(dm, 0, raw, mask, g, dr1_o, cross, sdr_o, rows, lanes)

        lane_loop(dm, th, body)

    @pl.when(step == pl.num_programs(0) - 1)
    def _():
        total = grn_total(dm, grid, [cross], grn)
        grn_cross(dm, norm1[...], gamma[pl.ds(ONE, 1), :], total[0], dsq_o, ggam_o)


def fourth_kernel(dm, grid, th, h1, phi1, dr1, coef1, dsq1, d1, normed, inv, xp1, taps, rel, cvec, hvec, ones, gmat,
                  w1, w2, mask, sdr1, pack2_i,
                  d0_o, out1_o, out2_o,
                  wide, toep, dp, dcol, corr, resp, dh, gfc1, gfc2, sdh, sums, pack1, pack2, out1, out2, send, recv, *sem):
    step = pl.program_id(0)
    tiles = dm.h // th
    stages1 = sum_stages(grid, pack1, out1, sem[:N_SUM])
    stages2 = sum_stages(grid, pack2, out2, sem[N_SUM:])

    @pl.when(step == 0)
    def _():
        clear_halo(dm, dp)
        greet(grid, True, True)
        for ref in (gfc1, gfc2, sdh, sums, corr, pack1):
            ref[...] = jnp.zeros_like(ref)
        pack2[...] = pack2_i[...]

    for j in range(6):
        @pl.when(step == j)
        def _():
            stages2[j]()

        @pl.when(step == tiles + j)
        def _():
            if 0 < j < 5:
                stages1[j - 1]()

    @pl.when(step == 0)
    def _():
        build_wide(dm, xp1, wide)

    @pl.when(step < tiles)
    def _():
        dconv = backward_tile(dm, 0, h1, phi1, dr1, coef1, dsq1, d1, normed, inv, cvec, hvec, ones, gmat, w1, w2, mask,
                              resp, dh, gfc1, gfc2, sdh, sums, th, None, WHOLE)
        for r in range(th):
            dp[step * th + r + RADIUS, dm.inner] = dconv[r * dm.rw:(r + 1) * dm.rw]
        for j in range(tiles):
            @pl.when(step == j)
            def _():
                dcol[:, j * th * dm.rw:(j + 1) * th * dm.rw] = dconv.T

    @pl.when(step == tiles)
    def _():
        copies = halo_copies(dm, grid, dp, send, recv)
        halo_start(copies)
        build_toeplitz(dm, taps.at[2], rel, toep)
        wgrad(dm, wide, dcol, rel, corr)
        pack_grads(dm, pack1, gfc1, gfc2, corr, sdh, sdr1, sums)
        halo_wait(copies)
        build_wide(dm, dp, wide)

    @pl.when(step >= tiles)
    def _():
        din = (d1[...].astype(F32) + conv_tile(dm, wide, toep, (step - tiles) * th, th)).astype(BF16)
        d0_o[...] = din

    @pl.when(step == pl.num_programs(0) - 1)
    def _():
        stages1[4]()
        stages1[5]()
        out1_o[...] = out1[...]
        out2_o[...] = out2[...]


def final_kernel(dm, out1, out2, ggam1, ggam2, gcw, gcb, gng, gnb, gf1w, gf1b, ggam, gbeta, gf2w, gf2b):
    c, hid = dm.c, dm.hid
    ggam[...] = jnp.concatenate([ggam1[...], ggam2[...]], axis=0)
    for k, ref in enumerate((out1, out2)):
        gf1w[k] = ref[:c, :hid]
        gf2w[k] = ref[c:2 * c, :hid].T * np.float32(KEEP)
        base = 2 * c
        for j in range(TAPS):
            for i in range(TAPS):
                gcw[k, i, j:j + 1, :] = ref[base + 8 * j + i:base + 8 * j + i + 1, :c]
        base += 8 * TAPS
        for row, out in enumerate((gf1b, gbeta, gcb, gng, gnb, gf2b)):
            value = ref[base + row:base + row + 1, :out.shape[1]]
            out[k:k + 1, :] = value * np.float32(KEEP) if out is gf2b else value


def to_rows(dm, act):
    t = act.reshape(dm.b, dm.h, dm.nw, RADIUS * dm.c).transpose(1, 2, 0, 3)
    return jnp.pad(t, ((0, 0), (0, 0), (0, 0), (0, dm.cp - RADIUS * dm.c))).reshape(dm.rows, dm.cp)


def from_rows(dm, flat):
    t = flat.reshape(dm.h, dm.nw, dm.b, dm.cp)[..., :RADIUS * dm.c].transpose(2, 0, 1, 3)
    return t.reshape(dm.b, dm.h, dm.w, dm.c)


def constants(dm):
    index = np.arange(dm.cp)
    col, chan = index // dm.c, index % dm.c
    live = (index[:, None] < RADIUS * dm.c) & (index[None, :] < RADIUS * dm.c)
    rel = np.where((chan[:, None] == chan[None, :]) & live, col[:, None] - col[None, :], -100).astype(np.int32)
    ones = ((col[:, None] == col[None, :]) & live).astype(np.float32)
    return jnp.asarray(rel), jnp.asarray(ones, BF16)


def call(dm, th, kernel, steps, ins, outs, scratch, name, cid=None):
    m, tiles = th * dm.rw, dm.h // th

    def spec(shape, first):
        if first is None:
            return FULL
        if first == 'any':
            return pl.BlockSpec(memory_space=pl.ANY)
        if first == 'both':
            return pl.BlockSpec((m, shape[1]), lambda s: (lax.rem(s, tiles), 0))
        return pl.BlockSpec((m, shape[1]), lambda s: (jnp.clip(s - first, 0, tiles - 1), 0))

    return pl.pallas_call(
        kernel, grid=(steps,), in_specs=[spec(a.shape, first) for a, first in ins],
        out_specs=[spec(shape, first) for shape, _, first in outs],
        out_shape=[jax.ShapeDtypeStruct(shape, dtype) for shape, dtype, _ in outs],
        scratch_shapes=scratch, name=name,
        compiler_params=pltpu.CompilerParams(dimension_semantics=('arbitrary',), vmem_limit_bytes=VMEM_LIMIT,
                                             collective_id=cid, has_side_effects=True))(*[a for a, _ in ins])


def solution(mesh):
    grid = (mesh.shape['sh'], mesh.shape['sw'])
    act_spec = P('dp', 'sh', 'sw', WHOLE)
    replicated = P()

    def local_step(act_in, drop_mask, grad_out, conv_w, conv_b, norm_g, norm_b, fc1_w, fc1_b, gamma, grn_beta, fc2_w, fc2_b):
        dm = Dims(act_in.shape, fc1_w.shape[-1])
        th = 4
        tiles, m = dm.h // th, th * dm.rw
        rel, ones = constants(dm)
        sds = jax.ShapeDtypeStruct
        taps, cvec, hvec, w1, w2, gmat, mask = pl.pallas_call(
            functools.partial(prep_kernel, dm),
            out_shape=[sds((4, TAPS * 8, dm.cp), F32), sds((2, 4, dm.cp), F32), sds((2, 2, dm.hp), F32), sds((2, dm.cp, dm.hp), BF16),
                       sds((2, dm.hp, dm.cp), BF16), sds((2, 3, dm.cp, dm.cp), BF16), sds((2, dm.b, dm.cp), F32)],
            in_specs=[FULL] * 11, out_specs=[FULL] * 7, name='prep')(
                conv_w, conv_b, norm_g, norm_b, fc1_w, fc1_b, grn_beta, fc2_w, fc2_b, drop_mask, ones)

        dma = pltpu.SemaphoreType.DMA
        V = pltpu.VMEM
        wide_s = V(((dm.h + 2 * RADIUS) * dm.rw, 3 * dm.cp), BF16)
        toep_s = V((TAPS * 3 * dm.cp, dm.cp), BF16)
        raw_s, hid_s = V((m, dm.hp), F32), V((m, dm.hp), BF16)
        img_s = V((dm.b, dm.hp), F32)
        acc_s = V((dm.cp, dm.hp), F32)
        xp_shape = (dm.h + 2 * RADIUS, (dm.nw + 2) * dm.b, dm.cp)
        halo_s = [dma((8,)), dma((8,))]
        c_shape, h_shape, s_shape, n_shape = (dm.rows, dm.cp), (dm.rows, dm.hp), (dm.b, dm.hp), (dm.b, dm.hid)
        g_shape = (1, dm.hid)
        p_shape = pack_shape(dm, grid)

        x1 = to_rows(dm, act_in)
        d2 = to_rows(dm, grad_out)

        normed1, inv1, h1, phi1, xp1, norm1, coef1 = call(
            dm, th, functools.partial(first_kernel, dm, grid, th), tiles,
            [(a, WHOLE) for a in (x1, taps, rel, cvec, hvec, ones, w1, gamma)],
            [(c_shape, F32, 0), (c_shape, F32, 0), (h_shape, BF16, 0), (h_shape, F32, 0), (xp_shape, BF16, 'any'), (n_shape, F32, WHOLE),
             (s_shape, F32, WHOLE)],
            [wide_s, toep_s, img_s, V(xp_shape, BF16), dma] + halo_s + grn_scratch(dm, grid, 1), 'first', 0)

        normed2, inv2, h2, phi2, dr2, xp2, sdr2, coef2, dsq2, ggam2 = call(
            dm, th, functools.partial(second_kernel, dm, grid, th), 2 * tiles,
            [(h1, 0), (phi1, 0), (x1, 0), (coef1, WHOLE)] + [(a, WHOLE) for a in (taps, rel, cvec, hvec, ones, w1, w2, gamma, mask)]
            + [(d2, tiles)],
            [(c_shape, F32, tiles), (c_shape, F32, tiles), (h_shape, BF16, tiles), (h_shape, F32, tiles), (h_shape, BF16, tiles),
             (xp_shape, BF16, 'any'), (s_shape, F32, WHOLE), (s_shape, F32, WHOLE), (s_shape, F32, WHOLE), (g_shape, F32, WHOLE)],
            [wide_s, toep_s, hid_s, raw_s, img_s, img_s, V(xp_shape, BF16), dma] + halo_s + grn_scratch(dm, grid, 2), 'second', 1)

        bwd_s = [wide_s, toep_s, V(xp_shape, BF16), V((dm.cp, dm.rows), BF16), V((3, 8, 3 * dm.cp), F32), hid_s, hid_s]
        acc = [acc_s, acc_s, img_s, V((4, dm.b, dm.cp), F32)]
        y2, d1, dr1, pack2, sdr1, dsq1, ggam1 = call(
            dm, th, functools.partial(third_kernel, dm, grid, th), 2 * tiles,
            [(h2, 0), (phi2, 0), (dr2, 0), (coef2, WHOLE), (dsq2, WHOLE), (d2, 'both'), (normed2, 0), (inv2, 0), (xp2, WHOLE),
             (h1, tiles), (phi1, tiles)] + [(a, WHOLE) for a in (norm1, taps, rel, cvec, hvec, ones, gmat, w1, w2, gamma, mask, sdr2)],
            [(c_shape, BF16, 0), (c_shape, BF16, tiles), (h_shape, BF16, tiles), (p_shape, F32, WHOLE), (s_shape, F32, WHOLE),
             (s_shape, F32, WHOLE), (g_shape, F32, WHOLE)],
            bwd_s + [raw_s] + acc + [img_s] + halo_s + grn_scratch(dm, grid, 1), 'third', 2)

        d0, out1, out2 = call(
            dm, th, functools.partial(fourth_kernel, dm, grid, th), 2 * tiles,
            [(h1, 0), (phi1, 0), (dr1, 0), (coef1, WHOLE), (dsq1, WHOLE), (d1, 'both'), (normed1, 0), (inv1, 0), (xp1, WHOLE)]
            + [(a, WHOLE) for a in (taps, rel, cvec, hvec, ones, gmat, w1, w2, mask, sdr1, pack2)],
            [(c_shape, BF16, tiles), (p_shape, F32, WHOLE), (p_shape, F32, WHOLE)],
            bwd_s + acc + [V(p_shape, F32)] * 4 + halo_s + sum_scratch(dm, grid) * 2, 'fourth', 3)

        grads = pl.pallas_call(
            functools.partial(final_kernel, dm),
            out_shape=[sds(s, F32) for s in (conv_w.shape, conv_b.shape, norm_g.shape, norm_b.shape, fc1_w.shape, fc1_b.shape, gamma.shape,
                                             grn_beta.shape, fc2_w.shape, fc2_b.shape)],
            in_specs=[FULL] * 4, out_specs=[FULL] * 10, name='final')(out1, out2, ggam1, ggam2)
        return (from_rows(dm, y2), from_rows(dm, d0)) + tuple(grads)

    return jax.shard_map(local_step, mesh=mesh,
                         in_specs=(act_spec, P('dp', WHOLE), act_spec) + (replicated,) * 10,
                         out_specs=(act_spec, act_spec) + (P('dp'),) * 10,
                         check_vma=False)
```

time: 624 us -> 282 us (0.45)
  Pallas kernels: 0 us -> 252 us
  matrix products: 221 us -> 0 us
  blocking collectives: 194 us -> 0 us
  other arithmetic: 75.7 us -> 0 us
  starting transfers between devices: 40.3 us -> 0 us
  waiting for transfers between devices: 29.9 us -> 0 us
  between operations: 15.9 us -> 0.78 us
  local copies, waits for them, and re-layouts: 42.6 us -> 27.9 us
    pallas_call x0 -> x6, Pallas kernels: none -> 252 us  [the longest x4 247 us: call(): pl.pallas_call(kernel, grid=(steps,), in_specs=[spec(a.shape, first) for...]
    psum x4 -> x0, blocking collectives: 194 us -> none  [the longest x2 95.3 us: block_forward(): lax.psum(jnp.sum(g_act * g_act, axis=(1, 2)), ('sh', 'sw'))]
    dot_general x16 -> x0, matrix products: 117 us -> none  [the longest x2 35.5 us: block_backward(): jnp.einsum('bhwc,kc->bhwk', d_out, fc2_w, preferred_element_type=jnp.floa...]
    conv_general_dilated x6 -> x0, matrix products: 104 us -> none  [the longest x4 68 us: depthwise(): lax.conv_general_dilated(padded, kernel[:, :, None, :], (1, 1), 'VALID',...]
    reduce_sum x10 -> x0, other arithmetic: 40.6 us -> none  [the longest x2 24.3 us: block_backward(): grad_fc1_b = jnp.sum(d_hidden, axis=(0, 1, 2), dtype=jnp.float32)]
    ppermute x16 -> x0, starting transfers between devices: 40.3 us -> none  [shift_from(): return lax.ppermute(strip, axis_name, perm_pairs)]
    ppermute x16 -> x0, waiting for transfers between devices: 29.8 us -> none  [shift_from(): return lax.ppermute(strip, axis_name, perm_pairs)]
    dot_general x2 -> x0, local copies, waits for them, and re-layouts: 17.6 us -> none  [block_backward(): grad_fc2_w = jnp.einsum('b,bkc->kc', mask_k, per_image)]
  transfers between devices with their start and end apart: 17 -> 0, of which waited for: 7 -> 0; matrix products, arithmetic and copies ran while one was open for 16% -> 0% of each run, Pallas kernels for 0% -> 0%
where the time goes in v2:
time: 282 us; the launch traced here: 281 us
  Pallas kernels  252 us (89%)
  local copies, waits for them, and re-layouts  27.9 us (10%)
    pallas_call x4, Pallas kernels, call(): pl.pallas_call(kernel, grid=(steps,), in_specs=[spec(a.shape, first) for...  247 us
    unnamed x19, local copies, waits for them, and re-layouts  17.8 us

profile of v2, /device:TPU:97, one launch (start us, length us, event | category | flops | bytes accessed | tf_op | source)
XLA Modules:
  0.0 281.2 jit_solution(12745918300187304223)
XLA Ops:
  0.6 1.4 copy.36.mask_i
  2.0 1.3 copy.34.conv_w
  3.3 1.7 copy.35.fc2_w
  5.1 2.0 copy.32
  7.1 1.6 reshape.48
  8.7 0.0 copy-start
  8.7 0.7 copy.47
  9.3 1.2 pad.7.clone
  10.6 0.0 copy-done
  10.6 0.6 copy.37
  11.1 1.6 reshape.50
  12.7 0.7 copy.48
  13.4 1.2 pad.8.clone
  14.6 3.3 %prep.1 = (f32[4,56,256]{2,1,0:T(8,128)}, f32[2,4,256]{2,1,0:T(4,128)}, f32[2,2,1024]{2,1,0:T(2,128)}, bf16[2,256,1024]{2,1,0:T(8,128)(2,1)}, bf16[2,1024,256]{2...) custom-call(bf16[2,7,7,80]{3,2,1,0:T(8,128)(2,1)} %copy.34.conv_w, f32[2,80]{1,0:T(2,128)} %conv_b.1, ...), custom_call_target="tpu_custom_call" | custom-call | tf_op jit(solution)/shard_map/prep/pallas_call | solution.py:771
  17.9 51.2 %first.1 = (f32[2304,256]{1,0:T(8,128)}, f32[2304,256]{1,0:T(8,128)}, bf16[2304,1024]{1,0:T(8,128)(2,1)}, f32[2304,1024]{1,0:T(8,128)}, bf16[30,144,256]{2,1,0:T...) custom-call(bf16[2304,256]{1,0:T(8,128)(2,1)} %bitcast.16, f32[4,56,256]{2,1,0:T(8,128)} %get-tuple-element.56.taps, ...), custom_call_target="tpu_custom_call" | custom-call | tf_op jit(solution)/shard_map/first/pallas_call | solution.py:751
  69.1 65.1 %second.1 = (f32[2304,256]{1,0:T(8,128)}, f32[2304,256]{1,0:T(8,128)}, bf16[2304,1024]{1,0:T(8,128)(2,1)}, f32[2304,1024]{1,0:T(8,128)}, bf16[2304,1024]{1,0:T(8...) custom-call(bf16[2304,1024]{1,0:T(8,128)(2,1)} %get-tuple-element.60, ...), custom_call_target="tpu_custom_call" | custom-call | tf_op jit(solution)/shard_map/second/pallas_call | solution.py:751
  134.3 68.1 %third.1 = (bf16[2304,256]{1,0:T(8,128)(2,1)}, bf16[2304,256]{1,0:T(8,128)(2,1)}, bf16[2304,1024]{1,0:T(8,128)(2,1)}, f32[256,384]{1,0:T(8,128)}, f32[24,1024]{1...) custom-call(bf16[2304,1024]{1,0:T(8,128)(2,1)} %get-tuple-element.65.h2, f32[2304,1024]{1,0:T(8,128)} %get-tuple-element.66.phi2, ...), custom_call_target="tpu_custom_call" | custom-call | tf_op jit(solution)/shard_map/third/pallas_call | solution.py:751
  202.4 0.0 copy-start.1
  202.4 62.6 %fourth.1 = (bf16[2304,256]{1,0:T(8,128)(2,1)}, f32[256,384]{1,0:T(8,128)}, f32[256,384]{1,0:T(8,128)}) custom-call(bf16[2304,1024]{1,0:T(8,128)(2,1)} %get-tuple-element.60.h1, f32[2304,1024]{1,0:T(8,128)} %get-tuple-element.61.phi1, bf16[2304,1024]{1,0:T(8,128)(2,1)} %get-tuple-element.77.dr1, f32[24,1024]{1,0:T(8,128)} %get-tuple-element.62.coef1, ...), custom_call_target="tpu_custom_call" | custom-call | tf_op jit(solution)/shard_map/fourth/pallas_call | solution.py:751
  265.1 0.0 copy-start.2
  265.1 0.0 copy-done.1
  265.1 0.6 copy.52
  265.7 0.6 copy-done.2
  266.3 1.6 copy.51
  267.9 2.1 final.1
  270.0 1.5 copy.43
  271.5 1.8 copy.44
  273.3 3.2 %reshape.55 = bf16[24,24,12,80]{3,2,1,0:T(8,128)(2,1)S(1)} reshape(bf16[24,24,4,240]{3,2,1,0:T(4,128)(2,1)} %bitcast.19) | data formatting | bytes 2211840 | tf_op jit(solution)/shard_map/reshape | solution.py:727
  276.5 1.7 copy.42
  278.1 1.3 reshape.53
  279.5 1.7 copy.41
Async XLA Ops:
  8.7 1.9 copy-start
  202.4 62.7 %copy-start.1 = (bf16[2304,256]{1,0:T(8,128)(2,1)S(1)}, bf16[2304,256]{1,0:T(8,128)(2,1)}, u32[]{:S(2)}) copy-start(bf16[2304,256]{1,0:T(8,128)(2,1)} %get-tuple-element.76) | copy-start | bytes 3538948
  265.1 1.3 copy-start.2

commit v3 on v2

v3 whole, which is shorter than its diff:
```python
import functools

import jax
import jax.numpy as jnp
import numpy as np
from jax import lax
from jax.experimental import pallas as pl
from jax.experimental.pallas import tpu as pltpu
from jax.sharding import PartitionSpec as P

EPSILON = 1e-6
RADIUS = 3
TAPS = 2 * RADIUS + 1
MESH = pl.DeviceIdType.MESH
F32 = jnp.float32
BF16 = jnp.bfloat16
KEEP = 4.0 / 3.0
VMEM_LIMIT = 60 * 1024 * 1024
FULL = pl.BlockSpec(memory_space=pltpu.VMEM)
WHOLE = None
CONV_B, NORM_G, NORM_B, FC2_B = range(4)
FC1_B, BETA = range(2)
ONE, TWO = range(2)


def round_up(value, unit):
    return (value + unit - 1) // unit * unit


class Dims:
    def lanes(self, g):
        return slice(g * self.cp, (g + 1) * self.cp)

    def __init__(self, act_shape, hidden):
        self.b, self.h, self.w, self.c = act_shape
        self.hid = hidden
        self.nw = self.w // RADIUS
        self.cp = round_up(RADIUS * self.c, 128)
        self.hp = round_up(RADIUS * hidden, 128)
        self.pairs = ((1, 2), (0, self.nw - 1))
        self.rw = 2 * self.b
        self.chunk = 2 * self.rw
        self.th = self.h // RADIUS
        self.half = RADIUS
        self.tiles = 2 * self.half
        self.m = self.th * self.rw
        self.rows = self.h * self.nw * self.b
        self.block = self.h * self.rw
        self.tall = (self.h + 2 * RADIUS) * self.rw
        self.inner = slice(self.b, self.b + self.nw * self.b)
        self.cs = [slice(q * self.c, (q + 1) * self.c) for q in range(RADIUS)]
        self.hs = [slice(q * hidden, (q + 1) * hidden) for q in range(RADIUS)]


def loop(count, body, init=0):
    return lax.fori_loop(0, count, body, init)


def dot(lhs, rhs):
    return jnp.dot(lhs, rhs, preferred_element_type=F32)


def dot_t(lhs, rhs):
    return lax.dot_general(lhs, rhs, (((0,), (0,)), ((), ())), preferred_element_type=F32)


def dot_split(values, rhs):
    hi = values.astype(BF16)
    rest = values - hi.astype(F32)
    mid = rest.astype(BF16)
    low = (rest - mid.astype(F32)).astype(BF16)
    return dot(hi, rhs) + dot(mid, rhs) + dot(low, rhs)


def build_wide(dm, src_ref, wide, pair):
    def body(row, carry):
        rows = pl.ds(pl.multiple_of(pair * dm.tall + row * dm.rw, 16), dm.rw)
        for g in range(RADIUS):
            parts = [src_ref[row, (wg + g) * dm.b:(wg + g + 1) * dm.b] for wg in dm.pairs[pair]]
            wide[rows, dm.lanes(g)] = jnp.concatenate(parts, axis=0)
        return carry

    loop(dm.h + 2 * RADIUS, body)


def each_part(dm, tile, col0, body):
    row0 = lax.rem(tile, dm.half) * dm.th
    for pair, groups in enumerate(dm.pairs):
        @pl.when(tile // dm.half == pair)
        def _():
            for r in range(dm.th):
                for j, wg in enumerate(groups):
                    at, col = r * dm.rw + j * dm.b, col0 + wg * dm.b
                    body(slice(at, at + dm.b), row0 + r, slice(col, col + dm.b))


def load_tile(dm, ref, tile_ref, tile, col0, row_off):
    def body(part, row, cols):
        tile_ref[part] = ref[row + row_off, cols]

    each_part(dm, tile, col0, body)


def store_tile(dm, ref, values, tile, col0, row_off):
    def body(part, row, cols):
        ref[row + row_off, cols] = values[part]

    each_part(dm, tile, col0, body)


def build_toeplitz(dm, taps_ref, rel_ref, toep):
    def body(i, carry):
        for g in range(RADIUS):
            acc = jnp.zeros((dm.cp, dm.cp), F32)
            for dj in range(-2, 3):
                j = 3 * g + dj
                if 0 <= j < TAPS:
                    acc = jnp.where(rel_ref[...] == dj, taps_ref[pl.ds(i * 8 + j, 1), :], acc)
            toep[pl.ds(pl.multiple_of((i * 3 + g) * dm.cp, 16), dm.cp), :] = acc.astype(BF16)
        return carry

    loop(TAPS, body)


def conv_tile(dm, wide, toep, tile):
    base = (tile // dm.half) * dm.tall + lax.rem(tile, dm.half) * dm.m
    acc = None
    for i in range(TAPS):
        rows = pl.ds(pl.multiple_of(base + i * dm.rw, 16), dm.m)
        part = dot(wide[rows, :], toep[i * 3 * dm.cp:(i + 1) * 3 * dm.cp, :])
        acc = part if acc is None else acc + part
    return acc


def lane_loop(dm, body):
    def outer(r, carry):
        def inner(lane, c2):
            body(pl.ds(pl.multiple_of(r * dm.chunk, 16), dm.chunk), pl.ds(pl.multiple_of(lane * 128, 128), 128))
            return c2
        return loop(dm.hp // 128, inner, carry)
    loop(dm.m // dm.chunk, outer)


def line(ref, k, row, lanes=slice(None)):
    return ref[k, row:row + 1, lanes]


def image_lines(ref, lanes):
    return ref[:, lanes][None]


def per_image(dm, values):
    return values.reshape(-1, dm.b, values.shape[-1])


def phi_of(hv):
    return 0.5 + 0.5 * lax.erf(hv * np.float32(0.7071067811865476))


def gelu_chunk(dm, h_ref, phi_ref, rows, lanes):
    hv = h_ref[rows, lanes].astype(F32)
    phi = phi_of(hv)
    phi_ref[rows, lanes] = phi
    return hv * phi


def forward_tile(dm, k, tile, wide, toep, cvec, hvec, ones, w1, normed_o, inv_o, h_o):
    d = (conv_tile(dm, wide, toep, tile) + line(cvec, k, CONV_B)).astype(BF16)
    mean = dot(d, ones[...]) * np.float32(1.0 / dm.c)
    centered = d.astype(F32) - mean
    var = dot_split(centered * centered, ones[...]) * np.float32(1.0 / dm.c)
    inv = lax.rsqrt(var + EPSILON)
    normed = centered * inv
    normed_o[...] = normed
    inv_o[...] = inv
    n = (normed * line(cvec, k, NORM_G) + line(cvec, k, NORM_B)).astype(BF16)
    h_o[...] = (dot(n, w1[k]) + line(hvec, k, FC1_B)).astype(BF16)


def dot_bt(lhs, rhs):
    return lax.dot_general(lhs, rhs, (((1,), (1,)), ((), ())), preferred_element_type=F32)


def cross_chunk(dm, k, raw, mask, g, dr_o, cross, sdr, rows, lanes):
    dr = (per_image(dm, raw[rows, lanes]) * mask[k, :, :128][None]).astype(BF16)
    dr_o[rows, lanes] = dr.reshape(dm.chunk, 128)
    dr32 = dr.astype(F32)
    cross[:, lanes] += jnp.sum(dr32 * per_image(dm, g), axis=0)
    sdr[:, lanes] += jnp.sum(dr32, axis=0)


def position():
    sh = lax.axis_index('sh')
    return sh // 2, sh % 2, lax.axis_index('sw')


def peers_of(grid):
    chip, core, sw = position()
    n_chip, n_sw = grid[0] // 2, grid[1]
    pair = {'sh': chip * 2 + 1 - core}
    row = [{'sh': lax.rem(chip + j, n_chip) * 2 + core} for j in range(1, n_chip)]
    col = [{'sw': lax.rem(sw + j, n_sw)} for j in range(1, n_sw)]
    return pair, row, col


DIRECTIONS = [(0, 1), (0, -1), (1, 0), (-1, 0), (1, 1), (1, -1), (-1, 1), (-1, -1)]


def greet(grid, halo, reduce):
    devices = []
    if halo:
        sh, sw = lax.axis_index('sh'), lax.axis_index('sw')
        for dh, dw in DIRECTIONS:
            devices.append({'sh': lax.rem(sh + dh + grid[0], grid[0]), 'sw': lax.rem(sw + dw + grid[1], grid[1])})
    if reduce:
        pair, row, col = peers_of(grid)
        devices += [pair] + row + col
    barrier = pltpu.get_barrier_semaphore()
    for device in devices:
        pl.semaphore_signal(barrier, inc=1, device_id=device, device_id_type=MESH)
    pl.semaphore_wait(barrier, len(devices))


def clear_halo(dm, xp):
    b, r = dm.b, RADIUS
    edge = (dm.nw + 1) * b
    xp[:r] = jnp.zeros((r,) + xp.shape[1:], BF16)
    xp[dm.h + r:] = jnp.zeros((r,) + xp.shape[1:], BF16)
    xp[r:dm.h + r, :b] = jnp.zeros((dm.h, b, dm.cp), BF16)
    xp[r:dm.h + r, edge:] = jnp.zeros((dm.h, b, dm.cp), BF16)


def halo_copies(dm, grid, xp, send_sem, recv_sem):
    sh, sw = lax.axis_index('sh'), lax.axis_index('sw')
    r, b = RADIUS, dm.b
    rows = {1: (dm.h, r, 0), -1: (r, r, dm.h + r), 0: (r, dm.h, r)}
    cols = {1: (dm.nw * b, b, 0), -1: (b, b, (dm.nw + 1) * b), 0: (b, dm.nw * b, b)}

    def inside(a, c):
        return (a >= 0) & (a < grid[0]) & (c >= 0) & (c < grid[1])

    found = []
    for d, (dh, dw) in enumerate(DIRECTIONS):
        r0, rn, rt = rows[dh]
        c0, cn, ct = cols[dw]
        target = {'sh': lax.rem(sh + dh + grid[0], grid[0]), 'sw': lax.rem(sw + dw + grid[1], grid[1])}
        copy = pltpu.make_async_remote_copy(
            src_ref=xp.at[pl.ds(r0, rn), pl.ds(c0, cn)], dst_ref=xp.at[pl.ds(rt, rn), pl.ds(ct, cn)],
            send_sem=send_sem.at[d], recv_sem=recv_sem.at[d], device_id=target, device_id_type=MESH)
        found.append((copy, inside(sh + dh, sw + dw), inside(sh - dh, sw - dw)))
    return found[:2] + found[4:], found[2:4]


def halo_start(copies):
    for copy, sends, _ in copies:
        @pl.when(sends)
        def _():
            copy.start()


def halo_wait(copies):
    for copy, sends, receives in copies:
        @pl.when(sends)
        def _():
            copy.wait_send()

        @pl.when(receives)
        def _():
            copy.wait_recv()


def exchange(slots, mine, devices, send_sem, recv_sem):
    copies = []
    for j, device in enumerate(devices):
        copy = pltpu.make_async_remote_copy(src_ref=slots.at[mine], dst_ref=slots.at[mine], send_sem=send_sem.at[j],
                                            recv_sem=recv_sem.at[j], device_id=device, device_id_type=MESH)
        copies.append(copy)
    return copies


def go(copies):
    for copy in copies:
        copy.start()


def finish(copies):
    for copy in copies:
        copy.wait()


def fold(values, parts):
    return sum(values[:, part] for part in parts)


def sum_slots(slots):
    total = slots[0]
    for j in range(1, slots.shape[0]):
        total = total + slots[j]
    return total


def gather_scratch(grid, block):
    n_chip, n_sw = grid[0] // 2, grid[1]
    dma = pltpu.SemaphoreType.DMA
    return [pltpu.VMEM((n,) + block, F32) for n in (2, n_chip, n_sw)] + [dma((max(n - 1, 1),)) for n in (2, 2, n_chip, n_chip, n_sw, n_sw)]


N_GATHER = 9


def gather_stages(grid, scratch):
    slots, sems = scratch[:3], scratch[3:]
    mine = [position()[1], position()[0], position()[2]]
    pair, row, col = peers_of(grid)
    copies = [exchange(slots[j], mine[j], devices, sems[2 * j], sems[2 * j + 1]) for j, devices in enumerate(([pair], row, col))]

    def stage(j):
        def run():
            if j > 0:
                finish(copies[j - 1])
            if j in (1, 2):
                slots[j][mine[j]] = sum_slots(slots[j - 1])
            if j < 3:
                go(copies[j])
        return run

    return [stage(j) for j in range(4)]


def grn_begin(dm, scratch, sums):
    core = position()[1]
    for j, ref in enumerate(sums):
        scratch[0][core, j] = fold(ref, dm.hs)


def grn_total(dm, grid, sums, scratch):
    grn_begin(dm, scratch, sums)
    for stage in gather_stages(grid, scratch):
        stage()
    return sum_slots(scratch[2])


def spread(dm, ref, values):
    ref[...] = jnp.zeros_like(ref)
    for part in dm.hs:
        ref[:, part] = values


def grn_cross(dm, norm, gamma, cross, dsq_o, ggam_o):
    mean = jnp.mean(norm, axis=-1, keepdims=True) + EPSILON
    d_scale = gamma * cross
    d_norm = d_scale / mean - jnp.sum(d_scale * norm, axis=-1, keepdims=True) / (mean * mean * dm.hid)
    spread(dm, dsq_o, d_norm / norm)
    ggam_o[...] = jnp.sum(cross * (norm / mean), axis=0, keepdims=True)


def grn_coef(dm, norm, gamma, coef_o):
    mean = jnp.mean(norm, axis=-1, keepdims=True) + EPSILON
    spread(dm, coef_o, gamma * (norm / mean) + 1.0)


def prep_kernel(dm, conv_w, conv_b, norm_g, norm_b, fc1_w, fc1_b, beta, fc2_t, fc2_b, mask_i, ones, place, perm, x, dout,
                taps_o, cvec_o, hvec_o, w1_o, w2t_o, gmat_o, mask_o, x_o, d_o):
    for ref in (taps_o, cvec_o, hvec_o, w1_o, w2t_o):
        ref[...] = jnp.zeros_like(ref)
    square = (dm.b, dm.b)
    diagonal = lax.broadcasted_iota(jnp.int32, square, 0) == lax.broadcasted_iota(jnp.int32, square, 1)
    for k in range(2):
        for cs, hs in zip(dm.cs, dm.hs):
            for j, ref in enumerate((conv_b, norm_g, norm_b, fc2_b)):
                cvec_o[k, j:j + 1, cs] = ref[k:k + 1, :]
            for j, ref in enumerate((fc1_b, beta)):
                hvec_o[k, j:j + 1, hs] = ref[k:k + 1, :]
            w1_o[k, cs, hs] = fc1_w[k]
            w2t_o[k, cs, hs] = fc2_t[k]
        column = jnp.sum(jnp.where(diagonal, mask_i[k:k + 1, :], 0.0), axis=1, keepdims=True)
        mask_o[k] = jnp.broadcast_to(column, (dm.b, dm.cp))
    for i in range(TAPS):
        for j in range(TAPS):
            both = conv_w[i, j].astype(F32)
            for k in range(2):
                for cs in dm.cs:
                    taps_o[k, pl.ds(i * 8 + j, 1), cs] = both[k:k + 1]
                    taps_o[2 + k, pl.ds((TAPS - 1 - i) * 8 + TAPS - 1 - j, 1), cs] = both[k:k + 1]
    for k in range(2):
        values = ones[...].astype(F32) * line(cvec_o, k, NORM_G)
        for j in range(3):
            part = values.astype(BF16)
            gmat_o[k, j] = part
            values = values - part.astype(F32)
    moves = move_rows(perm)
    for src, out in ((x, x_o), (dout, d_o)):
        for wg in range(dm.nw):
            joined = sum(dot(src[:, RADIUS * wg + q].reshape(-1, dm.c), place[q]) for q in range(RADIUS)).astype(BF16)
            moved = dot(moves, joined).astype(BF16)
            out[:, wg * dm.b:(wg + 1) * dm.b] = moved.reshape(dm.h, dm.b, dm.cp)


def first_kernel(dm, grid, x, taps, rel, cvec, hvec, ones, w1, gamma,
                 normed_o, inv_o, h_o, phi_o, xp_o, norm_o, coef_o, wide, toep, ss, xp, keep_sem, send, recv, *grn):
    step = pl.program_id(0)

    @pl.when(step == 0)
    def _():
        clear_halo(dm, xp)
        for row in range(dm.h):
            xp[row + RADIUS, dm.inner] = x[row]
        greet(grid, True, True)
        sides, ends = halo_copies(dm, grid, xp, send, recv)
        halo_start(ends)
        halo_start(sides)
        build_toeplitz(dm, taps.at[0], rel, toep)
        ss[...] = jnp.zeros_like(ss)
        halo_wait(ends)
        build_wide(dm, xp, wide, ONE)

    @pl.when(step == dm.half)
    def _():
        halo_wait(halo_copies(dm, grid, xp, send, recv)[0])
        pltpu.make_async_copy(xp, xp_o, keep_sem).start()
        build_wide(dm, xp, wide, TWO)

    forward_tile(dm, ONE, step, wide, toep, cvec, hvec, ones, w1, normed_o, inv_o, h_o)

    def body(rows, lanes):
        g = gelu_chunk(dm, h_o, phi_o, rows, lanes)
        ss[:, lanes] += jnp.sum(per_image(dm, g * g), axis=0)

    lane_loop(dm, body)

    @pl.when(step == pl.num_programs(0) - 1)
    def _():
        pltpu.make_async_copy(xp, xp_o, keep_sem).wait()
        norm = jnp.sqrt(grn_total(dm, grid, [ss], grn)[0])
        norm_o[...] = norm
        grn_coef(dm, norm, gamma[pl.ds(ONE, 1), :], coef_o)


def lead_tile(dm, step):
    return lax.rem(jnp.minimum(step, dm.tiles - 1) + dm.half, dm.tiles)


def halo_schedule(dm, grid, step, xp, wide, send, recv, between, after):
    @pl.when(step == dm.half)
    def _():
        halo_start(halo_copies(dm, grid, xp, send, recv)[0])

    @pl.when(step == dm.tiles)
    def _():
        ends = halo_copies(dm, grid, xp, send, recv)[1]
        halo_start(ends)
        between()
        halo_wait(ends)
        build_wide(dm, xp, wide, ONE)

    @pl.when(step == dm.tiles + dm.half)
    def _():
        halo_wait(halo_copies(dm, grid, xp, send, recv)[0])
        after()
        build_wide(dm, xp, wide, TWO)


def second_kernel(dm, grid, h1, phi1, xp1, coef1, taps, rel, cvec, hvec, ones, w1, w2t, gamma, mask, dout,
                  normed_o, inv_o, h_o, phi_o, dr_o, xp_o, sdr_o, coef_o, dsq_o, ggam_o,
                  wide, toep, resp, raw, ss, cross, tile_s, xp, keep_sem, send, recv, *grn):
    step = pl.program_id(0)
    keep = pltpu.make_async_copy(xp, xp_o, keep_sem)

    @pl.when(step == 0)
    def _():
        clear_halo(dm, xp)
        greet(grid, True, True)
        for ref in (ss, cross, sdr_o):
            ref[...] = jnp.zeros_like(ref)

    halo_schedule(dm, grid, step, xp, wide, send, recv, lambda: build_toeplitz(dm, taps.at[1], rel, toep), keep.start)

    @pl.when(step < dm.tiles)
    def _():
        tile = lead_tile(dm, step)

        def body(rows, lanes):
            g = h1[rows, lanes].astype(F32) * phi1[rows, lanes]
            r = per_image(dm, g) * image_lines(coef1, lanes) + line(hvec, ONE, BETA, lanes)
            resp[rows, lanes] = r.reshape(dm.chunk, 128).astype(BF16)

        lane_loop(dm, body)
        load_tile(dm, xp1, tile_s, tile, dm.b, RADIUS)
        o = (dot_bt(resp[...], w2t[ONE]) + line(cvec, ONE, FC2_B)).reshape(-1, dm.b, dm.cp)
        y = (tile_s[...].astype(F32) + (o * mask[ONE][None]).reshape(-1, dm.cp)).astype(BF16)
        store_tile(dm, xp, y, tile, dm.b, RADIUS)

    @pl.when(step >= dm.tiles)
    def _():
        tile = step - dm.tiles
        forward_tile(dm, TWO, tile, wide, toep, cvec, hvec, ones, w1, normed_o, inv_o, h_o)
        load_tile(dm, dout, tile_s, tile, 0, 0)
        raw[...] = dot(tile_s[...], w2t[TWO])

        def body(rows, lanes):
            g = gelu_chunk(dm, h_o, phi_o, rows, lanes)
            ss[:, lanes] += jnp.sum(per_image(dm, g * g), axis=0)
            cross_chunk(dm, TWO, raw, mask, g, dr_o, cross, sdr_o, rows, lanes)

        lane_loop(dm, body)

    @pl.when(step == pl.num_programs(0) - 1)
    def _():
        keep.wait()
        total = grn_total(dm, grid, [ss, cross], grn)
        norm = jnp.sqrt(total[0])
        grn_coef(dm, norm, gamma[pl.ds(TWO, 1), :], coef_o)
        grn_cross(dm, norm, gamma[pl.ds(TWO, 1), :], total[1], dsq_o, ggam_o)


def backward_tile(dm, k, h_i, phi_i, dr_i, coef, dsq, dout, normed_i, inv_i, cvec, hvec, ones, gmat, w1, w2t, mask,
                  resp, dh, gfc1, gfc2, sdh, sums, x_rows):
    def body(rows, lanes):
        hv = h_i[rows, lanes].astype(F32)
        phi = phi_i[rows, lanes]
        g = per_image(dm, hv * phi)
        a = image_lines(coef, lanes)
        resp[rows, lanes] = (g * a + line(hvec, k, BETA, lanes)).reshape(dm.chunk, 128).astype(BF16)
        slope = phi + hv * (np.float32(0.3989422804014327) * jnp.exp(-0.5 * hv * hv))
        dg = per_image(dm, dr_i[rows, lanes].astype(F32)) * a + g * image_lines(dsq, lanes)
        dhv = (dg.reshape(dm.chunk, 128) * slope).astype(BF16)
        dh[rows, lanes] = dhv
        sdh[:, lanes] += jnp.sum(per_image(dm, dhv.astype(F32)), axis=0)

    lane_loop(dm, body)
    dsel32 = jnp.where((mask[k] != 0.0)[None], dout[...].astype(F32).reshape(-1, dm.b, dm.cp), 0.0)
    sums[FC2_B] += jnp.sum(dsel32, axis=0)
    gfc2[...] += dot_t(dsel32.reshape(-1, dm.cp).astype(BF16), resp[...])
    y = None
    if x_rows is not None:
        o = (dot_bt(resp[...], w2t[k]) + line(cvec, k, FC2_B)).reshape(-1, dm.b, dm.cp)
        y = (x_rows[...].astype(F32) + (o * mask[k][None]).reshape(-1, dm.cp)).astype(BF16)
    normed = normed_i[...]
    norm_g = line(cvec, k, NORM_G)
    n = (normed * norm_g + line(cvec, k, NORM_B)).astype(BF16)
    gfc1[...] += dot_t(n, dh[...])
    dn16 = dot_bt(dh[...], w1[k]).astype(BF16)
    dn = dn16.astype(F32)
    scale = np.float32(1.0 / dm.c)
    mean1 = (dot_bt(dn16, gmat[k, 0]) + dot_bt(dn16, gmat[k, 1]) + dot_bt(dn16, gmat[k, 2])) * scale
    dnormed = dn * norm_g
    mean2 = dot_split(dnormed * normed, ones[...]) * scale
    dconv = (inv_i[...] * (dnormed - mean1 - normed * mean2)).astype(BF16)

    for row, values in ((CONV_B, dconv.astype(F32)), (NORM_G, dn * normed), (NORM_B, dn)):
        sums[row] += jnp.sum(values.reshape(-1, dm.b, dm.cp), axis=0)
    return dconv, y


def wgrad(dm, wide, dcol, rel, out, stages):
    keep = rel[...] > -50

    def body(i, carry):
        res = None
        for pair in range(2):
            rows = pl.ds(pl.multiple_of(pair * dm.tall + i * dm.rw, 16), dm.block)
            part = dot(dcol[:, pair * dm.block:(pair + 1) * dm.block], wide[rows, :])
            res = part if res is None else res + part
        for g in range(RADIUS):
            part = jnp.where(keep, res[:, dm.lanes(g)], 0.0)
            for q in range(RADIUS):
                out[q, pl.ds(i, 1), dm.lanes(g)] = jnp.sum(part[dm.cs[q]], axis=0, keepdims=True)
        for tap, stage in stages.items():
            pl.when(i == tap)(stage)
        return carry

    loop(TAPS, body)


def vector_rows(dm):
    return 2 * dm.c


def conv_rows(dm):
    return round_up(2 * dm.c + 6, 8)


def pack_conv(dm, out, base, corr):
    for j in range(TAPS):
        total = None
        for q in range(RADIUS):
            lane = ((q + j) // RADIUS) * dm.cp + ((q + j) % RADIUS) * dm.c
            part = corr[q, :, lane:lane + dm.c]
            total = part if total is None else total + part
        out[base + 8 * j:base + 8 * j + 8, :dm.c] = total


def pack_grads(dm, pack, gfc1, gfc2, sdh, sdr, sums):
    for base, ref in ((0, gfc1), (dm.c, gfc2)):
        pack[base:base + dm.c, :dm.hid] = sum(ref[cs, hs] for cs, hs in zip(dm.cs, dm.hs))
    base = vector_rows(dm)
    rows = [fold(jnp.sum(ref[...], axis=0, keepdims=True), dm.hs) for ref in (sdh, sdr)]
    rows += [fold(jnp.sum(sums[row], axis=0, keepdims=True), dm.cs) for row in range(4)]
    for j, row in enumerate(rows):
        pack[base + j:base + j + 1, :row.shape[1]] = row


def pack_shape(dm, grid, conv):
    rows = conv_rows(dm) + (8 * TAPS if conv else 0)
    return (round_up(rows, 8 * grid[0]), round_up(dm.hid, 128))


def conv_shape(dm):
    return (8 * TAPS, 128)


def sum_scratch(grid, shape):
    rows, lanes = shape
    n_chip, n_sw = grid[0] // 2, grid[1]
    dma = pltpu.SemaphoreType.DMA
    return ([pltpu.VMEM((rows // 2, lanes), F32)]
            + [pltpu.VMEM((n, rows // (2 * n_chip), lanes), F32) for n in (n_chip, n_chip, n_chip, n_sw)]
            + [dma((n,)) for n in (1, 1, n_chip - 1, n_chip - 1, n_sw - 1, n_sw - 1, n_chip - 1, n_chip - 1, 1, 1)])


N_SUM = 15


def sum_stages(grid, x, out, scratch):
    got1, half, got2, part, slots3, send1, recv1, send2, recv2, send3, recv3, send4, recv4, send5, recv5 = scratch
    chip, core, sw = position()
    n_chip = grid[0] // 2
    pair, row, col = peers_of(grid)
    rows = got1.shape[0]
    chunk = half.shape[1]

    def whole(ref, which):
        return ref.at[pl.ds(pl.multiple_of(which * rows, 8), rows)]

    def copies1():
        return [pltpu.make_async_remote_copy(src_ref=whole(x, 1 - core), dst_ref=got1, send_sem=send1.at[0], recv_sem=recv1.at[0],
                                             device_id=pair, device_id_type=MESH)]

    def copies2():
        made = []
        for j, device in enumerate(row):
            made.append(pltpu.make_async_remote_copy(
                src_ref=half.at[lax.rem(chip + j + 1, n_chip)], dst_ref=got2.at[chip], send_sem=send2.at[j],
                recv_sem=recv2.at[j], device_id=device, device_id_type=MESH))
        return made

    def copies5():
        return [pltpu.make_async_remote_copy(src_ref=whole(out, core), dst_ref=whole(out, core), send_sem=send5.at[0],
                                             recv_sem=recv5.at[0], device_id=pair, device_id_type=MESH)]

    def stage0():
        go(copies1())

    def stage1():
        finish(copies1())
        for j in range(n_chip):
            start = pl.multiple_of(core * rows + j * chunk, 8)
            half[j] = x[pl.ds(start, chunk)] + got1[j * chunk:(j + 1) * chunk]
        go(copies2())

    def stage2():
        got2[chip] = half[chip]
        finish(copies2())
        slots3[sw] = sum_slots(got2)
        go(exchange(slots3, sw, col, send3, recv3))

    def stage3():
        finish(exchange(slots3, sw, col, send3, recv3))
        part[chip] = sum_slots(slots3)
        go(exchange(part, chip, row, send4, recv4))

    def stage4():
        finish(exchange(part, chip, row, send4, recv4))
        for j in range(n_chip):
            out[pl.ds(pl.multiple_of(core * rows + j * chunk, 8), chunk)] = part[j]
        go(copies5())

    def stage5():
        finish(copies5())

    return [stage0, stage1, stage2, stage3, stage4, stage5]


def backward_phase(dm, step, k, dp, dcol, args, x_rows):
    tile = lead_tile(dm, step)
    dconv, y = backward_tile(dm, k, *args, x_rows)
    store_tile(dm, dp, dconv, tile, dm.b, RADIUS)
    dcol[:, pl.ds(pl.multiple_of(tile * dm.m, 128), dm.m)] = dconv.T
    return tile, y


def third_kernel(dm, grid, h2, phi2, dr2, coef2, dsq2, dout, normed, inv, xp2, h1, phi1, norm1, taps, rel, cvec, hvec, ones, gmat,
                 w1, w2t, gamma, mask, sdr2,
                 y_o, d1_o, dr1_o, pack, sdr_o, dsq_o, ggam_o,
                 wide, toep, dp, dcol, corr, resp, dh, tile_s, gfc1, gfc2, sdh, sums, raw, tile_x, cross, send, recv, *grn):
    step = pl.program_id(0)

    @pl.when(step == 0)
    def _():
        clear_halo(dm, dp)
        greet(grid, True, True)
        for ref in (cross, sdr_o, gfc1, gfc2, sdh, sums, corr, pack):
            ref[...] = jnp.zeros_like(ref)

    halo_schedule(dm, grid, step, dp, wide, send, recv, lambda: build_toeplitz(dm, taps.at[3], rel, toep), lambda: None)

    @pl.when(step < dm.tiles)
    def _():
        load_tile(dm, dout, tile_s, lead_tile(dm, step), 0, 0)
        load_tile(dm, xp2, tile_x, lead_tile(dm, step), dm.b, RADIUS)
        tile, y = backward_phase(dm, step, TWO, dp, dcol, (h2, phi2, dr2, coef2, dsq2, tile_s, normed, inv, cvec, hvec, ones, gmat,
                                                           w1, w2t, mask, resp, dh, gfc1, gfc2, sdh, sums), tile_x)
        store_tile(dm, y_o, y, tile, 0, 0)

    @pl.when(step >= dm.tiles)
    def _():
        tile = step - dm.tiles
        load_tile(dm, dout, tile_s, tile, 0, 0)
        din = (tile_s[...].astype(F32) + conv_tile(dm, wide, toep, tile)).astype(BF16)
        d1_o[...] = din
        raw[...] = dot(din, w2t[ONE])

        def body(rows, lanes):
            g = h1[rows, lanes].astype(F32) * phi1[rows, lanes]
            cross_chunk(dm, ONE, raw, mask, g, dr1_o, cross, sdr_o, rows, lanes)

        lane_loop(dm, body)

    @pl.when(step == pl.num_programs(0) - 1)
    def _():
        begin, row, col, end = gather_stages(grid, grn)
        grn_begin(dm, grn, [cross])
        begin()
        build_wide(dm, xp2, wide, ONE)
        build_wide(dm, xp2, wide, TWO)
        pack_grads(dm, pack, gfc1, gfc2, sdh, sdr2, sums)
        wgrad(dm, wide, dcol, rel, corr, {ONE: row, RADIUS: col})
        pack_conv(dm, pack, conv_rows(dm), corr)
        end()
        grn_cross(dm, norm1[...], gamma[pl.ds(ONE, 1), :], sum_slots(grn[2])[0], dsq_o, ggam_o)


def fourth_kernel(dm, grid, h1, phi1, dr1, coef1, dsq1, d1, normed, inv, xp1, taps, rel, cvec, hvec, ones, gmat,
                  w1, w2t, mask, sdr1, pack2_i,
                  d0_o, out1_o, out2_o, conv_o,
                  wide, toep, dp, dcol, corr, resp, dh, tile_s, gfc1, gfc2, sdh, sums, pack1, out1, pack2, out2, send, recv, *sem):
    step = pl.program_id(0)
    stages1 = sum_stages(grid, pack1, out1, sem[:N_SUM])
    stages2 = sum_stages(grid, pack2, out2, sem[N_SUM:2 * N_SUM])
    conv_sem = sem[2 * N_SUM:]
    conv_stages = gather_stages(grid, conv_sem)

    @pl.when(step == 0)
    def _():
        clear_halo(dm, dp)
        greet(grid, True, True)
        for ref in (gfc1, gfc2, sdh, sums, corr, pack1):
            ref[...] = jnp.zeros_like(ref)
        pack2[...] = pack2_i[...]

    begin1, *middle1, end1 = stages1
    conv_begin, conv_row, conv_col, conv_end = conv_stages
    a, b, c, d, e, f = stages2
    plan = [[a], [b], [], [c], [d], [e], [], [f, conv_row], [], [middle1.pop()], [conv_col]]
    for at, jobs in enumerate(plan):
        @pl.when(step == at)
        def _():
            for job in jobs:
                job()

    def between():
        pack_grads(dm, pack1, gfc1, gfc2, sdh, sdr1, sums)
        begin1()
        build_toeplitz(dm, taps.at[2], rel, toep)
        build_wide(dm, xp1, wide, ONE)
        build_wide(dm, xp1, wide, TWO)
        half, chip, column = middle1
        half()
        wgrad(dm, wide, dcol, rel, corr, {RADIUS: chip})
        core = position()[1]
        conv_sem[0][core] = jnp.zeros(conv_shape(dm), F32)
        pack_conv(dm, conv_sem[0].at[core], 0, corr)
        conv_begin()
        column()

    halo_schedule(dm, grid, step, dp, wide, send, recv, between, lambda: None)

    @pl.when(step < dm.tiles)
    def _():
        backward_phase(dm, step, ONE, dp, dcol, (h1, phi1, dr1, coef1, dsq1, d1, normed, inv, cvec, hvec, ones, gmat,
                                                 w1, w2t, mask, resp, dh, gfc1, gfc2, sdh, sums), None)

    @pl.when(step >= dm.tiles)
    def _():
        tile = step - dm.tiles
        din = (d1[...].astype(F32) + conv_tile(dm, wide, toep, tile)).astype(BF16)
        store_tile(dm, d0_o, din, tile, 0, 0)

    @pl.when(step == pl.num_programs(0) - 1)
    def _():
        end1()
        out1_o[...] = out1[...]
        out2_o[...] = out2[...]
        conv_end()
        conv_o[...] = sum_slots(conv_sem[2])


def final_kernel(dm, out1, out2, conv1, ggam1, ggam2, y, d, place, perm, yo, do, gcw, gcb, gng, gnb, gf1w, gf1b, ggam, gbeta, gf2w, gf2b):
    c, hid = dm.c, dm.hid
    ggam[...] = jnp.concatenate([ggam1[...], ggam2[...]], axis=0)
    for k, ref in enumerate((out1, out2)):
        gf1w[k] = ref[:c, :hid]
        gf2w[k] = ref[c:2 * c, :hid] * np.float32(KEEP)
        base = vector_rows(dm)
        for row, out in enumerate((gf1b, gbeta, gcb, gng, gnb, gf2b)):
            value = ref[base + row:base + row + 1, :out.shape[1]]
            out[k:k + 1, :] = value * np.float32(KEEP) if out is gf2b else value
    for k, (ref, base) in enumerate(((conv1, 0), (out2, conv_rows(dm)))):
        for j in range(TAPS):
            for i in range(TAPS):
                row = base + 8 * j + i
                gcw[i, j, k:k + 1, :] = ref[row:row + 1, :c]
    moves = move_rows(perm)
    for src, out in ((y, yo), (d, do)):
        for wg in range(dm.nw):
            rows = src[:, wg * dm.b:(wg + 1) * dm.b].reshape(-1, dm.cp)
            moved = dot(moves, rows).astype(BF16)
            for q in range(RADIUS):
                out[:, RADIUS * wg + q] = dot_bt(moved, place[q]).astype(BF16).reshape(dm.b, dm.h, dm.c)


def constants(dm):
    index = np.arange(dm.cp)
    col, chan = index // dm.c, index % dm.c
    live = (index[:, None] < RADIUS * dm.c) & (index[None, :] < RADIUS * dm.c)
    rel = np.where((chan[:, None] == chan[None, :]) & live, col[:, None] - col[None, :], -100).astype(np.int32)
    ones = ((col[:, None] == col[None, :]) & live).astype(np.float32)
    place = np.stack([np.eye(dm.c, dm.cp, q * dm.c) for q in range(RADIUS)])
    count = dm.h * dm.b
    order = np.arange(count, dtype=np.int32)
    moves = [order.reshape(shape).T.reshape(1, count) for shape in ((dm.h, dm.b), (dm.b, dm.h))]
    return [jnp.asarray(a) for a in [rel] + moves] + [jnp.asarray(a, BF16) for a in (ones, place)]


def move_rows(ref):
    count = ref.shape[1]
    rows = lax.broadcasted_iota(jnp.int32, (count, count), 0)
    return jnp.where(rows == ref[...], 1.0, 0.0).astype(BF16)


def call(dm, kernel, steps, ins, outs, scratch, name, cid):
    def spec(shape, mode):
        if mode is WHOLE:
            return FULL
        if mode == 'any':
            return pl.BlockSpec(memory_space=pl.ANY)
        maps = {'lead': lambda s: (lead_tile(dm, s), 0),
                'tail': lambda s: (jnp.maximum(s - dm.tiles, 0), 0),
                'both': lambda s: (jnp.where(s < dm.tiles, lead_tile(dm, s), s - dm.tiles), 0),
                'only': lambda s: (s, 0)}
        return pl.BlockSpec((dm.m, shape[1]), maps[mode])

    return pl.pallas_call(
        kernel, grid=(steps,), in_specs=[spec(a.shape, mode) for a, mode in ins],
        out_specs=[spec(shape, mode) for shape, _, mode in outs],
        out_shape=[jax.ShapeDtypeStruct(shape, dtype) for shape, dtype, _ in outs],
        scratch_shapes=scratch, name=name,
        compiler_params=pltpu.CompilerParams(dimension_semantics=('arbitrary',), vmem_limit_bytes=VMEM_LIMIT,
                                             collective_id=cid, has_side_effects=True))(*[a for a, _ in ins])


def solution(mesh):
    grid = (mesh.shape['sh'], mesh.shape['sw'])
    act_spec = P('dp', 'sh', 'sw', WHOLE)
    replicated = P()

    def local_step(act_in, drop_mask, grad_out, conv_w, conv_b, norm_g, norm_b, fc1_w, fc1_b, gamma, grn_beta, fc2_w, fc2_b):
        dm = Dims(act_in.shape, fc1_w.shape[-1])
        rel, perm, perm_back, ones, place = constants(dm)
        sds = jax.ShapeDtypeStruct
        c_shape, h_shape, s_shape, n_shape = (dm.rows, dm.cp), (dm.rows, dm.hp), (dm.b, dm.hp), (dm.b, dm.hid)
        x_shape = (dm.h, dm.nw * dm.b, dm.cp)
        act_t = (dm.b, dm.w, dm.h, dm.c)
        swap = (0, 2, 1, 3)
        big = pltpu.CompilerParams(vmem_limit_bytes=VMEM_LIMIT)
        taps, cvec, hvec, w1, w2t, gmat, mask, x1, d2 = pl.pallas_call(
            functools.partial(prep_kernel, dm),
            out_shape=[sds((4, TAPS * 8, dm.cp), F32), sds((2, 4, dm.cp), F32), sds((2, 2, dm.hp), F32), sds((2, dm.cp, dm.hp), BF16),
                       sds((2, dm.cp, dm.hp), BF16), sds((2, 3, dm.cp, dm.cp), BF16), sds((2, dm.b, dm.cp), F32),
                       sds(x_shape, BF16), sds(x_shape, BF16)],
            in_specs=[FULL] * 15, out_specs=[FULL] * 9, compiler_params=big, name='prep')(
                conv_w.transpose(1, 2, 0, 3), conv_b, norm_g, norm_b, fc1_w, fc1_b, grn_beta, fc2_w.transpose(0, 2, 1), fc2_b,
                drop_mask.T, ones, place, perm, act_in.transpose(swap), grad_out.transpose(swap))

        dma = pltpu.SemaphoreType.DMA
        V = pltpu.VMEM
        wide_s = V((2 * dm.tall, 3 * dm.cp), BF16)
        toep_s = V((TAPS * 3 * dm.cp, dm.cp), BF16)
        raw_s, hid_s, tile_s = V((dm.m, dm.hp), F32), V((dm.m, dm.hp), BF16), V((dm.m, dm.cp), BF16)
        img_s, acc_s = V(s_shape, F32), V((dm.cp, dm.hp), F32)
        xp_shape = (dm.h + 2 * RADIUS, (dm.nw + 2) * dm.b, dm.cp)
        xp_s = V(xp_shape, BF16)
        halo_s = [dma((8,)), dma((8,))]
        g_shape = (1, dm.hid)
        p1_shape, p2_shape = (pack_shape(dm, grid, conv) for conv in (False, True))

        def wholes(*arrays):
            return [(a, WHOLE) for a in arrays]

        def grn_s(count):
            return gather_scratch(grid, (count, dm.b, dm.hid))

        normed1, inv1, h1, phi1, xp1, norm1, coef1 = call(
            dm, functools.partial(first_kernel, dm, grid), dm.tiles, wholes(x1, taps, rel, cvec, hvec, ones, w1, gamma),
            [(c_shape, F32, 'only'), (c_shape, F32, 'only'), (h_shape, BF16, 'only'), (h_shape, F32, 'only'), (xp_shape, BF16, 'any'),
             (n_shape, F32, WHOLE), (s_shape, F32, WHOLE)],
            [wide_s, toep_s, img_s, xp_s, dma] + halo_s + grn_s(1), 'first', 0)

        normed2, inv2, h2, phi2, dr2, xp2, sdr2, coef2, dsq2, ggam2 = call(
            dm, functools.partial(second_kernel, dm, grid), 2 * dm.tiles,
            [(h1, 'lead'), (phi1, 'lead')] + wholes(xp1, coef1, taps, rel, cvec, hvec, ones, w1, w2t, gamma, mask, d2),
            [(c_shape, F32, 'tail'), (c_shape, F32, 'tail'), (h_shape, BF16, 'tail'), (h_shape, F32, 'tail'), (h_shape, BF16, 'tail'),
             (xp_shape, BF16, 'any')] + [(s_shape, F32, WHOLE)] * 3 + [(g_shape, F32, WHOLE)],
            [wide_s, toep_s, hid_s, raw_s, img_s, img_s, tile_s, xp_s, dma] + halo_s + grn_s(2), 'second', 1)

        bwd_s = [wide_s, toep_s, xp_s, V((dm.cp, dm.rows), BF16), V((3, 8, 3 * dm.cp), F32), hid_s, hid_s, tile_s,
                 acc_s, acc_s, img_s, V((4, dm.b, dm.cp), F32)]
        y2, d1, dr1, pack2, sdr1, dsq1, ggam1 = call(
            dm, functools.partial(third_kernel, dm, grid), 2 * dm.tiles,
            [(h2, 'lead'), (phi2, 'lead'), (dr2, 'lead')] + wholes(coef2, dsq2, d2) + [(normed2, 'lead'), (inv2, 'lead')] + wholes(xp2)
            + [(h1, 'tail'), (phi1, 'tail')] + wholes(norm1, taps, rel, cvec, hvec, ones, gmat, w1, w2t, gamma, mask, sdr2),
            [(x_shape, BF16, WHOLE), (c_shape, BF16, 'tail'), (h_shape, BF16, 'tail'), (p2_shape, F32, WHOLE), (s_shape, F32, WHOLE),
             (s_shape, F32, WHOLE), (g_shape, F32, WHOLE)],
            bwd_s + [raw_s, tile_s, img_s] + halo_s + grn_s(1), 'third', 2)

        d0, out1, out2, conv1 = call(
            dm, functools.partial(fourth_kernel, dm, grid), 2 * dm.tiles,
            [(h1, 'lead'), (phi1, 'lead'), (dr1, 'lead')] + wholes(coef1, dsq1) + [(d1, 'both'), (normed1, 'lead'), (inv1, 'lead')]
            + wholes(xp1, taps, rel, cvec, hvec, ones, gmat, w1, w2t, mask, sdr1, pack2),
            [(x_shape, BF16, WHOLE), (p1_shape, F32, WHOLE), (p2_shape, F32, WHOLE), (conv_shape(dm), F32, WHOLE)],
            bwd_s + [V(p1_shape, F32)] * 2 + [V(p2_shape, F32)] * 2 + halo_s + sum_scratch(grid, p1_shape) + sum_scratch(grid, p2_shape)
            + gather_scratch(grid, conv_shape(dm)), 'fourth', 3)

        conv_t, fc2_t = (TAPS, TAPS, 2, dm.c), (2, dm.c, dm.hid)
        y_t, d_t, gcw, gcb, gng, gnb, gf1w, gf1b, ggam, gbeta, gf2w, gf2b = pl.pallas_call(
            functools.partial(final_kernel, dm),
            out_shape=[sds(act_t, BF16)] * 2 + [sds(shape, F32) for shape in (
                conv_t, conv_b.shape, norm_g.shape, norm_b.shape, fc1_w.shape, fc1_b.shape, gamma.shape, grn_beta.shape, fc2_t, fc2_b.shape)],
            in_specs=[FULL] * 9, out_specs=[FULL] * 12, compiler_params=big, name='final')(
                out1, out2, conv1, ggam1, ggam2, y2, d0, place, perm_back)
        return (y_t.transpose(swap), d_t.transpose(swap), gcw.transpose(2, 0, 1, 3), gcb, gng, gnb, gf1w, gf1b, ggam, gbeta,
                gf2w.transpose(0, 2, 1), gf2b)

    return jax.shard_map(local_step, mesh=mesh,
                         in_specs=(act_spec, P('dp', WHOLE), act_spec) + (replicated,) * 10,
                         out_specs=(act_spec, act_spec) + (P('dp'),) * 10,
                         check_vma=False)
```

time: 282 us -> 244 us (0.87)
  local copies, waits for them, and re-layouts: 27.9 us -> 0 us
  Pallas kernels: 252 us -> 243 us
    unnamed x19 -> x0, local copies, waits for them, and re-layouts: 17.8 us -> none
    pallas_call x5, Pallas kernels: 249 us -> 234 us  [the longest x4 226 us: call(): pl.pallas_call(kernel, grid=(steps,), in_specs=[spec(a.shape, mode) for a...]
    reshape x4 -> x0, local copies, waits for them, and re-layouts: 7.63 us -> none  [the longest x2 4.5 us: from_rows(): return t.reshape(dm.b, dm.h, dm.w, dm.c)]
    pallas_call x1, Pallas kernels: 3.32 us -> 8.7 us  [local_step(): pl.pallas_call(functools.partial(prep_kernel, dm), out_shape=[sds((4, TAP...]
where the time goes in v3:
time: 244 us; the launch traced here: 243 us
  Pallas kernels  243 us (100%)
    pallas_call x4, Pallas kernels, call(): pl.pallas_call(kernel, grid=(steps,), in_specs=[spec(a.shape, mode) for a...  226 us
    pallas_call x1, Pallas kernels, local_step(): pl.pallas_call(functools.partial(prep_kernel, dm), out_shape=[sds((4, TAP...  8.7 us
    pallas_call x1, Pallas kernels, local_step(): pl.pallas_call(functools.partial(final_kernel, dm), out_shape=[sds(act_t,...  7.89 us

profile of v3, /device:TPU:97, one launch (start us, length us, event | category | flops | bytes accessed | tf_op | source)
XLA Modules:
  0.0 243.5 jit_solution(16735264670806106531)
XLA Ops:
  0.6 8.7 %prep.1 = (f32[4,56,256]{2,1,0:T(8,128)}, f32[2,4,256]{2,1,0:T(4,128)}, f32[2,2,1024]{2,1,0:T(2,128)}, bf16[2,256,1024]{2,1,0:T(8,128)(2,1)}, bf16[2,256,1024]{2...) custom-call(bf16[7,7,2,80]{3,2,1,0:T(2,128)(2,1)} %bitcast.12, ...), custom_call_target="tpu_custom_call" | custom-call | tf_op jit(solution)/shard_map/prep/pallas_call | solution.py:886
  9.3 44.9 %first.1 = (f32[2304,256]{1,0:T(8,128)}, f32[2304,256]{1,0:T(8,128)}, bf16[2304,1024]{1,0:T(8,128)(2,1)}, f32[2304,1024]{1,0:T(8,128)}, bf16[30,144,256]{2,1,0:T...) custom-call(bf16[24,96,256]{2,1,0:T(8,128)(2,1)} %get-tuple-element.61.x, f32[4,56,256]{2,1,0:T(8,128)} %get-tuple-element.62.taps, ...), custom_call_target="tpu_custom_call" | custom-call | tf_op jit(solution)/shard_map/first/pallas_call | solution.py:863
  54.2 61.4 %second.1 = (f32[2304,256]{1,0:T(8,128)}, f32[2304,256]{1,0:T(8,128)}, bf16[2304,1024]{1,0:T(8,128)(2,1)}, f32[2304,1024]{1,0:T(8,128)}, bf16[2304,1024]{1,0:T(8...) custom-call(bf16[2304,1024]{1,0:T(8,128)(2,1)} %get-tuple-element.66, ...), custom_call_target="tpu_custom_call" | custom-call | tf_op jit(solution)/shard_map/second/pallas_call | solution.py:863
  115.6 64.9 %third.1 = (bf16[24,96,256]{2,1,0:T(8,128)(2,1)}, bf16[2304,256]{1,0:T(8,128)(2,1)}, bf16[2304,1024]{1,0:T(8,128)(2,1)}, f32[256,384]{1,0:T(8,128)}, f32[24,1024...) custom-call(bf16[2304,1024]{1,0:T(8,128)(2,1)} %get-tuple-element.73.h2, f32[2304,1024]{1,0:T(8,128)} %get-tuple-element.74.phi2, ...), custom_call_target="tpu_custom_call" | custom-call | tf_op jit(solution)/shard_map/third/pallas_call | solution.py:863
  180.5 55.0 %fourth.1 = (bf16[24,96,256]{2,1,0:T(8,128)(2,1)}, f32[192,384]{1,0:T(8,128)}, f32[256,384]{1,0:T(8,128)}, f32[56,128]{1,0:T(8,128)}) custom-call(bf16[2304,1024]{1,0:T(8,128)(2,1)} %get-tuple-element.66.h1, f32[2304,1024]{1,0:T(8,128)} %get-tuple-element.67.phi1, bf16[2304,1024]{1,0:T(8,128)(2,1)} %get-tuple-element.84.dr1, ...), custom_call_target="tpu_custom_call" | custom-call | tf_op jit(solution)/shard_map/fourth/pallas_call | solution.py:863
  235.4 7.9 %final.1 = (bf16[24,12,24,80]{3,2,1,0:T(8,128)(2,1)}, bf16[24,12,24,80]{3,2,1,0:T(8,128)(2,1)}, f32[7,7,2,80]{3,2,1,0:T(2,128)}, f32[2,80]{1,0:T(2,128)}, f32[2,...) custom-call(f32[192,384]{1,0:T(8,128)} %get-tuple-element.91.out1, ...), custom_call_target="tpu_custom_call" | custom-call | tf_op jit(solution)/shard_map/final/pallas_call | solution.py:945

commit v4 on v3

--- a/solution.py
+++ b/solution.py
@@ -11,6 +11,7 @@
 EPSILON = 1e-6
 RADIUS = 3
 TAPS = 2 * RADIUS + 1
+CHUNKS = 1
 MESH = pl.DeviceIdType.MESH
 F32 = jnp.float32
 BF16 = jnp.bfloat16
@@ -39,6 +40,7 @@
         self.hp = round_up(RADIUS * hidden, 128)
         self.pairs = ((1, 2), (0, self.nw - 1))
         self.rw = 2 * self.b
+        self.pitch = self.hp + 128
         self.chunk = 2 * self.rw
         self.th = self.h // RADIUS
         self.half = RADIUS
@@ -122,14 +124,28 @@
     loop(TAPS, body)
 
 
-def conv_tile(dm, wide, toep, tile):
-    base = (tile // dm.half) * dm.tall + lax.rem(tile, dm.half) * dm.m
-    acc = None
-    for i in range(TAPS):
-        rows = pl.ds(pl.multiple_of(base + i * dm.rw, 16), dm.m)
-        part = dot(wide[rows, :], toep[i * 3 * dm.cp:(i + 1) * 3 * dm.cp, :])
-        acc = part if acc is None else acc + part
-    return acc
+def conv_pair(dm, wide, toep, tile, acc_s):
+    size = dm.block // CHUNKS
+
+    @pl.when(lax.rem(tile, dm.half) == 0)
+    def _():
+        base = (tile // dm.half) * dm.tall
+
+        def body(c, carry):
+            acc = None
+            for i in range(TAPS):
+                rows = pl.ds(pl.multiple_of(base + c * size + i * dm.rw, 16), size)
+                part = dot(wide[rows, :], toep[i * 3 * dm.cp:(i + 1) * 3 * dm.cp, :])
+                acc = part if acc is None else acc + part
+            acc_s[pl.ds(pl.multiple_of(c * size, 16), size), :] = acc
+            return carry
+
+        loop(CHUNKS, body)
+
+
+def conv_tile(dm, wide, toep, tile, acc_s):
+    conv_pair(dm, wide, toep, tile, acc_s)
+    return acc_s[pl.ds(pl.multiple_of(lax.rem(tile, dm.half) * dm.m, 16), dm.m), :]
 
 
 def lane_loop(dm, body):
@@ -164,8 +180,8 @@
     return hv * phi
 
 
-def forward_tile(dm, k, tile, wide, toep, cvec, hvec, ones, w1, normed_o, inv_o, h_o):
-    d = (conv_tile(dm, wide, toep, tile) + line(cvec, k, CONV_B)).astype(BF16)
+def forward_tile(dm, k, tile, wide, toep, acc_s, cvec, hvec, ones, w1, normed_o, inv_o, h_o):
+    d = (conv_tile(dm, wide, toep, tile, acc_s) + line(cvec, k, CONV_B)).astype(BF16)
     mean = dot(d, ones[...]) * np.float32(1.0 / dm.c)
     centered = d.astype(F32) - mean
     var = dot_split(centered * centered, ones[...]) * np.float32(1.0 / dm.c)
@@ -174,7 +190,7 @@
     normed_o[...] = normed
     inv_o[...] = inv
     n = (normed * line(cvec, k, NORM_G) + line(cvec, k, NORM_B)).astype(BF16)
-    h_o[...] = (dot(n, w1[k]) + line(hvec, k, FC1_B)).astype(BF16)
+    h_o[:, :dm.hp] = (dot(n, w1[k, :, :dm.hp]) + line(hvec, k, FC1_B)).astype(BF16)
 
 
 def dot_bt(lhs, rhs):
@@ -397,7 +413,7 @@
 
 
 def first_kernel(dm, grid, x, taps, rel, cvec, hvec, ones, w1, gamma,
-                 normed_o, inv_o, h_o, phi_o, xp_o, norm_o, coef_o, wide, toep, ss, xp, keep_sem, send, recv, *grn):
+                 normed_o, inv_o, h_o, phi_o, xp_o, norm_o, coef_o, wide, toep, acc_s, ss, xp, keep_sem, send, recv, *grn):
     step = pl.program_id(0)
 
     @pl.when(step == 0)
@@ -420,7 +436,7 @@
         pltpu.make_async_copy(xp, xp_o, keep_sem).start()
         build_wide(dm, xp, wide, TWO)
 
-    forward_tile(dm, ONE, step, wide, toep, cvec, hvec, ones, w1, normed_o, inv_o, h_o)
+    forward_tile(dm, ONE, step, wide, toep, acc_s, cvec, hvec, ones, w1, normed_o, inv_o, h_o)
 
     def body(rows, lanes):
         g = gelu_chunk(dm, h_o, phi_o, rows, lanes)
@@ -440,7 +456,7 @@
     return lax.rem(jnp.minimum(step, dm.tiles - 1) + dm.half, dm.tiles)
 
 
-def halo_schedule(dm, grid, step, xp, wide, send, recv, between, after):
+def halo_schedule(dm, grid, step, xp, wide, send, recv, between, after, ready=tuple):
     @pl.when(step == dm.half)
     def _():
         halo_start(halo_copies(dm, grid, xp, send, recv)[0])
@@ -452,6 +468,7 @@
         between()
         halo_wait(ends)
         build_wide(dm, xp, wide, ONE)
+        ready()
 
     @pl.when(step == dm.tiles + dm.half)
     def _():
@@ -462,7 +479,7 @@
 
 def second_kernel(dm, grid, h1, phi1, xp1, coef1, taps, rel, cvec, hvec, ones, w1, w2t, gamma, mask, dout,
                   normed_o, inv_o, h_o, phi_o, dr_o, xp_o, sdr_o, coef_o, dsq_o, ggam_o,
-                  wide, toep, resp, raw, ss, cross, tile_s, xp, keep_sem, send, recv, *grn):
+                  wide, toep, acc_s, resp, raw, ss, cross, tile_s, xp, keep_sem, send, recv, *grn):
     step = pl.program_id(0)
     keep = pltpu.make_async_copy(xp, xp_o, keep_sem)
 
@@ -486,16 +503,16 @@
 
         lane_loop(dm, body)
         load_tile(dm, xp1, tile_s, tile, dm.b, RADIUS)
-        o = (dot_bt(resp[...], w2t[ONE]) + line(cvec, ONE, FC2_B)).reshape(-1, dm.b, dm.cp)
+        o = (dot_bt(resp[:, :dm.hp], w2t[ONE, :, :dm.hp]) + line(cvec, ONE, FC2_B)).reshape(-1, dm.b, dm.cp)
         y = (tile_s[...].astype(F32) + (o * mask[ONE][None]).reshape(-1, dm.cp)).astype(BF16)
         store_tile(dm, xp, y, tile, dm.b, RADIUS)
 
     @pl.when(step >= dm.tiles)
     def _():
         tile = step - dm.tiles
-        forward_tile(dm, TWO, tile, wide, toep, cvec, hvec, ones, w1, normed_o, inv_o, h_o)
+        forward_tile(dm, TWO, tile, wide, toep, acc_s, cvec, hvec, ones, w1, normed_o, inv_o, h_o)
         load_tile(dm, dout, tile_s, tile, 0, 0)
-        raw[...] = dot(tile_s[...], w2t[TWO])
+        raw[...] = dot(tile_s[...], w2t[TWO, :, :dm.hp])
 
         def body(rows, lanes):
             g = gelu_chunk(dm, h_o, phi_o, rows, lanes)
@@ -530,16 +547,16 @@
     lane_loop(dm, body)
     dsel32 = jnp.where((mask[k] != 0.0)[None], dout[...].astype(F32).reshape(-1, dm.b, dm.cp), 0.0)
     sums[FC2_B] += jnp.sum(dsel32, axis=0)
-    gfc2[...] += dot_t(dsel32.reshape(-1, dm.cp).astype(BF16), resp[...])
+    gfc2[...] += dot_t(dsel32.reshape(-1, dm.cp).astype(BF16), resp[:, :dm.hp])
     y = None
     if x_rows is not None:
-        o = (dot_bt(resp[...], w2t[k]) + line(cvec, k, FC2_B)).reshape(-1, dm.b, dm.cp)
+        o = (dot_bt(resp[:, :dm.hp], w2t[k, :, :dm.hp]) + line(cvec, k, FC2_B)).reshape(-1, dm.b, dm.cp)
         y = (x_rows[...].astype(F32) + (o * mask[k][None]).reshape(-1, dm.cp)).astype(BF16)
     normed = normed_i[...]
     norm_g = line(cvec, k, NORM_G)
     n = (normed * norm_g + line(cvec, k, NORM_B)).astype(BF16)
-    gfc1[...] += dot_t(n, dh[...])
-    dn16 = dot_bt(dh[...], w1[k]).astype(BF16)
+    gfc1[...] += dot_t(n, dh[:, :dm.hp])
+    dn16 = dot_bt(dh[:, :dm.hp], w1[k, :, :dm.hp]).astype(BF16)
     dn = dn16.astype(F32)
     scale = np.float32(1.0 / dm.c)
     mean1 = (dot_bt(dn16, gmat[k, 0]) + dot_bt(dn16, gmat[k, 1]) + dot_bt(dn16, gmat[k, 2])) * scale
@@ -692,7 +709,7 @@
 def third_kernel(dm, grid, h2, phi2, dr2, coef2, dsq2, dout, normed, inv, xp2, h1, phi1, norm1, taps, rel, cvec, hvec, ones, gmat,
                  w1, w2t, gamma, mask, sdr2,
                  y_o, d1_o, dr1_o, pack, sdr_o, dsq_o, ggam_o,
-                 wide, toep, dp, dcol, corr, resp, dh, tile_s, gfc1, gfc2, sdh, sums, raw, tile_x, cross, send, recv, *grn):
+                 wide, toep, acc_s, dp, dcol, corr, resp, dh, tile_s, gfc1, gfc2, sdh, sums, raw, tile_x, cross, send, recv, *grn):
     step = pl.program_id(0)
 
     @pl.when(step == 0)
@@ -702,7 +719,7 @@
         for ref in (cross, sdr_o, gfc1, gfc2, sdh, sums, corr, pack):
             ref[...] = jnp.zeros_like(ref)
 
-    halo_schedule(dm, grid, step, dp, wide, send, recv, lambda: build_toeplitz(dm, taps.at[3], rel, toep), lambda: None)
+    halo_schedule(dm, grid, step, dp, wide, send, recv, lambda: build_toeplitz(dm, taps.at[3], rel, toep), tuple)
 
     @pl.when(step < dm.tiles)
     def _():
@@ -716,9 +733,9 @@
     def _():
         tile = step - dm.tiles
         load_tile(dm, dout, tile_s, tile, 0, 0)
-        din = (tile_s[...].astype(F32) + conv_tile(dm, wide, toep, tile)).astype(BF16)
+        din = (tile_s[...].astype(F32) + conv_tile(dm, wide, toep, tile, acc_s)).astype(BF16)
         d1_o[...] = din
-        raw[...] = dot(din, w2t[ONE])
+        raw[...] = dot(din, w2t[ONE, :, :dm.hp])
 
         def body(rows, lanes):
             g = h1[rows, lanes].astype(F32) * phi1[rows, lanes]
@@ -743,7 +760,7 @@
 def fourth_kernel(dm, grid, h1, phi1, dr1, coef1, dsq1, d1, normed, inv, xp1, taps, rel, cvec, hvec, ones, gmat,
                   w1, w2t, mask, sdr1, pack2_i,
                   d0_o, out1_o, out2_o, conv_o,
-                  wide, toep, dp, dcol, corr, resp, dh, tile_s, gfc1, gfc2, sdh, sums, pack1, out1, pack2, out2, send, recv, *sem):
+                  wide, toep, acc_s, dp, dcol, corr, resp, dh, tile_s, gfc1, gfc2, sdh, sums, pack1, out1, pack2, out2, send, recv, *sem):
     step = pl.program_id(0)
     stages1 = sum_stages(grid, pack1, out1, sem[:N_SUM])
     stages2 = sum_stages(grid, pack2, out2, sem[N_SUM:2 * N_SUM])
@@ -761,7 +778,7 @@
     begin1, *middle1, end1 = stages1
     conv_begin, conv_row, conv_col, conv_end = conv_stages
     a, b, c, d, e, f = stages2
-    plan = [[a], [b], [], [c], [d], [e], [], [f, conv_row], [], [middle1.pop()], [conv_col]]
+    plan = [[a], [b], [], [c], [d], [e], [], [f, conv_col], [], [middle1.pop()]]
     for at, jobs in enumerate(plan):
         @pl.when(step == at)
         def _():
@@ -783,7 +800,7 @@
         conv_begin()
         column()
 
-    halo_schedule(dm, grid, step, dp, wide, send, recv, between, lambda: None)
+    halo_schedule(dm, grid, step, dp, wide, send, recv, between, tuple, conv_row)
 
     @pl.when(step < dm.tiles)
     def _():
@@ -793,7 +810,7 @@
     @pl.when(step >= dm.tiles)
     def _():
         tile = step - dm.tiles
-        din = (d1[...].astype(F32) + conv_tile(dm, wide, toep, tile)).astype(BF16)
+        din = (d1[...].astype(F32) + conv_tile(dm, wide, toep, tile, acc_s)).astype(BF16)
         store_tile(dm, d0_o, din, tile, 0, 0)
 
     @pl.when(step == pl.num_programs(0) - 1)
@@ -878,15 +895,15 @@
         dm = Dims(act_in.shape, fc1_w.shape[-1])
         rel, perm, perm_back, ones, place = constants(dm)
         sds = jax.ShapeDtypeStruct
-        c_shape, h_shape, s_shape, n_shape = (dm.rows, dm.cp), (dm.rows, dm.hp), (dm.b, dm.hp), (dm.b, dm.hid)
+        c_shape, h_shape, p_shape, s_shape, n_shape = (dm.rows, dm.cp), (dm.rows, dm.hp), (dm.rows, dm.pitch), (dm.b, dm.hp), (dm.b, dm.hid)
         x_shape = (dm.h, dm.nw * dm.b, dm.cp)
         act_t = (dm.b, dm.w, dm.h, dm.c)
         swap = (0, 2, 1, 3)
         big = pltpu.CompilerParams(vmem_limit_bytes=VMEM_LIMIT)
         taps, cvec, hvec, w1, w2t, gmat, mask, x1, d2 = pl.pallas_call(
             functools.partial(prep_kernel, dm),
-            out_shape=[sds((4, TAPS * 8, dm.cp), F32), sds((2, 4, dm.cp), F32), sds((2, 2, dm.hp), F32), sds((2, dm.cp, dm.hp), BF16),
-                       sds((2, dm.cp, dm.hp), BF16), sds((2, 3, dm.cp, dm.cp), BF16), sds((2, dm.b, dm.cp), F32),
+            out_shape=[sds((4, TAPS * 8, dm.cp), F32), sds((2, 4, dm.cp), F32), sds((2, 2, dm.hp), F32), sds((2, dm.cp, dm.pitch), BF16),
+                       sds((2, dm.cp, dm.pitch), BF16), sds((2, 3, dm.cp, dm.cp), BF16), sds((2, dm.b, dm.cp), F32),
                        sds(x_shape, BF16), sds(x_shape, BF16)],
             in_specs=[FULL] * 15, out_specs=[FULL] * 9, compiler_params=big, name='prep')(
                 conv_w.transpose(1, 2, 0, 3), conv_b, norm_g, norm_b, fc1_w, fc1_b, grn_beta, fc2_w.transpose(0, 2, 1), fc2_b,
@@ -896,7 +913,8 @@
         V = pltpu.VMEM
         wide_s = V((2 * dm.tall, 3 * dm.cp), BF16)
         toep_s = V((TAPS * 3 * dm.cp, dm.cp), BF16)
-        raw_s, hid_s, tile_s = V((dm.m, dm.hp), F32), V((dm.m, dm.hp), BF16), V((dm.m, dm.cp), BF16)
+        raw_s, hid_s, tile_s = V((dm.m, dm.hp), F32), V((dm.m, dm.pitch), BF16), V((dm.m, dm.cp), BF16)
+        conv_s = V((dm.block, dm.cp), F32)
         img_s, acc_s = V(s_shape, F32), V((dm.cp, dm.hp), F32)
         xp_shape = (dm.h + 2 * RADIUS, (dm.nw + 2) * dm.b, dm.cp)
         xp_s = V(xp_shape, BF16)
@@ -912,24 +930,24 @@
 
         normed1, inv1, h1, phi1, xp1, norm1, coef1 = call(
             dm, functools.partial(first_kernel, dm, grid), dm.tiles, wholes(x1, taps, rel, cvec, hvec, ones, w1, gamma),
-            [(c_shape, F32, 'only'), (c_shape, F32, 'only'), (h_shape, BF16, 'only'), (h_shape, F32, 'only'), (xp_shape, BF16, 'any'),
+            [(c_shape, F32, 'only'), (c_shape, F32, 'only'), (p_shape, BF16, 'only'), (h_shape, F32, 'only'), (xp_shape, BF16, 'any'),
              (n_shape, F32, WHOLE), (s_shape, F32, WHOLE)],
-            [wide_s, toep_s, img_s, xp_s, dma] + halo_s + grn_s(1), 'first', 0)
+            [wide_s, toep_s, conv_s, img_s, xp_s, dma] + halo_s + grn_s(1), 'first', 0)
 
         normed2, inv2, h2, phi2, dr2, xp2, sdr2, coef2, dsq2, ggam2 = call(
             dm, functools.partial(second_kernel, dm, grid), 2 * dm.tiles,
             [(h1, 'lead'), (phi1, 'lead')] + wholes(xp1, coef1, taps, rel, cvec, hvec, ones, w1, w2t, gamma, mask, d2),
-            [(c_shape, F32, 'tail'), (c_shape, F32, 'tail'), (h_shape, BF16, 'tail'), (h_shape, F32, 'tail'), (h_shape, BF16, 'tail'),
+            [(c_shape, F32, 'tail'), (c_shape, F32, 'tail'), (p_shape, BF16, 'tail'), (h_shape, F32, 'tail'), (p_shape, BF16, 'tail'),
              (xp_shape, BF16, 'any')] + [(s_shape, F32, WHOLE)] * 3 + [(g_shape, F32, WHOLE)],
-            [wide_s, toep_s, hid_s, raw_s, img_s, img_s, tile_s, xp_s, dma] + halo_s + grn_s(2), 'second', 1)
-
-        bwd_s = [wide_s, toep_s, xp_s, V((dm.cp, dm.rows), BF16), V((3, 8, 3 * dm.cp), F32), hid_s, hid_s, tile_s,
+            [wide_s, toep_s, conv_s, hid_s, raw_s, img_s, img_s, tile_s, xp_s, dma] + halo_s + grn_s(2), 'second', 1)
+
+        bwd_s = [wide_s, toep_s, conv_s, xp_s, V((dm.cp, dm.rows), BF16), V((3, 8, 3 * dm.cp), F32), hid_s, hid_s, tile_s,
                  acc_s, acc_s, img_s, V((4, dm.b, dm.cp), F32)]
         y2, d1, dr1, pack2, sdr1, dsq1, ggam1 = call(
             dm, functools.partial(third_kernel, dm, grid), 2 * dm.tiles,
             [(h2, 'lead'), (phi2, 'lead'), (dr2, 'lead')] + wholes(coef2, dsq2, d2) + [(normed2, 'lead'), (inv2, 'lead')] + wholes(xp2)
             + [(h1, 'tail'), (phi1, 'tail')] + wholes(norm1, taps, rel, cvec, hvec, ones, gmat, w1, w2t, gamma, mask, sdr2),
-            [(x_shape, BF16, WHOLE), (c_shape, BF16, 'tail'), (h_shape, BF16, 'tail'), (p2_shape, F32, WHOLE), (s_shape, F32, WHOLE),
+            [(x_shape, BF16, WHOLE), (c_shape, BF16, 'tail'), (p_shape, BF16, 'tail'), (p2_shape, F32, WHOLE), (s_shape, F32, WHOLE),
              (s_shape, F32, WHOLE), (g_shape, F32, WHOLE)],
             bwd_s + [raw_s, tile_s, img_s] + halo_s + grn_s(1), 'third', 2)
 

time: 244 us -> 236 us (0.967)
  Pallas kernels: 243 us -> 235 us
    pallas_call x4, Pallas kernels: 226 us -> 218 us  [call(): pl.pallas_call(kernel, grid=(steps,), in_specs=[spec(a.shape, mode) for a...]
where the time goes in v4:
time: 236 us; the launch traced here: 235 us
  Pallas kernels  235 us (100%)
    pallas_call x4, Pallas kernels, call(): pl.pallas_call(kernel, grid=(steps,), in_specs=[spec(a.shape, mode) for a...  218 us
    pallas_call x1, Pallas kernels, local_step(): pl.pallas_call(functools.partial(prep_kernel, dm), out_shape=[sds((4, TAP...  8.84 us
    pallas_call x1, Pallas kernels, local_step(): pl.pallas_call(functools.partial(final_kernel, dm), out_shape=[sds(act_t,...  7.89 us

profile of v4, /device:TPU:97, one launch (start us, length us, event | category | flops | bytes accessed | tf_op | source)
XLA Modules:
  0.0 235.5 jit_solution(4238229670468486361)
XLA Ops:
  0.6 8.8 %prep.1 = (f32[4,56,256]{2,1,0:T(8,128)}, f32[2,4,256]{2,1,0:T(4,128)}, f32[2,2,1024]{2,1,0:T(2,128)}, bf16[2,256,1152]{2,1,0:T(8,128)(2,1)}, bf16[2,256,1152]{2...) custom-call(bf16[7,7,2,80]{3,2,1,0:T(2,128)(2,1)} %bitcast.12, ...), custom_call_target="tpu_custom_call" | custom-call | tf_op jit(solution)/shard_map/prep/pallas_call | solution.py:903
  9.5 42.7 %first.1 = (f32[2304,256]{1,0:T(8,128)}, f32[2304,256]{1,0:T(8,128)}, bf16[2304,1152]{1,0:T(8,128)(2,1)}, f32[2304,1024]{1,0:T(8,128)}, bf16[30,144,256]{2,1,0:T...) custom-call(bf16[24,96,256]{2,1,0:T(8,128)(2,1)} %get-tuple-element.61.x, f32[4,56,256]{2,1,0:T(8,128)} %get-tuple-element.62.taps, ...), custom_call_target="tpu_custom_call" | custom-call | tf_op jit(solution)/shard_map/first/pallas_call | solution.py:880
  52.2 55.9 %second.1 = (f32[2304,256]{1,0:T(8,128)}, f32[2304,256]{1,0:T(8,128)}, bf16[2304,1152]{1,0:T(8,128)(2,1)}, f32[2304,1024]{1,0:T(8,128)}, bf16[2304,1152]{1,0:T(8...) custom-call(bf16[2304,1152]{1,0:T(8,128)(2,1)} %get-tuple-element.66, ...), custom_call_target="tpu_custom_call" | custom-call | tf_op jit(solution)/shard_map/second/pallas_call | solution.py:880
  108.1 62.7 %third.1 = (bf16[24,96,256]{2,1,0:T(8,128)(2,1)}, bf16[2304,256]{1,0:T(8,128)(2,1)}, bf16[2304,1152]{1,0:T(8,128)(2,1)}, f32[256,384]{1,0:T(8,128)}, f32[24,1024...) custom-call(bf16[2304,1152]{1,0:T(8,128)(2,1)} %get-tuple-element.73.h2, f32[2304,1024]{1,0:T(8,128)} %get-tuple-element.74.phi2, ...), custom_call_target="tpu_custom_call" | custom-call | tf_op jit(solution)/shard_map/third/pallas_call | solution.py:880
  170.8 56.6 %fourth.1 = (bf16[24,96,256]{2,1,0:T(8,128)(2,1)}, f32[192,384]{1,0:T(8,128)}, f32[256,384]{1,0:T(8,128)}, f32[56,128]{1,0:T(8,128)}) custom-call(bf16[2304,1152]{1,0:T(8,128)(2,1)} %get-tuple-element.66.h1, f32[2304,1024]{1,0:T(8,128)} %get-tuple-element.67.phi1, bf16[2304,1152]{1,0:T(8,128)(2,1)} %get-tuple-element.84.dr1, ...), custom_call_target="tpu_custom_call" | custom-call | tf_op jit(solution)/shard_map/fourth/pallas_call | solution.py:880
  227.4 7.9 %final.1 = (bf16[24,12,24,80]{3,2,1,0:T(8,128)(2,1)}, bf16[24,12,24,80]{3,2,1,0:T(8,128)(2,1)}, f32[7,7,2,80]{3,2,1,0:T(2,128)}, f32[2,80]{1,0:T(2,128)}, f32[2,...) custom-call(f32[192,384]{1,0:T(8,128)} %get-tuple-element.91.out1, ...), custom_call_target="tpu_custom_call" | custom-call | tf_op jit(solution)/shard_map/final/pallas_call | solution.py:963
